TPU v7x, 128 devices: a whole 4x4x4 slice. The times are simulated.
128 devices in a mesh: gene: 8 (over x, z_lo), var: 8 (over y, core), perm: 2 (over z_hi).
Axes of the slice: x: 4, y: 4, z: 4 (z_hi: 2, z_lo: 2; z = z_hi * 2 + z_lo), core: 2. Of those that a mesh axis runs over, the one named last changes fastest.
Arguments:
- genotypes: bfloat16 [8, 6144, 768], P('gene', ('var', 'perm')), may hold values from 0 to 2
- phenotypes: float32 [1024, 768], P('gene'), may hold values from -6 to 6
- perm_rows: int32 [256, 768], P(('var', 'perm')), may hold values from 0 to 767, each once within a row
- starts: int32 [1024], P('gene'), may hold values from 0 to 2048, as said below
Outputs:
- maxima: float32 [256, 1024], P(('var', 'perm'), 'gene')
- moments: float32 [2, 1024], P(None, 'gene')
- pooled: float32 [2], replicated
Inputs may be any that keep to these rules, and one draw needn't show every extreme that they name: `perm_rows`: each row is a permutation of 0 to 767. Within each block of 128 genes the starts never fall; a gene's window of 4096 variants lies inside its block's 6144 variants.
All inputs are finite; a program needn't handle non-finite values.
Results may differ from a plain program's by a relative error of at most 0.0023.
Values may be sent and summed in bfloat16 or wider, within the bound.
No kernel may reach another device: no remote copies, remote signals or barrier semaphores. Data moves between devices by JAX's collectives and lax.ppermute only.
A program may use at most 64 MiB of HBM per device.

v0:
```python
import math

import jax
import jax.numpy as jnp
from jax import lax
from jax.sharding import PartitionSpec as P

WINDOW = 4096
PERMS = 256


def sent_to_all(array, axis):
    count = lax.axis_size(axis)
    return lax.all_to_all(
        jnp.broadcast_to(array[None], (count, *array.shape)), axis, 0, 0, tiled=True
    )


def taken_together(array, axis):
    everything = sent_to_all(array, axis)
    return jnp.sum(everything, axis=0)


def packed_total(arrays, axis):
    ends = [0]
    for a in arrays:
        ends.append(ends[-1] + a.size)
    subtotal = taken_together(jnp.concatenate([a.ravel() for a in arrays]), axis)
    return tuple((subtotal[b:e].reshape(a.shape) for a, b, e in zip(arrays, ends, ends[1:])))


def standard_rows(values):
    as_float = values.astype(jnp.float32)
    centred = as_float - jnp.mean(as_float, axis=1, keepdims=True)
    inv_norm = lax.rsqrt(jnp.sum(centred * centred, axis=1, keepdims=True) + 1.0)
    return (centred * inv_norm).astype(jnp.bfloat16)


def window_best(row_block, first_row, perm_table, starts):
    scores = lax.dot_general(
        row_block, perm_table, (((1,), (1,)), ((), ())), preferred_element_type=jnp.float32
    )
    row_index = first_row + lax.broadcasted_iota(jnp.int32, (row_block.shape[0], 1, 1), 0)
    inside = (row_index >= starts[None, None, :]) & (row_index < starts[None, None, :] + WINDOW)
    return jnp.max(jnp.where(inside, scores * scores, 0.0), axis=0)


def shards(genotypes, phenotypes, perm_rows, starts):
    standard = standard_rows(genotypes[0])
    table_base = standard_rows(phenotypes).T
    samples = phenotypes.shape[1]
    local_rows = standard.shape[0]
    width_own = perm_rows.shape[0]
    gene_count = phenotypes.shape[0]
    selector = jax.nn.one_hot(perm_rows, samples, dtype=jnp.bfloat16)
    perm_table = jnp.einsum(
        "pst,tg->psg", selector, table_base, preferred_element_type=jnp.float32
    ).astype(jnp.bfloat16)
    start_best = jnp.zeros((width_own, gene_count), jnp.float32)
    shard_rows = lax.all_gather(standard, ("var", "perm"), axis=0, tiled=True)
    step_rows = math.gcd(shard_rows.shape[0], local_rows)

    def one_block(block_step, carried):
        row_block = lax.dynamic_slice_in_dim(shard_rows, block_step * step_rows, step_rows, 0)
        found = window_best(row_block, block_step * step_rows, perm_table, starts)
        return jnp.maximum(carried, found)

    best_sq = lax.fori_loop(0, shard_rows.shape[0] // step_rows, one_block, start_best)
    maxima = best_sq * samples
    log_stat = jnp.log1p(maxima)
    totals = packed_total(
        (jnp.sum(log_stat, axis=0), jnp.sum(log_stat * log_stat, axis=0)), ("var", "perm")
    )
    moments = jnp.stack(totals) / PERMS
    pooled = taken_together(jnp.sum(moments, axis=1), "gene") / (gene_count * lax.axis_size("gene"))
    return (maxima, moments, pooled)


def solution(mesh):
    return jax.shard_map(
        shards,
        mesh=mesh,
        in_specs=(
            P("gene", ("var", "perm"), None),
            P("gene", None),
            P(("var", "perm"), None),
            P("gene"),
        ),
        out_specs=(P(("var", "perm"), "gene"), P(None, "gene"), P()),
        check_vma=False,
    )
```

profile of v0, /device:TPU:1, one launch (start us, length us, event | category | flops | bytes accessed | tf_op | source)
XLA Modules:
  0.0 180.2 jit_solution(4692813210141826806)
XLA Ops:
  7.2 1.3 convert_reduce_fusion
  8.5 1.4 fusion.9
  9.9 2.1 %fusion.10 = bf16[384,768]{1,0:T(8,128)(2,1)} fusion(bf16[1,384,768]{2,1,0:T(8,128)(2,1)} %param.6, f32[384]{0:T(512)S(1)} %add_rsqrt_fusion, f32[384]{0:T(512)S(1)} %broadcast_multiply_fusion.1), kind=kLoop, calls=%fused_computation.18 | loop fusion | flops 1179648 | bytes 1182720 | tf_op jit(solution)/shard_map/convert_element_type | solution.py:36
  12.4 8.3 %fusion.5 = bf16[16,768,128]{2,1,0:T(8,128)(2,1)} fusion(s32[16,768]{1,0:T(8,128)S(1)} %copy-done.2, f32[128,768]{1,0:T(8,128)S(1)} %copy-done, f32[128]{0:T(128)S(1)} %add_rsqrt_fusion.1, f32[128]{0:T(128)S(1)} %broadcast_multiply_fusion.3), kind=kOutput, calls=%fused_computation.11 | convolution fusion | flops 2427224064 | bytes 3589120 | tf_op jit(solution)/shard_map/pst,tg->psg/dot_general | solution.py:56
  20.7 72.2 %all-gather.2.cloned.1.call-done = bf16[6144,768]{1,0:T(8,128)(2,1)} async-done(((bf16[384,768]{1,0:T(8,128)(2,1)}), bf16[6144,768]{1,0:T(8,128)(2,1)}) %all-gather.2.cloned.1.call-update) | async-done | bytes 9437200 | tf_op jit(solution)/shard_map/all_gather | solution.py:60
  92.9 58.8 %while.14 = (s32[]{:T(128)}, f32[16,128]{1,0:T(8,128)S(1)}, s32[128]{0:T(128)S(1)}, bf16[6144,768]{1,0:T(8,128)(2,1)}, bf16[16,768,128]{2,1,0:T(8,128)(2,1)}, /*index=5*/s32[]{:T(128)}, s32[]{:T(128)}, s32[]{:T(128)}, s32[]{:T(128)}) while((s32[]{:T(128)}, f32[16,128]{1,0:T(8,128)S(1)}, s32[128]{0:T(128)S(1)}, ...), condition=%wide.region_6.7_spmd.clone, body=%wide.region_4.6_spmd.clone.sunk | while | flops 1210468864 | bytes 3871909 | solution.py:68
  93.0 3.5 %select_reduce_fusion.2 = f32[16,128]{1,0:T(8,128)S(1)} fusion(bf16[16,768,128]{2,1,0:T(8,128)(2,1)} %get-tuple-element.186, pred[384,128]{1,0:T(8,128)(4,1)S(1)} %compare_and_fusion.2, bf16[6144,768]{1,0:T(8,128)(2,1)} %get-tuple-element.185, s32[]{:T(128)S(6)} %select_n.21), kind=kOutput, calls=%fused_computation.clone.1 | convolution fusion | flops 1210316800 | bytes 3792900 | tf_op jit(solution)/shard_map/while/body/eval_jaxpr/dot_general | solution.py:40
  96.7 3.5 %select_reduce_fusion.2 = f32[16,128]{1,0:T(8,128)S(1)} fusion(bf16[16,768,128]{2,1,0:T(8,128)(2,1)} %get-tuple-element.186, pred[384,128]{1,0:T(8,128)(4,1)S(1)} %compare_and_fusion.2, bf16[6144,768]{1,0:T(8,128)(2,1)} %get-tuple-element.185, s32[]{:T(128)S(6)} %select_n.21), kind=kOutput, calls=%fused_computation.clone.1 | convolution fusion | flops 1210316800 | bytes 3792900 | tf_op jit(solution)/shard_map/while/body/eval_jaxpr/dot_general | solution.py:40
  100.4 3.5 %select_reduce_fusion.2 = f32[16,128]{1,0:T(8,128)S(1)} fusion(bf16[16,768,128]{2,1,0:T(8,128)(2,1)} %get-tuple-element.186, pred[384,128]{1,0:T(8,128)(4,1)S(1)} %compare_and_fusion.2, bf16[6144,768]{1,0:T(8,128)(2,1)} %get-tuple-element.185, s32[]{:T(128)S(6)} %select_n.21), kind=kOutput, calls=%fused_computation.clone.1 | convolution fusion | flops 1210316800 | bytes 3792900 | tf_op jit(solution)/shard_map/while/body/eval_jaxpr/dot_general | solution.py:40
  104.0 3.5 %select_reduce_fusion.2 = f32[16,128]{1,0:T(8,128)S(1)} fusion(bf16[16,768,128]{2,1,0:T(8,128)(2,1)} %get-tuple-element.186, pred[384,128]{1,0:T(8,128)(4,1)S(1)} %compare_and_fusion.2, bf16[6144,768]{1,0:T(8,128)(2,1)} %get-tuple-element.185, s32[]{:T(128)S(6)} %select_n.21), kind=kOutput, calls=%fused_computation.clone.1 | convolution fusion | flops 1210316800 | bytes 3792900 | tf_op jit(solution)/shard_map/while/body/eval_jaxpr/dot_general | solution.py:40
  107.7 3.5 %select_reduce_fusion.2 = f32[16,128]{1,0:T(8,128)S(1)} fusion(bf16[16,768,128]{2,1,0:T(8,128)(2,1)} %get-tuple-element.186, pred[384,128]{1,0:T(8,128)(4,1)S(1)} %compare_and_fusion.2, bf16[6144,768]{1,0:T(8,128)(2,1)} %get-tuple-element.185, s32[]{:T(128)S(6)} %select_n.21), kind=kOutput, calls=%fused_computation.clone.1 | convolution fusion | flops 1210316800 | bytes 3792900 | tf_op jit(solution)/shard_map/while/body/eval_jaxpr/dot_general | solution.py:40
  111.4 3.5 %select_reduce_fusion.2 = f32[16,128]{1,0:T(8,128)S(1)} fusion(bf16[16,768,128]{2,1,0:T(8,128)(2,1)} %get-tuple-element.186, pred[384,128]{1,0:T(8,128)(4,1)S(1)} %compare_and_fusion.2, bf16[6144,768]{1,0:T(8,128)(2,1)} %get-tuple-element.185, s32[]{:T(128)S(6)} %select_n.21), kind=kOutput, calls=%fused_computation.clone.1 | convolution fusion | flops 1210316800 | bytes 3792900 | tf_op jit(solution)/shard_map/while/body/eval_jaxpr/dot_general | solution.py:40
  115.1 3.5 %select_reduce_fusion.2 = f32[16,128]{1,0:T(8,128)S(1)} fusion(bf16[16,768,128]{2,1,0:T(8,128)(2,1)} %get-tuple-element.186, pred[384,128]{1,0:T(8,128)(4,1)S(1)} %compare_and_fusion.2, bf16[6144,768]{1,0:T(8,128)(2,1)} %get-tuple-element.185, s32[]{:T(128)S(6)} %select_n.21), kind=kOutput, calls=%fused_computation.clone.1 | convolution fusion | flops 1210316800 | bytes 3792900 | tf_op jit(solution)/shard_map/while/body/eval_jaxpr/dot_general | solution.py:40
  118.8 3.5 %select_reduce_fusion.2 = f32[16,128]{1,0:T(8,128)S(1)} fusion(bf16[16,768,128]{2,1,0:T(8,128)(2,1)} %get-tuple-element.186, pred[384,128]{1,0:T(8,128)(4,1)S(1)} %compare_and_fusion.2, bf16[6144,768]{1,0:T(8,128)(2,1)} %get-tuple-element.185, s32[]{:T(128)S(6)} %select_n.21), kind=kOutput, calls=%fused_computation.clone.1 | convolution fusion | flops 1210316800 | bytes 3792900 | tf_op jit(solution)/shard_map/while/body/eval_jaxpr/dot_general | solution.py:40
  122.4 3.5 %select_reduce_fusion.2 = f32[16,128]{1,0:T(8,128)S(1)} fusion(bf16[16,768,128]{2,1,0:T(8,128)(2,1)} %get-tuple-element.186, pred[384,128]{1,0:T(8,128)(4,1)S(1)} %compare_and_fusion.2, bf16[6144,768]{1,0:T(8,128)(2,1)} %get-tuple-element.185, s32[]{:T(128)S(6)} %select_n.21), kind=kOutput, calls=%fused_computation.clone.1 | convolution fusion | flops 1210316800 | bytes 3792900 | tf_op jit(solution)/shard_map/while/body/eval_jaxpr/dot_general | solution.py:40
  126.1 3.5 %select_reduce_fusion.2 = f32[16,128]{1,0:T(8,128)S(1)} fusion(bf16[16,768,128]{2,1,0:T(8,128)(2,1)} %get-tuple-element.186, pred[384,128]{1,0:T(8,128)(4,1)S(1)} %compare_and_fusion.2, bf16[6144,768]{1,0:T(8,128)(2,1)} %get-tuple-element.185, s32[]{:T(128)S(6)} %select_n.21), kind=kOutput, calls=%fused_computation.clone.1 | convolution fusion | flops 1210316800 | bytes 3792900 | tf_op jit(solution)/shard_map/while/body/eval_jaxpr/dot_general | solution.py:40
  129.8 3.5 %select_reduce_fusion.2 = f32[16,128]{1,0:T(8,128)S(1)} fusion(bf16[16,768,128]{2,1,0:T(8,128)(2,1)} %get-tuple-element.186, pred[384,128]{1,0:T(8,128)(4,1)S(1)} %compare_and_fusion.2, bf16[6144,768]{1,0:T(8,128)(2,1)} %get-tuple-element.185, s32[]{:T(128)S(6)} %select_n.21), kind=kOutput, calls=%fused_computation.clone.1 | convolution fusion | flops 1210316800 | bytes 3792900 | tf_op jit(solution)/shard_map/while/body/eval_jaxpr/dot_general | solution.py:40
  133.5 3.5 %select_reduce_fusion.2 = f32[16,128]{1,0:T(8,128)S(1)} fusion(bf16[16,768,128]{2,1,0:T(8,128)(2,1)} %get-tuple-element.186, pred[384,128]{1,0:T(8,128)(4,1)S(1)} %compare_and_fusion.2, bf16[6144,768]{1,0:T(8,128)(2,1)} %get-tuple-element.185, s32[]{:T(128)S(6)} %select_n.21), kind=kOutput, calls=%fused_computation.clone.1 | convolution fusion | flops 1210316800 | bytes 3792900 | tf_op jit(solution)/shard_map/while/body/eval_jaxpr/dot_general | solution.py:40
  137.1 3.5 %select_reduce_fusion.2 = f32[16,128]{1,0:T(8,128)S(1)} fusion(bf16[16,768,128]{2,1,0:T(8,128)(2,1)} %get-tuple-element.186, pred[384,128]{1,0:T(8,128)(4,1)S(1)} %compare_and_fusion.2, bf16[6144,768]{1,0:T(8,128)(2,1)} %get-tuple-element.185, s32[]{:T(128)S(6)} %select_n.21), kind=kOutput, calls=%fused_computation.clone.1 | convolution fusion | flops 1210316800 | bytes 3792900 | tf_op jit(solution)/shard_map/while/body/eval_jaxpr/dot_general | solution.py:40
  140.8 3.5 %select_reduce_fusion.2 = f32[16,128]{1,0:T(8,128)S(1)} fusion(bf16[16,768,128]{2,1,0:T(8,128)(2,1)} %get-tuple-element.186, pred[384,128]{1,0:T(8,128)(4,1)S(1)} %compare_and_fusion.2, bf16[6144,768]{1,0:T(8,128)(2,1)} %get-tuple-element.185, s32[]{:T(128)S(6)} %select_n.21), kind=kOutput, calls=%fused_computation.clone.1 | convolution fusion | flops 1210316800 | bytes 3792900 | tf_op jit(solution)/shard_map/while/body/eval_jaxpr/dot_general | solution.py:40
  144.5 3.5 %select_reduce_fusion.2 = f32[16,128]{1,0:T(8,128)S(1)} fusion(bf16[16,768,128]{2,1,0:T(8,128)(2,1)} %get-tuple-element.186, pred[384,128]{1,0:T(8,128)(4,1)S(1)} %compare_and_fusion.2, bf16[6144,768]{1,0:T(8,128)(2,1)} %get-tuple-element.185, s32[]{:T(128)S(6)} %select_n.21), kind=kOutput, calls=%fused_computation.clone.1 | convolution fusion | flops 1210316800 | bytes 3792900 | tf_op jit(solution)/shard_map/while/body/eval_jaxpr/dot_general | solution.py:40
  148.2 3.5 %select_reduce_fusion.2 = f32[16,128]{1,0:T(8,128)S(1)} fusion(bf16[16,768,128]{2,1,0:T(8,128)(2,1)} %get-tuple-element.186, pred[384,128]{1,0:T(8,128)(4,1)S(1)} %compare_and_fusion.2, bf16[6144,768]{1,0:T(8,128)(2,1)} %get-tuple-element.185, s32[]{:T(128)S(6)} %select_n.21), kind=kOutput, calls=%fused_computation.clone.1 | convolution fusion | flops 1210316800 | bytes 3792900 | tf_op jit(solution)/shard_map/while/body/eval_jaxpr/dot_general | solution.py:40
  152.3 10.1 %all_to_all.12 = f32[16,1,256]{2,1,0:T(1,128)S(1)} all-to-all(f32[16,1,256]{2,1,0:T(1,128)S(1)} %broadcast_in_dim.52), channel_id=1, replica_groups=mesh['gene'=8,'var'=8,'perm'=2] {'var','perm'}, dimensions={0} | all-to-all | bytes 32768 | tf_op jit(solution)/shard_map/all_to_all | solution.py:14
  163.2 9.6 %all_to_all.13 = f32[8,1,2]{2,1,0:T(1,128)S(1)} all-to-all(f32[8,1,2]{2,1,0:T(1,128)S(1)} %broadcast_in_dim.53), channel_id=1, replica_groups=mesh['gene'=8,'var'=8,'perm'=2] {'gene'}, dimensions={0} | all-to-all | bytes 128 | tf_op jit(solution)/shard_map/all_to_all | solution.py:14
  (88 shorter events, 4.4 us)
Async XLA Ops:
  7.2 4.9 %copy-start = (f32[128,768]{1,0:T(8,128)S(1)}, f32[128,768]{1,0:T(8,128)}, u32[]{:S(2)}) copy-start(f32[128,768]{1,0:T(8,128)} %param.7) | copy-start | bytes 1179652
  7.2 5.2 %copy-start.2 = (s32[16,768]{1,0:T(8,128)S(1)}, s32[16,768]{1,0:T(8,128)}, u32[]{:S(2)}) copy-start(s32[16,768]{1,0:T(8,128)} %param.8) | copy-start | bytes 147460
  7.2 85.7 %all-gather.2.cloned.1.call-start = ((), (), s32[]{:S(2)}) async-start(), calls=%async_computation.2 | async-start | bytes 10027008 | tf_op jit(solution)/shard_map/all_gather | solution.py:60
  12.4 80.5 %copy-start.1 = (s32[128]{0:T(128)S(1)}, s32[128]{0:T(128)}, u32[]{:S(2)}) copy-start(s32[128]{0:T(128)} %param.9) | copy-start | bytes 1540
Sparse Core Ops, SparseCore 0:
  12.1 80.6 all-gather.1
where the time goes:
time: 181 us; the launch traced here: 180 us
  waiting for transfers between devices  72.2 us (40%)
  matrix products  64 us (35%)
  blocking collectives  19.7 us (11%)
  between operations  14.1 us (8%)
  other arithmetic  9.07 us (5%)
    all_gather x1, waiting for transfers between devices, shards(): shard_rows = lax.all_gather(standard, ('var', 'perm'), axis=0, tiled=True)  72.2 us
    dot_general x16, matrix products, window_best(): lax.dot_general(row_block, perm_table, (((1,), (1,)), ((), ())), preferre...  55.8 us
    all_to_all x2, blocking collectives, sent_to_all(): lax.all_to_all(jnp.broadcast_to(array[None], (count, *array.shape)), axis...  19.7 us
    dot_general x1, matrix products, shards(): jnp.einsum('pst,tg->psg', selector, table_base, preferred_element_type=jn...  8.28 us
  transfers between devices with their start and end apart: 1, of which 1 were waited for; matrix products, arithmetic and copies ran while one was open for 5% of the time, Pallas kernels for 0%

commit v1 on v0

v1 whole, which is shorter than its diff:
```python
import functools

import jax
import jax.numpy as jnp
from jax import lax
from jax.experimental import pallas as pl
from jax.experimental.pallas import tpu as pltpu
from jax.sharding import PartitionSpec as P

WINDOW = 4096
PERMS = 256
GROUP = 16
FOLD = 256
TILE = 256


def standardized(values):
    centred = values - jnp.mean(values, axis=1, keepdims=True)
    inv_norm = lax.rsqrt(jnp.sum(centred * centred, axis=1, keepdims=True) + 1.0)
    return (centred * inv_norm).astype(jnp.bfloat16)


def standard_kernel(x_ref, o_ref):
    o_ref[...] = standardized(x_ref[0].astype(jnp.float32))


def standard_rows(genotypes):
    _, rows, samples = genotypes.shape
    step = rows // 3
    return pl.pallas_call(
        standard_kernel,
        grid=(3,),
        in_specs=[pl.BlockSpec((1, step, samples), lambda i: (0, i, 0))],
        out_specs=pl.BlockSpec((step, samples), lambda i: (i, 0)),
        out_shape=jax.ShapeDtypeStruct((rows, samples), jnp.bfloat16),
        name="standard",
    )(genotypes)


def table_kernel(per_step, pheno_ref, perm_ref, out_ref, base_ref):
    genes, samples = pheno_ref.shape
    folds = samples // FOLD

    @pl.when(pl.program_id(0) == 0)
    def _():
        std = standardized(pheno_ref[...])
        for b in range(folds):
            base_ref[b * genes:(b + 1) * genes, :] = std[:, b * FOLD:(b + 1) * FOLD]

    within = lax.broadcasted_iota(jnp.int32, (FOLD, samples), 0)
    for k in range(per_step):
        index = perm_ref[0, k:k + 1, :]
        low = jnp.bitwise_and(index, FOLD - 1)
        block = jnp.right_shift(index, FOLD.bit_length() - 1)
        hot = jnp.where(within == low, 1.0, 0.0).astype(jnp.bfloat16)
        picked = jnp.dot(base_ref[...], hot, preferred_element_type=jnp.float32)
        chosen = picked[:genes]
        for b in range(1, folds):
            chosen = jnp.where(block == b, picked[b * genes:(b + 1) * genes], chosen)
        chosen = chosen.astype(jnp.bfloat16)
        for g in range(genes // GROUP):
            out_ref[g, k * GROUP:(k + 1) * GROUP, :] = chosen[g * GROUP:(g + 1) * GROUP]


def perm_tables(phenotypes, perm_rows):
    genes, samples = phenotypes.shape
    perms = perm_rows.shape[0]
    per_step = 4
    steps = perms // per_step
    return pl.pallas_call(
        functools.partial(table_kernel, per_step),
        grid=(steps,),
        in_specs=[
            pl.BlockSpec((genes, samples), lambda i: (0, 0)),
            pl.BlockSpec((1, per_step, samples), lambda i: (i, 0, 0)),
        ],
        out_specs=pl.BlockSpec((genes // GROUP, per_step * GROUP, samples), lambda i: (0, i, 0)),
        out_shape=jax.ShapeDtypeStruct((genes // GROUP, perms * GROUP, samples), jnp.bfloat16),
        scratch_shapes=[pltpu.VMEM((samples // FOLD * genes, FOLD), jnp.bfloat16)],
        name="tables",
    )(phenotypes, perm_rows.reshape(steps, per_step, samples))


def score_kernel(count, first_ref, table_ref, starts_ref, *refs):
    shards, out_ref, best_ref = refs[:count], refs[count], refs[count + 1]
    step = pl.program_id(0)
    rows = table_ref.shape[1]
    perms = rows // GROUP
    local = shards[0].shape[0]
    half = TILE // 2
    pieces = [(i, r) for i in range(count) for r in range(0, local, half)]
    lead = starts_ref[0]
    best = None
    for t in range(0, len(pieces), 2):
        pair = pieces[t:t + 2]
        weights = jnp.concatenate([shards[i][r:r + half, :] for i, r in pair], axis=0)
        scores = lax.dot_general(
            table_ref[0], weights, (((1,), (1,)), ((), ())), preferred_element_type=jnp.float32
        )
        for n, (i, r) in enumerate(pair):
            at = lax.broadcasted_iota(jnp.int32, (GROUP, half), 1) + (first_ref[i] + r)
            inside = (at >= lead) & (at < lead + WINDOW)
            part = jnp.abs(scores[:, n * half:(n + 1) * half]).reshape(perms, GROUP, half)
            part = jnp.where(inside[None], part, 0.0)
            best = part if best is None else jnp.maximum(best, part)
    best_ref[step] = best

    @pl.when(step == pl.num_programs(0) - 1)
    def _():
        groups = best_ref.shape[0]
        lane = lax.broadcasted_iota(jnp.int32, (1, GROUP, half), 2)
        gene = lax.broadcasted_iota(jnp.int32, (1, GROUP, half), 1)
        total = None
        for g in range(groups):
            top = jnp.max(best_ref[g], axis=2, keepdims=True)
            spread = jnp.max(jnp.where(lane == gene + g * GROUP, top, 0.0), axis=1)
            total = spread if total is None else jnp.maximum(total, spread)
        out_ref[...] = total


def window_best(table, starts, shards, firsts):
    groups, rows, samples = table.shape
    perms = rows // GROUP
    local = shards[0].shape[0]
    genes = groups * GROUP
    count = len(shards)
    lead = jnp.broadcast_to(starts.reshape(groups, GROUP, 1), (groups, GROUP, TILE // 2))
    whole = pl.BlockSpec((local, samples), lambda i: (0, 0), pipeline_mode=pl.Buffered(1))
    return pl.pallas_call(
        functools.partial(score_kernel, count),
        grid=(groups,),
        in_specs=[
            pl.BlockSpec(memory_space=pltpu.SMEM),
            pl.BlockSpec((1, rows, samples), lambda i: (i, 0, 0)),
            pl.BlockSpec((1, GROUP, TILE // 2), lambda i: (i, 0, 0)),
            *[whole] * count,
        ],
        out_specs=pl.BlockSpec((perms, genes), lambda i: (0, 0)),
        out_shape=jax.ShapeDtypeStruct((perms, genes), jnp.float32),
        scratch_shapes=[pltpu.VMEM((groups, perms, GROUP, TILE // 2), jnp.float32)],
        name="scores",
    )(jnp.stack(firsts).astype(jnp.int32), table, lead, *shards)


def shards_program(genotypes, phenotypes, perm_rows, starts):
    var_n = lax.axis_size("var")
    rows_n = var_n // 2
    both = ("var", "perm")
    samples = phenotypes.shape[1]
    local = genotypes.shape[1]
    gene_count = phenotypes.shape[0]

    def along(step):
        return [(v, ((v // 2 + step) % rows_n) * 2 + v % 2) for v in range(var_n)]

    twin = [(v, v ^ 1) for v in range(var_n)]
    across = [(0, 1), (1, 0)]
    mate = [
        (v * 2 + z, ((((v // 2 + rows_n // 2) % rows_n) * 2 + v % 2) * 2 + 1 - z))
        for v in range(var_n) for z in range(2)
    ]
    me = lax.axis_index("var")
    z = lax.axis_index("perm")
    y, core = me // 2, me % 2

    def first(row, c, deep):
        return ((((row + rows_n) % rows_n) * 2 + c) * 2 + deep) * local

    mate_rows = lax.ppermute(perm_rows, both, mate)
    own = standard_rows(genotypes)
    below = lax.ppermute(own, "var", along(1))
    above = lax.ppermute(own, "var", along(-1))
    deep = lax.ppermute(own, "perm", across)
    own_twin = lax.ppermute(own, "var", twin)
    table_own = perm_tables(phenotypes, perm_rows)
    table_mate = perm_tables(phenotypes, mate_rows)

    near = (own, own_twin)
    near_first = (first(y, core, z), first(y, 1 - core, z))
    far = [below, above, deep]
    far_at = [(y - 1, z), (y + 1, z), (y, 1 - z)]
    far_first = [first(a, core, d) for a, d in far_at] + [first(a, 1 - core, d) for a, d in far_at]
    far = far + [lax.ppermute(f, "var", twin) for f in far]

    near_own = window_best(table_own, starts, near, near_first)
    near_mate = window_best(table_mate, starts, near, near_first)
    far_mate = window_best(table_mate, starts, far, far_first)
    from_mate = lax.ppermute(jnp.maximum(near_mate, far_mate), both, mate)
    far_own = window_best(table_own, starts, far, far_first)
    best = jnp.maximum(jnp.maximum(near_own, far_own), from_mate)

    maxima = best * best * samples
    log_stat = jnp.log1p(maxima)
    sums = jnp.stack((jnp.sum(log_stat, axis=0), jnp.sum(log_stat * log_stat, axis=0)))
    everyone = ("gene", "var", "perm")
    count = lax.axis_size(everyone)
    blocks = lax.axis_size("gene")
    sent = lax.all_to_all(jnp.broadcast_to(sums[None], (count, *sums.shape)), everyone, 0, 0, tiled=True)
    per_block = jnp.sum(sent.reshape(blocks, count // blocks, *sums.shape), axis=1) / PERMS
    moments = lax.dynamic_index_in_dim(per_block, lax.axis_index("gene"), 0, keepdims=False)
    pooled = jnp.sum(per_block, axis=(0, 2)) / (gene_count * blocks)
    return (maxima, moments, pooled)


def solution(mesh):
    return jax.shard_map(
        shards_program,
        mesh=mesh,
        in_specs=(
            P("gene", ("var", "perm"), None),
            P("gene", None),
            P(("var", "perm"), None),
            P("gene"),
        ),
        out_specs=(P(("var", "perm"), "gene"), P(None, "gene"), P()),
        check_vma=False,
    )
```

time: 181 us -> 115 us (0.64)
  matrix products: 64 us -> 0 us
  Pallas kernels: 0 us -> 55.3 us
  waiting for transfers between devices: 72.2 us -> 21.2 us
  starting transfers between devices: 0.04 us -> 26.9 us
  blocking collectives: 19.7 us -> 0 us
  between operations: 14.1 us -> 0.74 us
  local copies, waits for them, and re-layouts: 0.04 us -> 6.57 us
  other arithmetic: 9.07 us -> 3.27 us
    all_gather x1 -> x0, waiting for transfers between devices: 72.2 us -> none  [shards(): shard_rows = lax.all_gather(standard, ('var', 'perm'), axis=0, tiled=True)]
    dot_general x17 -> x0, matrix products: 64 us -> none  [the longest x16 55.8 us: window_best(): lax.dot_general(row_block, perm_table, (((1,), (1,)), ((), ())), preferre...]
    pallas_call x0 -> x7, Pallas kernels: none -> 55.3 us  [the longest x4 40.8 us: window_best(): pl.pallas_call(functools.partial(score_kernel, count), grid=(groups,), in...]
    ppermute x0 -> x9, starting transfers between devices: none -> 20.4 us  [the longest x1 4.29 us: shards_program(): mate_rows = lax.ppermute(perm_rows, both, mate)]
    all_to_all x2 -> x0, blocking collectives: 19.7 us -> none  [sent_to_all(): lax.all_to_all(jnp.broadcast_to(array[None], (count, *array.shape)), axis...]
    ppermute x0 -> x9, waiting for transfers between devices: none -> 11.1 us  [the longest x1 8.07 us: shards_program(): below = lax.ppermute(own, 'var', along(1))]
    all_to_all x0 -> x1, waiting for transfers between devices: none -> 10.1 us  [shards_program(): lax.all_to_all(jnp.broadcast_to(sums[None], (count, *sums.shape)), everyo...]
    all_to_all x0 -> x1, starting transfers between devices: none -> 6.55 us  [shards_program(): lax.all_to_all(jnp.broadcast_to(sums[None], (count, *sums.shape)), everyo...]
  transfers between devices with their start and end apart: 1 -> 10, of which waited for: 1 -> 4; matrix products, arithmetic and copies ran while one was open for 5% -> 4% of each run, Pallas kernels for 0% -> 35%
where the time goes in v1:
time: 115 us; the launch traced here: 114 us
  Pallas kernels  55.3 us (48%)
  starting transfers between devices  26.9 us (23%)
  waiting for transfers between devices  21.2 us (18%)
  local copies, waits for them, and re-layouts  6.57 us (6%)
  other arithmetic  3.27 us (3%)
    pallas_call x4, Pallas kernels, window_best(): pl.pallas_call(functools.partial(score_kernel, count), grid=(groups,), in...  40.8 us
    pallas_call x2, Pallas kernels, perm_tables(): pl.pallas_call(functools.partial(table_kernel, per_step), grid=(steps,),...  11.4 us
    all_to_all x1, waiting for transfers between devices, shards_program(): lax.all_to_all(jnp.broadcast_to(sums[None], (count, *sums.shape)), everyo...  10.1 us
    ppermute x1, waiting for transfers between devices, shards_program(): below = lax.ppermute(own, 'var', along(1))  8.07 us
    all_to_all x1, starting transfers between devices, shards_program(): lax.all_to_all(jnp.broadcast_to(sums[None], (count, *sums.shape)), everyo...  6.55 us
    ppermute x1, starting transfers between devices, shards_program(): mate_rows = lax.ppermute(perm_rows, both, mate)  4.29 us
    ppermute x1, starting transfers between devices, shards_program(): from_mate = lax.ppermute(jnp.maximum(near_mate, far_mate), both, mate)  4.29 us
    ppermute x1, starting transfers between devices, shards_program(): deep = lax.ppermute(own, 'perm', across)  3.6 us
  transfers between devices with their start and end apart: 10, of which 4 were waited for; matrix products, arithmetic and copies ran while one was open for 4% of the time, Pallas kernels for 35%

profile of v1, /device:TPU:1, one launch (start us, length us, event | category | flops | bytes accessed | tf_op | source)
XLA Modules:
  0.0 114.0 jit_solution(10752332736499400117)
XLA Ops:
  0.6 3.1 %standard.1.refs_0_ = bf16[384,768]{1,0:T(8,128)(2,1)} custom-call(bf16[1,384,768]{2,1,0:T(8,128)(2,1)} %x_ref.1), custom_call_target="tpu_custom_call" | custom-call | tf_op jit(solution)/shard_map/standard/pallas_call | solution.py:30
  3.7 2.1 %collective-permute-start.1 = (bf16[384,768]{1,0:T(8,128)(2,1)}, bf16[384,768]{1,0:T(8,128)(2,1)S(1)}, u32[]{:S(2)}, u32[]{:S(2)}) collective-permute-start(bf16[384,768]{1,0:T(8,128)(2,1)} %standard.1.refs_0_), channel_id=1, source_target_pairs={{0,4},{2,6},{4,8},{6,10},{8,12},{10,14},{12,0},{14,2},{1,5},{3,7},... | collective-permute-start | bytes 1769480 | tf_op jit(solution)/shard_map/ppermute | solution.py:171
  5.8 1.4 %collective-permute-start.2 = (bf16[384,768]{1,0:T(8,128)(2,1)}, bf16[384,768]{1,0:T(8,128)(2,1)S(1)}, u32[]{:S(2)}, u32[]{:S(2)}) collective-permute-start(bf16[384,768]{1,0:T(8,128)(2,1)} %standard.1.refs_0_), channel_id=1, source_target_pairs={{0,12},{2,14},{4,0},{6,2},{8,4},{10,6},{12,8},{14,10},{1,13},{3,15... | collective-permute-start | bytes 1769480 | tf_op jit(solution)/shard_map/ppermute | solution.py:172
  7.3 3.6 %collective-permute-start.3 = (bf16[384,768]{1,0:T(8,128)(2,1)}, bf16[384,768]{1,0:T(8,128)(2,1)S(1)}, u32[]{:S(2)}, u32[]{:S(2)}) collective-permute-start(bf16[384,768]{1,0:T(8,128)(2,1)} %standard.1.refs_0_), channel_id=1, source_target_pairs={{0,1},{1,0},{2,3},{3,2},{4,5},{5,4},{6,7},{7,6},{8,9},{9,8},{10,11... | collective-permute-start | bytes 1769480 | tf_op jit(solution)/shard_map/ppermute | solution.py:173
  10.9 1.5 %collective-permute-start = (bf16[384,768]{1,0:T(8,128)(2,1)}, bf16[384,768]{1,0:T(8,128)(2,1)S(1)}, u32[]{:S(2)}, u32[]{:S(2)}) collective-permute-start(bf16[384,768]{1,0:T(8,128)(2,1)} %standard.1.refs_0_), channel_id=1, source_target_pairs={{0,2},{2,0},{4,6},{6,4},{8,10},{10,8},{12,14},{14,12},{1,3},{3,1},... | collective-permute-start | bytes 1769480 | tf_op jit(solution)/shard_map/ppermute | solution.py:174
  12.3 8.1 %collective-permute-done.1.refs_0_ = bf16[384,768]{1,0:T(8,128)(2,1)S(1)} collective-permute-done((bf16[384,768]{1,0:T(8,128)(2,1)}, bf16[384,768]{1,0:T(8,128)(2,1)S(1)}, u32[]{:S(2)}, u32[]{:S(2)}) %collective-permute-start.1) | collective-permute-done | bytes 589856 | tf_op jit(solution)/shard_map/ppermute | solution.py:171
  20.4 1.4 %collective-permute-start.4 = (bf16[384,768]{1,0:T(8,128)(2,1)S(1)}, bf16[384,768]{1,0:T(8,128)(2,1)S(1)}, u32[]{:S(2)}, u32[]{:S(2)}) collective-permute-start(bf16[384,768]{1,0:T(8,128)(2,1)S(1)} %collective-permute-done.1.refs_0_), channel_id=1, source_target_pairs={{0,2},{2,0},{4,6},{6,4},{8,10},{10,8},{12,14},{14,12},{1,3},{3,1},... | collective-permute-start | bytes 1769480 | tf_op jit(solution)/shard_map/ppermute | solution.py:183
  21.9 1.8 %collective-permute-done.3.refs_2_ = bf16[384,768]{1,0:T(8,128)(2,1)S(1)} collective-permute-done((bf16[384,768]{1,0:T(8,128)(2,1)}, bf16[384,768]{1,0:T(8,128)(2,1)S(1)}, u32[]{:S(2)}, u32[]{:S(2)}) %collective-permute-start.3) | collective-permute-done | bytes 589856 | tf_op jit(solution)/shard_map/ppermute | solution.py:173
  23.7 1.7 %collective-permute-start.6 = (bf16[384,768]{1,0:T(8,128)(2,1)S(1)}, bf16[384,768]{1,0:T(8,128)(2,1)}, u32[]{:S(2)}, u32[]{:S(2)}) collective-permute-start(bf16[384,768]{1,0:T(8,128)(2,1)S(1)} %collective-permute-done.3.refs_2_), channel_id=1, source_target_pairs={{0,2},{2,0},{4,6},{6,4},{8,10},{10,8},{12,14},{14,12},{1,3},{3,1},... | collective-permute-start | bytes 1769480 | tf_op jit(solution)/shard_map/ppermute | solution.py:183
  25.4 4.3 %collective-permute-start.7 = (s32[16,768]{1,0:T(8,128)}, s32[16,768]{1,0:T(8,128)}, u32[]{:S(2)}, u32[]{:S(2)}) collective-permute-start(s32[16,768]{1,0:T(8,128)} %param.6), channel_id=1, source_target_pairs={{0,9},{1,8},{2,11},{3,10},{4,13},{5,12},{6,15},{7,14},{8,1},{9,0},... | collective-permute-start | bytes 147464 | tf_op jit(solution)/shard_map/ppermute | solution.py:169
  31.7 1.2 %collective-permute-done.7 = s32[16,768]{1,0:T(8,128)} collective-permute-done((s32[16,768]{1,0:T(8,128)}, s32[16,768]{1,0:T(8,128)}, u32[]{:S(2)}, u32[]{:S(2)}) %collective-permute-start.7) | collective-permute-done | bytes 49184 | tf_op jit(solution)/shard_map/ppermute | solution.py:169
  32.9 1.4 %reshape.22.perm_ref = s32[4,4,768]{2,1,0:T(4,128)} reshape(s32[16,768]{1,0:T(8,128)} %collective-permute-done.7) | data formatting | bytes 98304 | tf_op jit(solution)/shard_map/reshape | solution.py:81
  34.3 5.7 %tables.3.table_ref = bf16[8,256,768]{2,1,0:T(8,128)(2,1)} custom-call(f32[128,768]{1,0:T(8,128)} %pheno_ref.3, s32[4,4,768]{2,1,0:T(4,128)} %reshape.22.perm_ref), custom_call_target="tpu_custom_call" | custom-call | tf_op jit(solution)/shard_map/tables/pallas_call | solution.py:70
  40.1 0.8 broadcast_in_dim.7.starts_ref
  40.9 8.1 %scores.6 = f32[16,128]{1,0:T(8,128)} custom-call(s32[2]{0:T(128)} %pad_add_fusion.first_ref, bf16[8,256,768]{2,1,0:T(8,128)(2,1)} %tables.3.table_ref, s32[8,16,128]{2,1,0:T(8,128)} %broadcast_in_dim.7.starts_ref, bf16[384,768]{1,0:T(8,128)(2,1)} %standard.1.refs_0_, bf16[384,768]{1,0:T(8,128)(2,1)} %copy-done), custom_call_target="tpu_custom_call" | custom-call | tf_op jit(solution)/shard_map/scores/pallas_call | solution.py:129
  49.1 0.8 copy-done.4
  50.1 12.3 %scores.7 = f32[16,128]{1,0:T(8,128)} custom-call(s32[6]{0:T(128)} %stack.58.first_ref, bf16[8,256,768]{2,1,0:T(8,128)(2,1)} %tables.3.table_ref, s32[8,16,128]{2,1,0:T(8,128)} %broadcast_in_dim.7.starts_ref, bf16[384,768]{1,0:T(8,128)(2,1)} %copy-done.1, bf16[384,768]{1,0:T(8,128)(2,1)} %copy-done.2, bf16[384,768]{1,0:T(8,128)(2,1)} %copy-done.3, ...), custom_call_target="tpu_custom_call" | custom-call | tf_op jit(solution)/shard_map/scores/pallas_call | solution.py:129
  63.1 4.3 %collective-permute-start.8 = (f32[16,128]{1,0:T(8,128)S(1)}, f32[16,128]{1,0:T(8,128)S(1)}, u32[]{:S(2)}, u32[]{:S(2)}) collective-permute-start(f32[16,128]{1,0:T(8,128)S(1)} %max.10), channel_id=1, source_target_pairs={{0,9},{1,8},{2,11},{3,10},{4,13},{5,12},{6,15},{7,14},{8,1},{9,0},... | collective-permute-start | bytes 24584 | tf_op jit(solution)/shard_map/ppermute | solution.py:188
  68.0 5.7 %tables.2.table_ref = bf16[8,256,768]{2,1,0:T(8,128)(2,1)} custom-call(f32[128,768]{1,0:T(8,128)} %pheno_ref.3, s32[4,4,768]{2,1,0:T(4,128)} %reshape.21.perm_ref), custom_call_target="tpu_custom_call" | custom-call | tf_op jit(solution)/shard_map/tables/pallas_call | solution.py:70
  73.7 8.1 %scores.4 = f32[16,128]{1,0:T(8,128)} custom-call(s32[2]{0:T(128)} %pad_add_fusion.first_ref, bf16[8,256,768]{2,1,0:T(8,128)(2,1)} %tables.2.table_ref, s32[8,16,128]{2,1,0:T(8,128)} %broadcast_in_dim.7.starts_ref, bf16[384,768]{1,0:T(8,128)(2,1)} %standard.1.refs_0_, bf16[384,768]{1,0:T(8,128)(2,1)} %copy-done), custom_call_target="tpu_custom_call" | custom-call | tf_op jit(solution)/shard_map/scores/pallas_call | solution.py:129
  81.8 12.3 %scores.5 = f32[16,128]{1,0:T(8,128)} custom-call(s32[6]{0:T(128)} %stack.58.first_ref, bf16[8,256,768]{2,1,0:T(8,128)(2,1)} %tables.2.table_ref, s32[8,16,128]{2,1,0:T(8,128)} %broadcast_in_dim.7.starts_ref, bf16[384,768]{1,0:T(8,128)(2,1)} %copy-done.1, bf16[384,768]{1,0:T(8,128)(2,1)} %copy-done.2, bf16[384,768]{1,0:T(8,128)(2,1)} %copy-done.3, ...), custom_call_target="tpu_custom_call" | custom-call | tf_op jit(solution)/shard_map/scores/pallas_call | solution.py:129
  94.1 1.3 %log-plus-one_reduce_fusion = (f32[128]{0:T(128)S(1)}, f32[128]{0:T(128)S(1)}, f32[16,128]{1,0:T(8,128)}) fusion(f32[16,128]{1,0:T(8,128)S(1)} %collective-permute-done.8, f32[16,128]{1,0:T(8,128)S(1)} %copy-done.8, f32[16,128]{1,0:T(8,128)} %scores.5), kind=kLoop, calls=%fused_computation.3 | loop fusion | flops 14080 | bytes 33792 | tf_op jit(solution)/shard_map/reduce_sum | solution.py:194
  96.1 6.6 %all-to-all-start = ((f32[128,2,128]{2,1,0:T(2,128)}), f32[128,2,128]{2,1,0:T(2,128)S(1)}, u32[]{:S(2)}, u32[]{:S(2)}) async-start(f32[128,2,128]{2,1,0:T(2,128)} %broadcast_in_dim.8), calls=%async_computation | async-start | bytes 262144 | tf_op jit(solution)/shard_map/all_to_all | solution.py:198
  102.7 10.1 %all-to-all-done = f32[128,2,128]{2,1,0:T(2,128)S(1)} async-done(((f32[128,2,128]{2,1,0:T(2,128)}), f32[128,2,128]{2,1,0:T(2,128)S(1)}, u32[]{:S(2)}, u32[]{:S(2)}) %all-to-all-start) | async-done | bytes 131104 | tf_op jit(solution)/shard_map/all_to_all | solution.py:198
  (35 shorter events, 5.6 us)
Async XLA Ops:
  3.7 16.7 %collective-permute-start.1 = (bf16[384,768]{1,0:T(8,128)(2,1)}, bf16[384,768]{1,0:T(8,128)(2,1)S(1)}, u32[]{:S(2)}, u32[]{:S(2)}) collective-permute-start(bf16[384,768]{1,0:T(8,128)(2,1)} %standard.1.refs_0_), channel_id=1, source_target_pairs={{0,4},{2,6},{4,8},{6,10},{8,12},{10,14},{12,0},{14,2},{1,5},{3,7},... | collective-permute-start | bytes 1769480 | tf_op jit(solution)/shard_map/ppermute | solution.py:171
  5.8 15.9 %collective-permute-start.2 = (bf16[384,768]{1,0:T(8,128)(2,1)}, bf16[384,768]{1,0:T(8,128)(2,1)S(1)}, u32[]{:S(2)}, u32[]{:S(2)}) collective-permute-start(bf16[384,768]{1,0:T(8,128)(2,1)} %standard.1.refs_0_), channel_id=1, source_target_pairs={{0,12},{2,14},{4,0},{6,2},{8,4},{10,6},{12,8},{14,10},{1,13},{3,15... | collective-permute-start | bytes 1769480 | tf_op jit(solution)/shard_map/ppermute | solution.py:172
  7.3 16.4 %collective-permute-start.3 = (bf16[384,768]{1,0:T(8,128)(2,1)}, bf16[384,768]{1,0:T(8,128)(2,1)S(1)}, u32[]{:S(2)}, u32[]{:S(2)}) collective-permute-start(bf16[384,768]{1,0:T(8,128)(2,1)} %standard.1.refs_0_), channel_id=1, source_target_pairs={{0,1},{1,0},{2,3},{3,2},{4,5},{5,4},{6,7},{7,6},{8,9},{9,8},{10,11... | collective-permute-start | bytes 1769480 | tf_op jit(solution)/shard_map/ppermute | solution.py:173
  10.9 29.2 %collective-permute-start = (bf16[384,768]{1,0:T(8,128)(2,1)}, bf16[384,768]{1,0:T(8,128)(2,1)S(1)}, u32[]{:S(2)}, u32[]{:S(2)}) collective-permute-start(bf16[384,768]{1,0:T(8,128)(2,1)} %standard.1.refs_0_), channel_id=1, source_target_pairs={{0,2},{2,0},{4,6},{6,4},{8,10},{10,8},{12,14},{14,12},{1,3},{3,1},... | collective-permute-start | bytes 1769480 | tf_op jit(solution)/shard_map/ppermute | solution.py:174
  20.4 28.6 %copy-start.1 = (bf16[384,768]{1,0:T(8,128)(2,1)}, bf16[384,768]{1,0:T(8,128)(2,1)S(1)}, u32[]{:S(2)}) copy-start(bf16[384,768]{1,0:T(8,128)(2,1)S(1)} %collective-permute-done.1.refs_0_) | copy-start | bytes 1769476
  20.4 28.6 %collective-permute-start.4 = (bf16[384,768]{1,0:T(8,128)(2,1)S(1)}, bf16[384,768]{1,0:T(8,128)(2,1)S(1)}, u32[]{:S(2)}, u32[]{:S(2)}) collective-permute-start(bf16[384,768]{1,0:T(8,128)(2,1)S(1)} %collective-permute-done.1.refs_0_), channel_id=1, source_target_pairs={{0,2},{2,0},{4,6},{6,4},{8,10},{10,8},{12,14},{14,12},{1,3},{3,1},... | collective-permute-start | bytes 1769480 | tf_op jit(solution)/shard_map/ppermute | solution.py:183
  21.8 27.2 %copy-start.2 = (bf16[384,768]{1,0:T(8,128)(2,1)}, bf16[384,768]{1,0:T(8,128)(2,1)S(1)}, u32[]{:S(2)}) copy-start(bf16[384,768]{1,0:T(8,128)(2,1)S(1)} %collective-permute-done.2.refs_1_) | copy-start | bytes 1769476
  21.8 27.3 %collective-permute-start.5 = (bf16[384,768]{1,0:T(8,128)(2,1)S(1)}, bf16[384,768]{1,0:T(8,128)(2,1)S(1)}, u32[]{:S(2)}, u32[]{:S(2)}) collective-permute-start(bf16[384,768]{1,0:T(8,128)(2,1)S(1)} %collective-permute-done.2.refs_1_), channel_id=1, source_target_pairs={{0,2},{2,0},{4,6},{6,4},{8,10},{10,8},{12,14},{14,12},{1,3},{3,1},... | collective-permute-start | bytes 1769480 | tf_op jit(solution)/shard_map/ppermute | solution.py:183
  23.6 25.3 %copy-start.3 = (bf16[384,768]{1,0:T(8,128)(2,1)}, bf16[384,768]{1,0:T(8,128)(2,1)S(1)}, u32[]{:S(2)}) copy-start(bf16[384,768]{1,0:T(8,128)(2,1)S(1)} %collective-permute-done.3.refs_2_) | copy-start | bytes 1769476
  23.7 25.4 %collective-permute-start.6 = (bf16[384,768]{1,0:T(8,128)(2,1)S(1)}, bf16[384,768]{1,0:T(8,128)(2,1)}, u32[]{:S(2)}, u32[]{:S(2)}) collective-permute-start(bf16[384,768]{1,0:T(8,128)(2,1)S(1)} %collective-permute-done.3.refs_2_), channel_id=1, source_target_pairs={{0,2},{2,0},{4,6},{6,4},{8,10},{10,8},{12,14},{14,12},{1,3},{3,1},... | collective-permute-start | bytes 1769480 | tf_op jit(solution)/shard_map/ppermute | solution.py:183
  25.4 7.5 %collective-permute-start.7 = (s32[16,768]{1,0:T(8,128)}, s32[16,768]{1,0:T(8,128)}, u32[]{:S(2)}, u32[]{:S(2)}) collective-permute-start(s32[16,768]{1,0:T(8,128)} %param.6), channel_id=1, source_target_pairs={{0,9},{1,8},{2,11},{3,10},{4,13},{5,12},{6,15},{7,14},{8,1},{9,0},... | collective-permute-start | bytes 147464 | tf_op jit(solution)/shard_map/ppermute | solution.py:169
  40.1 0.8 copy-start
  49.0 13.4 %copy-start.7 = (f32[16,128]{1,0:T(8,128)S(1)}, f32[16,128]{1,0:T(8,128)}, u32[]{:S(2)}) copy-start(f32[16,128]{1,0:T(8,128)} %scores.6) | copy-start | bytes 24580
  49.0 18.4 %copy-start.6 = (s32[16,768]{1,0:T(8,128)S(1)}, s32[16,768]{1,0:T(8,128)}, u32[]{:S(2)}) copy-start(s32[16,768]{1,0:T(8,128)} %param.6) | copy-start | bytes 147460
  49.0 0.8 copy-start.4
  49.0 1.0 copy-start.5
  63.1 31.0 %collective-permute-start.8 = (f32[16,128]{1,0:T(8,128)S(1)}, f32[16,128]{1,0:T(8,128)S(1)}, u32[]{:S(2)}, u32[]{:S(2)}) collective-permute-start(f32[16,128]{1,0:T(8,128)S(1)} %max.10), channel_id=1, source_target_pairs={{0,9},{1,8},{2,11},{3,10},{4,13},{5,12},{6,15},{7,14},{8,1},{9,0},... | collective-permute-start | bytes 24584 | tf_op jit(solution)/shard_map/ppermute | solution.py:188
  81.8 12.3 %copy-start.8 = (f32[16,128]{1,0:T(8,128)S(1)}, f32[16,128]{1,0:T(8,128)}, u32[]{:S(2)}) copy-start(f32[16,128]{1,0:T(8,128)} %scores.4) | copy-start | bytes 24580
  96.1 16.7 %all-to-all-start = ((f32[128,2,128]{2,1,0:T(2,128)}), f32[128,2,128]{2,1,0:T(2,128)S(1)}, u32[]{:S(2)}, u32[]{:S(2)}) async-start(f32[128,2,128]{2,1,0:T(2,128)} %broadcast_in_dim.8), calls=%async_computation | async-start | bytes 262144 | tf_op jit(solution)/shard_map/all_to_all | solution.py:198

commit v2 on v1

v2 whole, which is shorter than its diff:
```python
import functools

import jax
import jax.numpy as jnp
from jax import lax
from jax.experimental import pallas as pl
from jax.experimental.pallas import tpu as pltpu
from jax.sharding import PartitionSpec as P

WINDOW = 4096
PERMS = 256
FOLD = 256
TILE = 256
LARGE = 3.0e38


def standardized(values):
    centred = values - jnp.mean(values, axis=1, keepdims=True)
    inv_norm = lax.rsqrt(jnp.sum(centred * centred, axis=1, keepdims=True) + 1.0)
    return (centred * inv_norm).astype(jnp.bfloat16)


def standard_kernel(x_ref, o_ref):
    o_ref[...] = standardized(x_ref[0].astype(jnp.float32))


def standard_rows(genotypes):
    _, rows, samples = genotypes.shape
    step = rows // 3
    return pl.pallas_call(
        standard_kernel,
        grid=(3,),
        in_specs=[pl.BlockSpec((1, step, samples), lambda i: (0, i, 0))],
        out_specs=pl.BlockSpec((step, samples), lambda i: (i, 0)),
        out_shape=jax.ShapeDtypeStruct((rows, samples), jnp.bfloat16),
        cost_estimate=cost(8 * rows * samples),
        compiler_params=params(16),
        name="standard",
    )(genotypes)


def cost(flops):
    return pl.CostEstimate(flops=flops, bytes_accessed=0, transcendentals=0)


def places(local):
    var_n, me, z = lax.axis_size("var"), lax.axis_index("var"), lax.axis_index("perm")
    rows_n = var_n // 2
    y, core = lax.div(me, 2), lax.rem(me, 2)

    def first(up, same_core, same_depth):
        c = core if same_core else 1 - core
        d = z if same_depth else 1 - z
        return ((lax.rem(y + up + rows_n, rows_n) * 2 + c) * 2 + d) * local

    near = [first(0, True, True), first(0, False, True)]
    far = [first(u, c, d) for c in (True, False) for u, d in ((-1, True), (1, True), (0, False))]
    return near, far


def fill_masks(firsts, lead, mask_ref, local):
    half = TILE // 2
    lane = lax.broadcasted_iota(jnp.int32, lead.shape, 1)
    for i in range(len(firsts)):
        for r in range(0, local, half):
            past = lane + (firsts[i] + r) - lead
            inside = (past >= 0) & (past < WINDOW)
            at = i * local + r
            mask_ref[:, at:at + half] = jnp.where(inside, LARGE, 0.0)


def weight_tiles(shards, local):
    half = TILE // 2
    pieces = [(i, r) for i in range(len(shards)) for r in range(0, local, half)]
    for t in range(0, len(pieces), 2):
        pair = pieces[t:t + 2]
        yield t * half, jnp.concatenate([shards[i][r:r + half, :] for i, r in pair], axis=0)


def lane_best(rows_bf16, shards, local, mask_ref, copies):
    half = TILE // 2
    genes = mask_ref.shape[0]
    best = None
    for at, weights in weight_tiles(shards, local):
        scores = lax.dot_general(
            rows_bf16, weights, (((1,), (1,)), ((), ())), preferred_element_type=jnp.float32
        )
        for n in range(weights.shape[0] // half):
            part = jnp.abs(scores[:, n * half:(n + 1) * half]).reshape(copies, genes, half)
            part = jnp.minimum(part, mask_ref[:, at + n * half:at + (n + 1) * half][None])
            best = part if best is None else jnp.maximum(best, part)
    return best


def reduce_lanes(best_ref, out_ref):
    perms, genes, half = best_ref.shape
    lane = lax.broadcasted_iota(jnp.int32, (genes, half), 1)
    gene = lax.broadcasted_iota(jnp.int32, (genes, half), 0)
    for p in range(perms):
        top = jnp.max(best_ref[p], axis=1, keepdims=True)
        out_ref[p:p + 1, :] = jnp.max(jnp.where(lane == gene, top, 0.0), axis=0, keepdims=True)


def near_kernel(per_step, pheno_ref, perm_ref, mate_ref, starts_ref, own_ref, twin_ref,
                table_ref, out_ref, lead_ref, base_ref, rows_ref, mask_ref, best_ref):
    genes, samples = pheno_ref.shape
    folds = samples // FOLD
    local = own_ref.shape[0]
    half_perms = perm_ref.shape[0]
    step = pl.program_id(0)

    @pl.when(step == 0)
    def _():
        std = standardized(pheno_ref[...])
        for b in range(folds):
            base_ref[b * genes:(b + 1) * genes, :] = std[:, b * FOLD:(b + 1) * FOLD]
        rows_ref[:half_perms, :] = perm_ref[...]
        rows_ref[half_perms:, :] = mate_ref[...]
        wide = jnp.broadcast_to(starts_ref[...].astype(jnp.float32), lead_ref.shape)
        lead = wide.T.astype(jnp.int32)
        lead_ref[...] = lead
        fill_masks(places(local)[0], lead, mask_ref, local)

    within = lax.broadcasted_iota(jnp.int32, (FOLD, samples), 0)
    for k in range(per_step):
        index = rows_ref[pl.ds(step * per_step + k, 1), :]
        low = jnp.bitwise_and(index, FOLD - 1)
        block = jnp.right_shift(index, FOLD.bit_length() - 1)
        hot = jnp.where(within == low, 1.0, 0.0).astype(jnp.bfloat16)
        picked = jnp.dot(base_ref[...], hot, preferred_element_type=jnp.float32)
        chosen = picked[:genes]
        for b in range(1, folds):
            chosen = jnp.where(block == b, picked[b * genes:(b + 1) * genes], chosen)
        table_ref[k * genes:(k + 1) * genes, :] = chosen.astype(jnp.bfloat16)
    best = lane_best(table_ref[...], (own_ref, twin_ref), local, mask_ref, per_step)
    best_ref[pl.ds(step * per_step, per_step)] = best

    @pl.when(step == pl.num_programs(0) - 1)
    def _():
        reduce_lanes(best_ref, out_ref)


def params(limit):
    return pltpu.CompilerParams(vmem_limit_bytes=limit * 1024 * 1024)


def near_best(phenotypes, perm_rows, mate_rows, starts, shards):
    genes, samples = phenotypes.shape
    perms = perm_rows.shape[0] + mate_rows.shape[0]
    local = shards[0].shape[0]
    per_step = 2
    once = pl.Buffered(1)

    def whole(shape):
        return pl.BlockSpec(shape, lambda i: (0, 0), pipeline_mode=once)

    return pl.pallas_call(
        functools.partial(near_kernel, per_step),
        grid=(perms // per_step,),
        in_specs=[
            whole((genes, samples)),
            whole(perm_rows.shape),
            whole(mate_rows.shape),
            whole((1, genes)),
            whole((local, samples)),
            whole((local, samples)),
        ],
        out_specs=[
            pl.BlockSpec((per_step * genes, samples), lambda i: (i, 0)),
            pl.BlockSpec((perms, genes), lambda i: (0, 0)),
            pl.BlockSpec((genes, TILE // 2), lambda i: (0, 0)),
        ],
        out_shape=[
            jax.ShapeDtypeStruct((perms * genes, samples), jnp.bfloat16),
            jax.ShapeDtypeStruct((perms, genes), jnp.float32),
            jax.ShapeDtypeStruct((genes, TILE // 2), jnp.int32),
        ],
        scratch_shapes=[
            pltpu.VMEM((samples // FOLD * genes, FOLD), jnp.bfloat16),
            pltpu.VMEM((perms, samples), jnp.int32),
            pltpu.VMEM((genes, 2 * local), jnp.float32),
            pltpu.VMEM((perms, genes, TILE // 2), jnp.float32),
        ],
        cost_estimate=cost(2 * perms * genes * samples * (2 * local + samples)),
        compiler_params=params(24),
        name="near",
    )(phenotypes, perm_rows, mate_rows, starts.reshape(1, genes), *shards)


def far_kernel(count, per_step, table_ref, lead_ref, before_ref, *refs):
    shards, (out_ref, mask_ref, best_ref) = refs[:count], refs[count:]
    local = shards[0].shape[0]
    step = pl.program_id(0)

    @pl.when(step == 0)
    def _():
        fill_masks(places(local)[1], lead_ref[...], mask_ref, local)

    best = lane_best(table_ref[...], shards, local, mask_ref, per_step)
    best_ref[pl.ds(step * per_step, per_step)] = best

    @pl.when(step == pl.num_programs(0) - 1)
    def _():
        reduce_lanes(best_ref, out_ref)
        out_ref[...] = jnp.maximum(out_ref[...], before_ref[...])


def far_best(table, part, lead, before, shards):
    samples = table.shape[1]
    genes = lead.shape[0]
    perms = before.shape[0] // 2
    local = shards[0].shape[0]
    count = len(shards)
    per_step = 2
    steps = perms // per_step
    once = pl.Buffered(1)
    whole = pl.BlockSpec((local, samples), lambda i: (0, 0), pipeline_mode=once)
    return pl.pallas_call(
        functools.partial(far_kernel, count, per_step),
        grid=(steps,),
        in_specs=[
            pl.BlockSpec((per_step * genes, samples), lambda i: (i + part * steps, 0)),
            pl.BlockSpec(lead.shape, lambda i: (0, 0), pipeline_mode=once),
            pl.BlockSpec((perms, genes), lambda i: (part, 0), pipeline_mode=once),
            *[whole] * count,
        ],
        out_specs=pl.BlockSpec((perms, genes), lambda i: (0, 0)),
        out_shape=jax.ShapeDtypeStruct((perms, genes), jnp.float32),
        scratch_shapes=[
            pltpu.VMEM((genes, count * local), jnp.float32),
            pltpu.VMEM((perms, genes, TILE // 2), jnp.float32),
        ],
        cost_estimate=cost(2 * perms * genes * samples * count * local),
        compiler_params=params(24),
        name="far",
    )(table, lead, before, *shards)


def finish_kernel(spread, best_ref, mate_ref, maxima_ref, sums_ref, *, samples):
    best = jnp.maximum(best_ref[...], mate_ref[...])
    maxima = best * best * samples
    maxima_ref[...] = maxima
    log_stat = jnp.log1p(maxima)
    sums = jnp.stack((jnp.sum(log_stat, axis=0), jnp.sum(log_stat * log_stat, axis=0)))
    sums_ref[...] = jnp.broadcast_to(sums[None], sums_ref.shape)


def finished(best, from_mate, samples, spread):
    perms, genes = best.shape
    return pl.pallas_call(
        functools.partial(finish_kernel, spread, samples=samples),
        out_shape=[
            jax.ShapeDtypeStruct((perms, genes), jnp.float32),
            jax.ShapeDtypeStruct((spread, 2, genes), jnp.float32),
        ],
        compiler_params=params(4),
        name="finish",
    )(best, from_mate)


def shards_program(genotypes, phenotypes, perm_rows, starts):
    var_n = lax.axis_size("var")
    rows_n = var_n // 2
    both = ("var", "perm")
    samples = phenotypes.shape[1]
    gene_count = phenotypes.shape[0]

    def along(step):
        return [(v, ((v // 2 + step) % rows_n) * 2 + v % 2) for v in range(var_n)]

    twin = [(v, v ^ 1) for v in range(var_n)]
    across = [(0, 1), (1, 0)]
    mate = [
        (v * 2 + z, ((((v // 2 + rows_n // 2) % rows_n) * 2 + v % 2) * 2 + 1 - z))
        for v in range(var_n) for z in range(2)
    ]

    mate_rows = lax.ppermute(perm_rows, both, mate)
    own = standard_rows(genotypes)
    below = lax.ppermute(own, "var", along(1))
    above = lax.ppermute(own, "var", along(-1))
    deep = lax.ppermute(own, "perm", across)
    own_twin = lax.ppermute(own, "var", twin)
    table, near, lead = near_best(phenotypes, perm_rows, mate_rows, starts, (own, own_twin))
    below, above, deep, lead = lax.optimization_barrier((below, above, deep, lead))
    far = [below, above, deep]
    far = far + [lax.ppermute(f, "var", twin) for f in far]
    to_mate = far_best(table, 1, lead, near, far)
    from_mate = lax.ppermute(to_mate, both, mate)
    best = far_best(table, 0, lead, near, far)
    count = lax.axis_size(("gene", "var", "perm"))
    maxima, sums = finished(best, from_mate, samples, count)

    everyone = ("gene", "var", "perm")
    blocks = lax.axis_size("gene")
    sent = lax.all_to_all(sums, everyone, 0, 0, tiled=True)
    per_block = jnp.sum(sent.reshape(blocks, count // blocks, *sums.shape[1:]), axis=1) / PERMS
    moments = lax.dynamic_index_in_dim(per_block, lax.axis_index("gene"), 0, keepdims=False)
    pooled = jnp.sum(per_block, axis=(0, 2)) / (gene_count * blocks)
    return (maxima, moments, pooled)


def solution(mesh):
    return jax.shard_map(
        shards_program,
        mesh=mesh,
        in_specs=(
            P("gene", ("var", "perm"), None),
            P("gene", None),
            P(("var", "perm"), None),
            P("gene"),
        ),
        out_specs=(P(("var", "perm"), "gene"), P(None, "gene"), P()),
        check_vma=False,
    )
```

time: 115 us -> 78.5 us (0.68)
  Pallas kernels: 55.3 us -> 37.1 us
  waiting for transfers between devices: 21.2 us -> 12.9 us
  starting transfers between devices: 26.9 us -> 22.7 us
  other arithmetic: 3.27 us -> 0.68 us
  local copies, waits for them, and re-layouts: 6.57 us -> 4.06 us
    pallas_call x6 -> x4, Pallas kernels: 52.2 us -> 36.3 us  [the longest x2 19.2 us: far_best(): pl.pallas_call(functools.partial(far_kernel, count, per_step), grid=(step...]
    ppermute x1, waiting for transfers between devices: 8.07 us -> 0.01 us  [shards_program(): below = lax.ppermute(own, 'var', along(1))]
    ppermute x1, starting transfers between devices: 3.6 us -> 0.01 us  [shards_program(): deep = lax.ppermute(own, 'perm', across)]
    ppermute x3, waiting for transfers between devices: 0.01 us -> 2.81 us  [shards_program(): far = far + [lax.ppermute(f, 'var', twin) for f in far]]
    unnamed x18 -> x8, local copies, waits for them, and re-layouts: 1.08 us -> 3.5 us
    pallas_call x1, Pallas kernels: 3.09 us -> 0.71 us  [standard_rows(): pl.pallas_call(standard_kernel, grid=(3,), in_specs=[pl.BlockSpec((1, ste...]
    broadcast_in_dim x3 -> x0, local copies, waits for them, and re-layouts: 2.2 us -> none  [the longest x2 1.52 us: window_best(): jnp.broadcast_to(starts.reshape(groups, GROUP, 1), (groups, GROUP, TILE /...]
    reshape x2 -> x0, local copies, waits for them, and re-layouts: 2.05 us -> none  [perm_tables(): perm_rows.reshape(steps, per_step, samples)]
  transfers between devices with their start and end apart: 10 -> 10, of which waited for: 4 -> 4; matrix products, arithmetic and copies ran while one was open for 4% -> 0% of each run, Pallas kernels for 35% -> 33%
where the time goes in v2:
time: 78.5 us; the launch traced here: 78.2 us
  Pallas kernels  37.1 us (47%)
  starting transfers between devices  22.7 us (29%)
  waiting for transfers between devices  12.9 us (16%)
  local copies, waits for them, and re-layouts  4.06 us (5%)
    pallas_call x2, Pallas kernels, far_best(): pl.pallas_call(functools.partial(far_kernel, count, per_step), grid=(step...  19.2 us
    pallas_call x1, Pallas kernels, near_best(): pl.pallas_call(functools.partial(near_kernel, per_step), grid=(perms // p...  16.4 us
    all_to_all x1, waiting for transfers between devices, shards_program(): sent = lax.all_to_all(sums, everyone, 0, 0, tiled=True)  10.1 us
    ppermute x1, starting transfers between devices, shards_program(): mate_rows = lax.ppermute(perm_rows, both, mate)  6.34 us
    all_to_all x1, starting transfers between devices, shards_program(): sent = lax.all_to_all(sums, everyone, 0, 0, tiled=True)  5.44 us
    ppermute x1, starting transfers between devices, shards_program(): from_mate = lax.ppermute(to_mate, both, mate)  5.28 us
    unnamed x8, local copies, waits for them, and re-layouts  3.5 us
    ppermute x3, waiting for transfers between devices, shards_program(): far = far + [lax.ppermute(f, 'var', twin) for f in far]  2.81 us
  transfers between devices with their start and end apart: 10, of which 4 were waited for; matrix products, arithmetic and copies ran while one was open for 0% of the time, Pallas kernels for 33%

profile of v2, /device:TPU:1, one launch (start us, length us, event | category | flops | bytes accessed | tf_op | source)
XLA Modules:
  0.0 78.2 jit_solution(17815543890240183351)
XLA Ops:
  0.6 1.1 %copy-done = bf16[1,384,768]{2,1,0:T(8,128)(2,1)S(1)} copy-done((bf16[1,384,768]{2,1,0:T(8,128)(2,1)S(1)}, bf16[1,384,768]{2,1,0:T(8,128)(2,1)}, u32[]{:S(2)}) %copy-start) | copy-done | bytes 589848
  1.7 0.7 standard.1.own_ref
  2.4 1.5 %collective-permute-start.1 = (bf16[384,768]{1,0:T(8,128)(2,1)S(1)}, bf16[384,768]{1,0:T(8,128)(2,1)S(1)}, u32[]{:S(2)}, u32[]{:S(2)}) collective-permute-start(bf16[384,768]{1,0:T(8,128)(2,1)S(1)} %standard.1.own_ref), channel_id=1, source_target_pairs={{0,2},{2,0},{4,6},{6,4},{8,10},{10,8},{12,14},{14,12},{1,3},{3,1},... | collective-permute-start | bytes 1769480 | tf_op jit(solution)/shard_map/ppermute | solution.py:283
  3.9 6.3 %collective-permute-start = (s32[16,768]{1,0:T(8,128)}, s32[16,768]{1,0:T(8,128)S(1)}, u32[]{:S(2)}, u32[]{:S(2)}) collective-permute-start(s32[16,768]{1,0:T(8,128)} %perm_ref.1), channel_id=1, source_target_pairs={{0,9},{1,8},{2,11},{3,10},{4,13},{5,12},{6,15},{7,14},{8,1},{9,0},... | collective-permute-start | bytes 147464 | tf_op jit(solution)/shard_map/ppermute | solution.py:278
  10.2 0.4 collective-permute-start.2
  10.6 2.3 %collective-permute-start.3 = (bf16[384,768]{1,0:T(8,128)(2,1)S(1)}, bf16[384,768]{1,0:T(8,128)(2,1)S(1)}, u32[]{:S(2)}, u32[]{:S(2)}) collective-permute-start(bf16[384,768]{1,0:T(8,128)(2,1)S(1)} %standard.1.own_ref), channel_id=1, source_target_pairs={{0,12},{2,14},{4,0},{6,2},{8,4},{10,6},{12,8},{14,10},{1,13},{3,15... | collective-permute-start | bytes 1769480 | tf_op jit(solution)/shard_map/ppermute | solution.py:281
  12.9 1.0 %copy-done.1 = f32[128,768]{1,0:T(8,128)S(1)} copy-done((f32[128,768]{1,0:T(8,128)S(1)}, f32[128,768]{1,0:T(8,128)}, u32[]{:S(2)}) %copy-start.1) | copy-done | bytes 393240
  13.9 0.8 %copy-done.2 = s32[16,768]{1,0:T(8,128)S(1)} copy-done((s32[16,768]{1,0:T(8,128)S(1)}, s32[16,768]{1,0:T(8,128)}, u32[]{:S(2)}) %copy-start.2) | copy-done | bytes 49176
  14.7 0.7 copy-done.3
  15.4 16.4 %near.1 = (bf16[4096,768]{1,0:T(8,128)(2,1)S(1)}, f32[32,128]{1,0:T(8,128)S(1)}, s32[128,128]{1,0:T(8,128)S(1)}) custom-call(f32[128,768]{1,0:T(8,128)S(1)} %copy-done.1, s32[16,768]{1,0:T(8,128)S(1)} %copy-done.2, s32[16,768]{1,0:T(8,128)S(1)} %collective-permute-done.mate_ref, s32[1,128]{1,0:T(1,128)S(1)} %bitcast.5, ...), custom_call_target="tpu_custom_call" | custom-call | flops 9663676416 | tf_op jit(solution)/shard_map/near/pallas_call | solution.py:157
  31.8 1.0 %collective-permute-start.5 = (bf16[384,768]{1,0:T(8,128)(2,1)S(1)}, bf16[384,768]{1,0:T(8,128)(2,1)S(1)}, u32[]{:S(2)}, u32[]{:S(2)}) collective-permute-start(bf16[384,768]{1,0:T(8,128)(2,1)S(1)} %collective-permute-done.2.refs_0_), channel_id=1, source_target_pairs={{0,2},{2,0},{4,6},{6,4},{8,10},{10,8},{12,14},{14,12},{1,3},{3,1},... | collective-permute-start | bytes 1769480 | tf_op jit(solution)/shard_map/ppermute | solution.py:287
  32.9 0.4 collective-permute-start.7
  33.3 1.1 %collective-permute-done.5.refs_3_ = bf16[384,768]{1,0:T(8,128)(2,1)S(1)} collective-permute-done((bf16[384,768]{1,0:T(8,128)(2,1)S(1)}, bf16[384,768]{1,0:T(8,128)(2,1)S(1)}, u32[]{:S(2)}, u32[]{:S(2)}) %collective-permute-start.5) | collective-permute-done | bytes 589856 | tf_op jit(solution)/shard_map/ppermute | solution.py:287
  34.4 0.8 %collective-permute-done.6.refs_4_ = bf16[384,768]{1,0:T(8,128)(2,1)S(1)} collective-permute-done((bf16[384,768]{1,0:T(8,128)(2,1)S(1)}, bf16[384,768]{1,0:T(8,128)(2,1)S(1)}, u32[]{:S(2)}, u32[]{:S(2)}) %collective-permute-start.6) | collective-permute-done | bytes 589856 | tf_op jit(solution)/shard_map/ppermute | solution.py:287
  35.3 0.8 %collective-permute-done.7.refs_5_ = bf16[384,768]{1,0:T(8,128)(2,1)S(1)} collective-permute-done((bf16[384,768]{1,0:T(8,128)(2,1)S(1)}, bf16[384,768]{1,0:T(8,128)(2,1)S(1)}, u32[]{:S(2)}, u32[]{:S(2)}) %collective-permute-start.7) | collective-permute-done | bytes 589856 | tf_op jit(solution)/shard_map/ppermute | solution.py:287
  36.1 9.6 %far.3 = f32[16,128]{1,0:T(8,128)S(1)} custom-call(bf16[4096,768]{1,0:T(8,128)(2,1)S(1)} %get-tuple-element.12.table_ref, s32[128,128]{1,0:T(8,128)S(1)} %get-tuple-element.14.lead_ref, f32[32,128]{1,0:T(8,128)S(1)} %get-tuple-element.15.before_ref, bf16[384,768]{1,0:T(8,128)(2,1)S(1)} %collective-permute-done.2.refs_0_, ...), custom_call_target="tpu_custom_call" | custom-call | flops 7247757312 | tf_op jit(solution)/shard_map/far/pallas_call | solution.py:218
  45.8 5.3 %collective-permute-start.8 = (f32[16,128]{1,0:T(8,128)S(1)}, f32[16,128]{1,0:T(8,128)S(1)}, u32[]{:S(2)}, u32[]{:S(2)}) collective-permute-start(f32[16,128]{1,0:T(8,128)S(1)} %far.3), channel_id=1, source_target_pairs={{0,9},{1,8},{2,11},{3,10},{4,13},{5,12},{6,15},{7,14},{8,1},{9,0},... | collective-permute-start | bytes 24584 | tf_op jit(solution)/shard_map/ppermute | solution.py:289
  51.0 9.6 %far.2.best_ref = f32[16,128]{1,0:T(8,128)S(1)} custom-call(bf16[4096,768]{1,0:T(8,128)(2,1)S(1)} %get-tuple-element.12.table_ref, s32[128,128]{1,0:T(8,128)S(1)} %get-tuple-element.14.lead_ref, f32[32,128]{1,0:T(8,128)S(1)} %get-tuple-element.15.before_ref, bf16[384,768]{1,0:T(8,128)(2,1)S(1)} %collective-permute-done.2.refs_0_, ...), custom_call_target="tpu_custom_call" | custom-call | flops 7247757312 | tf_op jit(solution)/shard_map/far/pallas_call | solution.py:218
  60.7 0.7 finish.1
  61.4 5.4 %all-to-all-start = ((f32[128,2,128]{2,1,0:T(2,128)}), f32[128,2,128]{2,1,0:T(2,128)S(1)}, u32[]{:S(2)}, u32[]{:S(2)}) async-start(f32[128,2,128]{2,1,0:T(2,128)} %get-tuple-element.20), calls=%async_computation | async-start | bytes 262144 | tf_op jit(solution)/shard_map/all_to_all | solution.py:296
  66.8 10.1 %all-to-all-done = f32[128,2,128]{2,1,0:T(2,128)S(1)} async-done(((f32[128,2,128]{2,1,0:T(2,128)}), f32[128,2,128]{2,1,0:T(2,128)S(1)}, u32[]{:S(2)}, u32[]{:S(2)}) %all-to-all-start) | async-done | bytes 131104 | tf_op jit(solution)/shard_map/all_to_all | solution.py:296
  77.0 0.1 fusion
  77.1 0.5 broadcast_multiply_fusion.1
  77.6 0.6 dynamic-slice_bitcast_fusion
  (13 shorter events, 0.2 us)
Async XLA Ops:
  0.6 1.1 %copy-start = (bf16[1,384,768]{2,1,0:T(8,128)(2,1)S(1)}, bf16[1,384,768]{2,1,0:T(8,128)(2,1)}, u32[]{:S(2)}) copy-start(bf16[1,384,768]{2,1,0:T(8,128)(2,1)} %x_ref.1) | copy-start | bytes 1769476
  2.4 10.5 %collective-permute-start.1 = (bf16[384,768]{1,0:T(8,128)(2,1)S(1)}, bf16[384,768]{1,0:T(8,128)(2,1)S(1)}, u32[]{:S(2)}, u32[]{:S(2)}) collective-permute-start(bf16[384,768]{1,0:T(8,128)(2,1)S(1)} %standard.1.own_ref), channel_id=1, source_target_pairs={{0,2},{2,0},{4,6},{6,4},{8,10},{10,8},{12,14},{14,12},{1,3},{3,1},... | collective-permute-start | bytes 1769480 | tf_op jit(solution)/shard_map/ppermute | solution.py:283
  3.9 9.0 %collective-permute-start = (s32[16,768]{1,0:T(8,128)}, s32[16,768]{1,0:T(8,128)S(1)}, u32[]{:S(2)}, u32[]{:S(2)}) collective-permute-start(s32[16,768]{1,0:T(8,128)} %perm_ref.1), channel_id=1, source_target_pairs={{0,9},{1,8},{2,11},{3,10},{4,13},{5,12},{6,15},{7,14},{8,1},{9,0},... | collective-permute-start | bytes 147464 | tf_op jit(solution)/shard_map/ppermute | solution.py:278
  10.2 21.6 %collective-permute-start.2 = (bf16[384,768]{1,0:T(8,128)(2,1)S(1)}, bf16[384,768]{1,0:T(8,128)(2,1)S(1)}, u32[]{:S(2)}, u32[]{:S(2)}) collective-permute-start(bf16[384,768]{1,0:T(8,128)(2,1)S(1)} %standard.1.own_ref), channel_id=1, source_target_pairs={{0,4},{2,6},{4,8},{6,10},{8,12},{10,14},{12,0},{14,2},{1,5},{3,7},... | collective-permute-start | bytes 1769480 | tf_op jit(solution)/shard_map/ppermute | solution.py:280
  10.6 21.2 %collective-permute-start.3 = (bf16[384,768]{1,0:T(8,128)(2,1)S(1)}, bf16[384,768]{1,0:T(8,128)(2,1)S(1)}, u32[]{:S(2)}, u32[]{:S(2)}) collective-permute-start(bf16[384,768]{1,0:T(8,128)(2,1)S(1)} %standard.1.own_ref), channel_id=1, source_target_pairs={{0,12},{2,14},{4,0},{6,2},{8,4},{10,6},{12,8},{14,10},{1,13},{3,15... | collective-permute-start | bytes 1769480 | tf_op jit(solution)/shard_map/ppermute | solution.py:281
  12.9 18.9 %collective-permute-start.4 = (bf16[384,768]{1,0:T(8,128)(2,1)S(1)}, bf16[384,768]{1,0:T(8,128)(2,1)S(1)}, u32[]{:S(2)}, u32[]{:S(2)}) collective-permute-start(bf16[384,768]{1,0:T(8,128)(2,1)S(1)} %standard.1.own_ref), channel_id=1, source_target_pairs={{0,1},{1,0},{2,3},{3,2},{4,5},{5,4},{6,7},{7,6},{8,9},{9,8},{10,11... | collective-permute-start | bytes 1769480 | tf_op jit(solution)/shard_map/ppermute | solution.py:282
  12.9 1.0 %copy-start.1 = (f32[128,768]{1,0:T(8,128)S(1)}, f32[128,768]{1,0:T(8,128)}, u32[]{:S(2)}) copy-start(f32[128,768]{1,0:T(8,128)} %pheno_ref.1) | copy-start | bytes 1179652
  13.9 0.8 %copy-start.2 = (s32[16,768]{1,0:T(8,128)S(1)}, s32[16,768]{1,0:T(8,128)}, u32[]{:S(2)}) copy-start(s32[16,768]{1,0:T(8,128)} %perm_ref.1) | copy-start | bytes 147460
  14.7 0.7 copy-start.3
  31.8 2.6 %collective-permute-start.5 = (bf16[384,768]{1,0:T(8,128)(2,1)S(1)}, bf16[384,768]{1,0:T(8,128)(2,1)S(1)}, u32[]{:S(2)}, u32[]{:S(2)}) collective-permute-start(bf16[384,768]{1,0:T(8,128)(2,1)S(1)} %collective-permute-done.2.refs_0_), channel_id=1, source_target_pairs={{0,2},{2,0},{4,6},{6,4},{8,10},{10,8},{12,14},{14,12},{1,3},{3,1},... | collective-permute-start | bytes 1769480 | tf_op jit(solution)/shard_map/ppermute | solution.py:287
  32.8 2.5 %collective-permute-start.6 = (bf16[384,768]{1,0:T(8,128)(2,1)S(1)}, bf16[384,768]{1,0:T(8,128)(2,1)S(1)}, u32[]{:S(2)}, u32[]{:S(2)}) collective-permute-start(bf16[384,768]{1,0:T(8,128)(2,1)S(1)} %collective-permute-done.3.refs_1_), channel_id=1, source_target_pairs={{0,2},{2,0},{4,6},{6,4},{8,10},{10,8},{12,14},{14,12},{1,3},{3,1},... | collective-permute-start | bytes 1769480 | tf_op jit(solution)/shard_map/ppermute | solution.py:287
  32.9 3.2 %collective-permute-start.7 = (bf16[384,768]{1,0:T(8,128)(2,1)S(1)}, bf16[384,768]{1,0:T(8,128)(2,1)S(1)}, u32[]{:S(2)}, u32[]{:S(2)}) collective-permute-start(bf16[384,768]{1,0:T(8,128)(2,1)S(1)} %collective-permute-done.4.refs_2_), channel_id=1, source_target_pairs={{0,2},{2,0},{4,6},{6,4},{8,10},{10,8},{12,14},{14,12},{1,3},{3,1},... | collective-permute-start | bytes 1769480 | tf_op jit(solution)/shard_map/ppermute | solution.py:287
  45.8 14.9 %collective-permute-start.8 = (f32[16,128]{1,0:T(8,128)S(1)}, f32[16,128]{1,0:T(8,128)S(1)}, u32[]{:S(2)}, u32[]{:S(2)}) collective-permute-start(f32[16,128]{1,0:T(8,128)S(1)} %far.3), channel_id=1, source_target_pairs={{0,9},{1,8},{2,11},{3,10},{4,13},{5,12},{6,15},{7,14},{8,1},{9,0},... | collective-permute-start | bytes 24584 | tf_op jit(solution)/shard_map/ppermute | solution.py:289
  61.4 15.6 %all-to-all-start = ((f32[128,2,128]{2,1,0:T(2,128)}), f32[128,2,128]{2,1,0:T(2,128)S(1)}, u32[]{:S(2)}, u32[]{:S(2)}) async-start(f32[128,2,128]{2,1,0:T(2,128)} %get-tuple-element.20), calls=%async_computation | async-start | bytes 262144 | tf_op jit(solution)/shard_map/all_to_all | solution.py:296

commit v3 on v2

--- a/solution.py
+++ b/solution.py
@@ -144,11 +144,15 @@
     return pltpu.CompilerParams(vmem_limit_bytes=limit * 1024 * 1024)
 
 
+def in_hbm(array):
+    return pltpu.with_memory_space_constraint(array, pltpu.HBM)
+
+
 def near_best(phenotypes, perm_rows, mate_rows, starts, shards):
     genes, samples = phenotypes.shape
     perms = perm_rows.shape[0] + mate_rows.shape[0]
     local = shards[0].shape[0]
-    per_step = 2
+    per_step = 4
     once = pl.Buffered(1)
 
     def whole(shape):
@@ -184,7 +188,7 @@
         cost_estimate=cost(2 * perms * genes * samples * (2 * local + samples)),
         compiler_params=params(24),
         name="near",
-    )(phenotypes, perm_rows, mate_rows, starts.reshape(1, genes), *shards)
+    )(in_hbm(phenotypes), in_hbm(perm_rows), mate_rows, in_hbm(starts.reshape(1, genes)), *shards)
 
 
 def far_kernel(count, per_step, table_ref, lead_ref, before_ref, *refs):
@@ -211,7 +215,7 @@
     perms = before.shape[0] // 2
     local = shards[0].shape[0]
     count = len(shards)
-    per_step = 2
+    per_step = 8
     steps = perms // per_step
     once = pl.Buffered(1)
     whole = pl.BlockSpec((local, samples), lambda i: (0, 0), pipeline_mode=once)
@@ -258,12 +262,37 @@
     )(best, from_mate)
 
 
+def totals_kernel(sent_ref, moments_ref, pooled_ref):
+    count, _, genes = sent_ref.shape
+    blocks = lax.axis_size("gene")
+    members = count // blocks
+    mine = pl.multiple_of(lax.axis_index("gene") * members, members)
+    moments_ref[...] = jnp.sum(sent_ref[pl.ds(mine, members)], axis=0) / PERMS
+    every = jnp.sum(sent_ref[...], axis=0) / PERMS
+    both = jnp.sum(every, axis=1, keepdims=True) / (genes * blocks)
+    lane = lax.broadcasted_iota(jnp.int32, every.shape, 1)
+    row = lax.broadcasted_iota(jnp.int32, every.shape, 0)
+    spread = jnp.sum(jnp.where(lane == row, both, 0.0), axis=0, keepdims=True)
+    pooled_ref[...] = spread[:, :2]
+
+
+def totals(sent):
+    return pl.pallas_call(
+        totals_kernel,
+        out_shape=[
+            jax.ShapeDtypeStruct(sent.shape[1:], jnp.float32),
+            jax.ShapeDtypeStruct((1, 2), jnp.float32),
+        ],
+        compiler_params=params(4),
+        name="totals",
+    )(sent)
+
+
 def shards_program(genotypes, phenotypes, perm_rows, starts):
     var_n = lax.axis_size("var")
     rows_n = var_n // 2
     both = ("var", "perm")
     samples = phenotypes.shape[1]
-    gene_count = phenotypes.shape[0]
 
     def along(step):
         return [(v, ((v // 2 + step) % rows_n) * 2 + v % 2) for v in range(var_n)]
@@ -291,13 +320,9 @@
     count = lax.axis_size(("gene", "var", "perm"))
     maxima, sums = finished(best, from_mate, samples, count)
 
-    everyone = ("gene", "var", "perm")
-    blocks = lax.axis_size("gene")
-    sent = lax.all_to_all(sums, everyone, 0, 0, tiled=True)
-    per_block = jnp.sum(sent.reshape(blocks, count // blocks, *sums.shape[1:]), axis=1) / PERMS
-    moments = lax.dynamic_index_in_dim(per_block, lax.axis_index("gene"), 0, keepdims=False)
-    pooled = jnp.sum(per_block, axis=(0, 2)) / (gene_count * blocks)
-    return (maxima, moments, pooled)
+    sent = lax.all_to_all(sums, ("gene", "var", "perm"), 0, 0, tiled=True)
+    moments, pooled = totals(sent)
+    return (maxima, moments, pooled.reshape(2))
 
 
 def solution(mesh):

time: 78.5 us -> 70 us (0.89)
  blocking collectives: 0 us -> 16.2 us
  waiting for transfers between devices: 12.9 us -> 4.15 us
  starting transfers between devices: 22.7 us -> 15.5 us
  Pallas kernels: 37.1 us -> 32.1 us
  local copies, waits for them, and re-layouts: 4.06 us -> 1.06 us
    all_to_all x0 -> x1, blocking collectives: none -> 16.2 us  [shards_program(): sent = lax.all_to_all(sums, ('gene', 'var', 'perm'), 0, 0, tiled=True)]
    all_to_all x1 -> x0, waiting for transfers between devices: 10.1 us -> none  [shards_program(): sent = lax.all_to_all(sums, everyone, 0, 0, tiled=True)]
    all_to_all x1 -> x0, starting transfers between devices: 5.44 us -> none  [shards_program(): sent = lax.all_to_all(sums, everyone, 0, 0, tiled=True)]
    pallas_call x1, Pallas kernels: 16.4 us -> 13.4 us  [near_best(): pl.pallas_call(functools.partial(near_kernel, per_step), grid=(perms // p...]
    pallas_call x2, Pallas kernels: 19.2 us -> 16.7 us  [far_best(): pl.pallas_call(functools.partial(far_kernel, count, per_step), grid=(step...]
    unnamed x8 -> x2, local copies, waits for them, and re-layouts: 3.5 us -> 1.06 us
    ppermute x1, starting transfers between devices: 2.28 us -> 0.78 us  [shards_program(): above = lax.ppermute(own, 'var', along(-1))]
    ppermute x1, starting transfers between devices: 5.28 us -> 4.25 us  [shards_program(): from_mate = lax.ppermute(to_mate, both, mate)]
  transfers between devices with their start and end apart: 10 -> 9, of which waited for: 4 -> 6; matrix products, arithmetic and copies ran while one was open for 0% -> 0% of each run, Pallas kernels for 33% -> 31%
where the time goes in v3:
time: 70 us; the launch traced here: 69.8 us
  Pallas kernels  32.1 us (46%)
  blocking collectives  16.2 us (23%)
  starting transfers between devices  15.5 us (22%)
  waiting for transfers between devices  4.15 us (6%)
  local copies, waits for them, and re-layouts  1.06 us (2%)
    pallas_call x2, Pallas kernels, far_best(): pl.pallas_call(functools.partial(far_kernel, count, per_step), grid=(step...  16.7 us
    all_to_all x1, blocking collectives, shards_program(): sent = lax.all_to_all(sums, ('gene', 'var', 'perm'), 0, 0, tiled=True)  16.2 us
    pallas_call x1, Pallas kernels, near_best(): pl.pallas_call(functools.partial(near_kernel, per_step), grid=(perms // p...  13.4 us
    ppermute x1, starting transfers between devices, shards_program(): mate_rows = lax.ppermute(perm_rows, both, mate)  6.34 us
    ppermute x1, starting transfers between devices, shards_program(): from_mate = lax.ppermute(to_mate, both, mate)  4.25 us
    ppermute x3, waiting for transfers between devices, shards_program(): far = far + [lax.ppermute(f, 'var', twin) for f in far]  2.81 us
    ppermute x3, starting transfers between devices, shards_program(): far = far + [lax.ppermute(f, 'var', twin) for f in far]  2.02 us
    ppermute x1, starting transfers between devices, shards_program(): own_twin = lax.ppermute(own, 'var', twin)  1.46 us
  transfers between devices with their start and end apart: 9, of which 6 were waited for; matrix products, arithmetic and copies ran while one was open for 0% of the time, Pallas kernels for 31%

profile of v3, /device:TPU:1, one launch (start us, length us, event | category | flops | bytes accessed | tf_op | source)
XLA Modules:
  0.0 69.8 jit_solution(4304028449538854962)
XLA Ops:
  0.6 1.1 %copy-done = bf16[1,384,768]{2,1,0:T(8,128)(2,1)S(1)} copy-done((bf16[1,384,768]{2,1,0:T(8,128)(2,1)S(1)}, bf16[1,384,768]{2,1,0:T(8,128)(2,1)}, u32[]{:S(2)}) %copy-start) | copy-done | bytes 589848
  1.7 0.7 %standard.1.own_ref = bf16[384,768]{1,0:T(8,128)(2,1)S(1)} custom-call(bf16[1,384,768]{2,1,0:T(8,128)(2,1)S(1)} %copy-done), custom_call_target="tpu_custom_call" | custom-call | flops 2359296 | tf_op jit(solution)/shard_map/standard/pallas_call | solution.py:30
  2.4 1.5 %collective-permute-start.1 = (bf16[384,768]{1,0:T(8,128)(2,1)S(1)}, bf16[384,768]{1,0:T(8,128)(2,1)S(1)}, u32[]{:S(2)}, u32[]{:S(2)}) collective-permute-start(bf16[384,768]{1,0:T(8,128)(2,1)S(1)} %standard.1.own_ref), channel_id=1, source_target_pairs={{0,2},{2,0},{4,6},{6,4},{8,10},{10,8},{12,14},{14,12},{1,3},{3,1},... | collective-permute-start | bytes 1769480 | tf_op jit(solution)/shard_map/ppermute | solution.py:312
  3.9 6.3 %collective-permute-start = (s32[16,768]{1,0:T(8,128)}, s32[16,768]{1,0:T(8,128)S(1)}, u32[]{:S(2)}, u32[]{:S(2)}) collective-permute-start(s32[16,768]{1,0:T(8,128)} %perm_ref.1), channel_id=1, source_target_pairs={{0,9},{1,8},{2,11},{3,10},{4,13},{5,12},{6,15},{7,14},{8,1},{9,0},... | collective-permute-start | bytes 147464 | tf_op jit(solution)/shard_map/ppermute | solution.py:307
  10.2 0.8 %collective-permute-start.3 = (bf16[384,768]{1,0:T(8,128)(2,1)S(1)}, bf16[384,768]{1,0:T(8,128)(2,1)S(1)}, u32[]{:S(2)}, u32[]{:S(2)}) collective-permute-start(bf16[384,768]{1,0:T(8,128)(2,1)S(1)} %standard.1.own_ref), channel_id=1, source_target_pairs={{0,12},{2,14},{4,0},{6,2},{8,4},{10,6},{12,8},{14,10},{1,13},{3,15... | collective-permute-start | bytes 1769480 | tf_op jit(solution)/shard_map/ppermute | solution.py:310
  11.0 0.7 collective-permute-start.2
  11.7 0.8 %collective-permute-done.mate_ref = s32[16,768]{1,0:T(8,128)S(1)} collective-permute-done((s32[16,768]{1,0:T(8,128)}, s32[16,768]{1,0:T(8,128)S(1)}, u32[]{:S(2)}, u32[]{:S(2)}) %collective-permute-start) | collective-permute-done | bytes 49184 | tf_op jit(solution)/shard_map/ppermute | solution.py:307
  12.4 0.0 collective-permute-done.1.twin_ref
  12.4 13.4 %near.1 = (bf16[4096,768]{1,0:T(8,128)(2,1)S(1)}, f32[32,128]{1,0:T(8,128)S(1)}, s32[128,128]{1,0:T(8,128)S(1)}) custom-call(f32[128,768]{1,0:T(8,128)} %pheno_ref.1, s32[16,768]{1,0:T(8,128)} %perm_ref.1, s32[16,768]{1,0:T(8,128)S(1)} %collective-permute-done.mate_ref, s32[1,128]{1,0:T(1,128)} %bitcast.2, bf16[384,768]{1,0:T(8,128)(2,1)S(1)} %standard.1.own_ref, ...), custom_call_target="tpu_custom_call" | custom-call | flops 9663676416 | tf_op jit(solution)/shard_map/near/pallas_call | solution.py:161
  25.9 0.4 collective-permute-done.4.refs_2_
  26.2 0.0 collective-permute-done.3.refs_1_
  26.2 0.2 collective-permute-done.2.refs_0_
  26.4 1.5 %collective-permute-start.5 = (bf16[384,768]{1,0:T(8,128)(2,1)S(1)}, bf16[384,768]{1,0:T(8,128)(2,1)S(1)}, u32[]{:S(2)}, u32[]{:S(2)}) collective-permute-start(bf16[384,768]{1,0:T(8,128)(2,1)S(1)} %collective-permute-done.2.refs_0_), channel_id=1, source_target_pairs={{0,2},{2,0},{4,6},{6,4},{8,10},{10,8},{12,14},{14,12},{1,3},{3,1},... | collective-permute-start | bytes 1769480 | tf_op jit(solution)/shard_map/ppermute | solution.py:316
  27.9 0.0 collective-permute-start.6
  27.9 0.5 collective-permute-start.7
  28.5 1.1 %collective-permute-done.5.refs_3_ = bf16[384,768]{1,0:T(8,128)(2,1)S(1)} collective-permute-done((bf16[384,768]{1,0:T(8,128)(2,1)S(1)}, bf16[384,768]{1,0:T(8,128)(2,1)S(1)}, u32[]{:S(2)}, u32[]{:S(2)}) %collective-permute-start.5) | collective-permute-done | bytes 589856 | tf_op jit(solution)/shard_map/ppermute | solution.py:316
  29.6 0.8 %collective-permute-done.6.refs_4_ = bf16[384,768]{1,0:T(8,128)(2,1)S(1)} collective-permute-done((bf16[384,768]{1,0:T(8,128)(2,1)S(1)}, bf16[384,768]{1,0:T(8,128)(2,1)S(1)}, u32[]{:S(2)}, u32[]{:S(2)}) %collective-permute-start.6) | collective-permute-done | bytes 589856 | tf_op jit(solution)/shard_map/ppermute | solution.py:316
  30.4 0.8 %collective-permute-done.7.refs_5_ = bf16[384,768]{1,0:T(8,128)(2,1)S(1)} collective-permute-done((bf16[384,768]{1,0:T(8,128)(2,1)S(1)}, bf16[384,768]{1,0:T(8,128)(2,1)S(1)}, u32[]{:S(2)}, u32[]{:S(2)}) %collective-permute-start.7) | collective-permute-done | bytes 589856 | tf_op jit(solution)/shard_map/ppermute | solution.py:316
  31.3 8.3 %far.3 = f32[16,128]{1,0:T(8,128)S(1)} custom-call(bf16[4096,768]{1,0:T(8,128)(2,1)S(1)} %get-tuple-element.14.table_ref, s32[128,128]{1,0:T(8,128)S(1)} %get-tuple-element.16.lead_ref, f32[32,128]{1,0:T(8,128)S(1)} %get-tuple-element.17.before_ref, bf16[384,768]{1,0:T(8,128)(2,1)S(1)} %collective-permute-done.2.refs_0_, ...), custom_call_target="tpu_custom_call" | custom-call | flops 7247757312 | tf_op jit(solution)/shard_map/far/pallas_call | solution.py:222
  39.6 4.2 %collective-permute-start.8 = (f32[16,128]{1,0:T(8,128)S(1)}, f32[16,128]{1,0:T(8,128)S(1)}, u32[]{:S(2)}, u32[]{:S(2)}) collective-permute-start(f32[16,128]{1,0:T(8,128)S(1)} %far.3), channel_id=1, source_target_pairs={{0,9},{1,8},{2,11},{3,10},{4,13},{5,12},{6,15},{7,14},{8,1},{9,0},... | collective-permute-start | bytes 24584 | tf_op jit(solution)/shard_map/ppermute | solution.py:318
  43.9 8.3 %far.2.best_ref = f32[16,128]{1,0:T(8,128)S(1)} custom-call(bf16[4096,768]{1,0:T(8,128)(2,1)S(1)} %get-tuple-element.14.table_ref, s32[128,128]{1,0:T(8,128)S(1)} %get-tuple-element.16.lead_ref, f32[32,128]{1,0:T(8,128)S(1)} %get-tuple-element.17.before_ref, bf16[384,768]{1,0:T(8,128)(2,1)S(1)} %collective-permute-done.2.refs_0_, ...), custom_call_target="tpu_custom_call" | custom-call | flops 7247757312 | tf_op jit(solution)/shard_map/far/pallas_call | solution.py:222
  52.2 0.6 finish.1
  52.8 16.2 %all_to_all.5.sent_ref = f32[128,2,128]{2,1,0:T(2,128)S(1)} all-to-all(f32[128,2,128]{2,1,0:T(2,128)S(1)} %get-tuple-element.22), channel_id=1, replica_groups=mesh['gene'=8,'var'=8,'perm'=2] {'gene','var','perm'}, dimensions={0} | all-to-all | bytes 262144 | tf_op jit(solution)/shard_map/all_to_all | solution.py:323
  69.0 0.7 %totals.1 = (f32[2,128]{1,0:T(2,128)}, f32[1,2]{1,0:T(1,128)}) custom-call(f32[128,2,128]{2,1,0:T(2,128)S(1)} %all_to_all.5.sent_ref), custom_call_target="tpu_custom_call" | custom-call | tf_op jit(solution)/shard_map/totals/pallas_call | solution.py:280
  (3 shorter events, 0.0 us)
Async XLA Ops:
  0.6 1.1 %copy-start = (bf16[1,384,768]{2,1,0:T(8,128)(2,1)S(1)}, bf16[1,384,768]{2,1,0:T(8,128)(2,1)}, u32[]{:S(2)}) copy-start(bf16[1,384,768]{2,1,0:T(8,128)(2,1)} %x_ref.1) | copy-start | bytes 1769476
  2.4 10.0 %collective-permute-start.1 = (bf16[384,768]{1,0:T(8,128)(2,1)S(1)}, bf16[384,768]{1,0:T(8,128)(2,1)S(1)}, u32[]{:S(2)}, u32[]{:S(2)}) collective-permute-start(bf16[384,768]{1,0:T(8,128)(2,1)S(1)} %standard.1.own_ref), channel_id=1, source_target_pairs={{0,2},{2,0},{4,6},{6,4},{8,10},{10,8},{12,14},{14,12},{1,3},{3,1},... | collective-permute-start | bytes 1769480 | tf_op jit(solution)/shard_map/ppermute | solution.py:312
  3.9 8.6 %collective-permute-start = (s32[16,768]{1,0:T(8,128)}, s32[16,768]{1,0:T(8,128)S(1)}, u32[]{:S(2)}, u32[]{:S(2)}) collective-permute-start(s32[16,768]{1,0:T(8,128)} %perm_ref.1), channel_id=1, source_target_pairs={{0,9},{1,8},{2,11},{3,10},{4,13},{5,12},{6,15},{7,14},{8,1},{9,0},... | collective-permute-start | bytes 147464 | tf_op jit(solution)/shard_map/ppermute | solution.py:307
  10.2 16.0 %collective-permute-start.4 = (bf16[384,768]{1,0:T(8,128)(2,1)S(1)}, bf16[384,768]{1,0:T(8,128)(2,1)S(1)}, u32[]{:S(2)}, u32[]{:S(2)}) collective-permute-start(bf16[384,768]{1,0:T(8,128)(2,1)S(1)} %standard.1.own_ref), channel_id=1, source_target_pairs={{0,1},{1,0},{2,3},{3,2},{4,5},{5,4},{6,7},{7,6},{8,9},{9,8},{10,11... | collective-permute-start | bytes 1769480 | tf_op jit(solution)/shard_map/ppermute | solution.py:311
  10.2 16.0 %collective-permute-start.3 = (bf16[384,768]{1,0:T(8,128)(2,1)S(1)}, bf16[384,768]{1,0:T(8,128)(2,1)S(1)}, u32[]{:S(2)}, u32[]{:S(2)}) collective-permute-start(bf16[384,768]{1,0:T(8,128)(2,1)S(1)} %standard.1.own_ref), channel_id=1, source_target_pairs={{0,12},{2,14},{4,0},{6,2},{8,4},{10,6},{12,8},{14,10},{1,13},{3,15... | collective-permute-start | bytes 1769480 | tf_op jit(solution)/shard_map/ppermute | solution.py:310
  11.0 15.4 %collective-permute-start.2 = (bf16[384,768]{1,0:T(8,128)(2,1)S(1)}, bf16[384,768]{1,0:T(8,128)(2,1)S(1)}, u32[]{:S(2)}, u32[]{:S(2)}) collective-permute-start(bf16[384,768]{1,0:T(8,128)(2,1)S(1)} %standard.1.own_ref), channel_id=1, source_target_pairs={{0,4},{2,6},{4,8},{6,10},{8,12},{10,14},{12,0},{14,2},{1,5},{3,7},... | collective-permute-start | bytes 1769480 | tf_op jit(solution)/shard_map/ppermute | solution.py:309
  26.4 3.1 %collective-permute-start.5 = (bf16[384,768]{1,0:T(8,128)(2,1)S(1)}, bf16[384,768]{1,0:T(8,128)(2,1)S(1)}, u32[]{:S(2)}, u32[]{:S(2)}) collective-permute-start(bf16[384,768]{1,0:T(8,128)(2,1)S(1)} %collective-permute-done.2.refs_0_), channel_id=1, source_target_pairs={{0,2},{2,0},{4,6},{6,4},{8,10},{10,8},{12,14},{14,12},{1,3},{3,1},... | collective-permute-start | bytes 1769480 | tf_op jit(solution)/shard_map/ppermute | solution.py:316
  27.9 2.5 %collective-permute-start.6 = (bf16[384,768]{1,0:T(8,128)(2,1)S(1)}, bf16[384,768]{1,0:T(8,128)(2,1)S(1)}, u32[]{:S(2)}, u32[]{:S(2)}) collective-permute-start(bf16[384,768]{1,0:T(8,128)(2,1)S(1)} %collective-permute-done.3.refs_1_), channel_id=1, source_target_pairs={{0,2},{2,0},{4,6},{6,4},{8,10},{10,8},{12,14},{14,12},{1,3},{3,1},... | collective-permute-start | bytes 1769480 | tf_op jit(solution)/shard_map/ppermute | solution.py:316
  27.9 3.3 %collective-permute-start.7 = (bf16[384,768]{1,0:T(8,128)(2,1)S(1)}, bf16[384,768]{1,0:T(8,128)(2,1)S(1)}, u32[]{:S(2)}, u32[]{:S(2)}) collective-permute-start(bf16[384,768]{1,0:T(8,128)(2,1)S(1)} %collective-permute-done.4.refs_2_), channel_id=1, source_target_pairs={{0,2},{2,0},{4,6},{6,4},{8,10},{10,8},{12,14},{14,12},{1,3},{3,1},... | collective-permute-start | bytes 1769480 | tf_op jit(solution)/shard_map/ppermute | solution.py:316
  39.6 12.6 %collective-permute-start.8 = (f32[16,128]{1,0:T(8,128)S(1)}, f32[16,128]{1,0:T(8,128)S(1)}, u32[]{:S(2)}, u32[]{:S(2)}) collective-permute-start(f32[16,128]{1,0:T(8,128)S(1)} %far.3), channel_id=1, source_target_pairs={{0,9},{1,8},{2,11},{3,10},{4,13},{5,12},{6,15},{7,14},{8,1},{9,0},... | collective-permute-start | bytes 24584 | tf_op jit(solution)/shard_map/ppermute | solution.py:318

commit v4 on v3

--- a/solution.py
+++ b/solution.py
@@ -58,15 +58,14 @@
     return near, far
 
 
-def fill_masks(firsts, lead, mask_ref, local):
+def window_mask(first, lead, width):
     half = TILE // 2
     lane = lax.broadcasted_iota(jnp.int32, lead.shape, 1)
-    for i in range(len(firsts)):
-        for r in range(0, local, half):
-            past = lane + (firsts[i] + r) - lead
-            inside = (past >= 0) & (past < WINDOW)
-            at = i * local + r
-            mask_ref[:, at:at + half] = jnp.where(inside, LARGE, 0.0)
+    masks = []
+    for r in range(0, width, half):
+        past = lane + (first + r) - lead
+        masks.append(jnp.where((past >= 0) & (past < WINDOW), LARGE, 0.0))
+    return jnp.concatenate(masks, axis=1)
 
 
 def weight_tiles(shards, local):
@@ -77,37 +76,52 @@
         yield t * half, jnp.concatenate([shards[i][r:r + half, :] for i, r in pair], axis=0)
 
 
-def lane_best(rows_bf16, shards, local, mask_ref, copies):
+def lane_best(rows_bf16, shards, local, masks, copies):
     half = TILE // 2
-    genes = mask_ref.shape[0]
     best = None
     for at, weights in weight_tiles(shards, local):
         scores = lax.dot_general(
             rows_bf16, weights, (((1,), (1,)), ((), ())), preferred_element_type=jnp.float32
         )
         for n in range(weights.shape[0] // half):
-            part = jnp.abs(scores[:, n * half:(n + 1) * half]).reshape(copies, genes, half)
-            part = jnp.minimum(part, mask_ref[:, at + n * half:at + (n + 1) * half][None])
+            i, r = divmod(at + n * half, local)
+            mask_ref, k = masks[i]
+            mask = mask_ref[k, :, r:r + half]
+            part = jnp.abs(scores[:, n * half:(n + 1) * half]).reshape(copies, mask.shape[0], half)
+            part = jnp.minimum(part, mask[None])
             best = part if best is None else jnp.maximum(best, part)
     return best
 
 
-def reduce_lanes(best_ref, out_ref):
-    perms, genes, half = best_ref.shape
+def reduce_lanes(best_ref, slot, out_ref, row):
+    _, perms, genes, half = best_ref.shape
     lane = lax.broadcasted_iota(jnp.int32, (genes, half), 1)
     gene = lax.broadcasted_iota(jnp.int32, (genes, half), 0)
     for p in range(perms):
-        top = jnp.max(best_ref[p], axis=1, keepdims=True)
-        out_ref[p:p + 1, :] = jnp.max(jnp.where(lane == gene, top, 0.0), axis=0, keepdims=True)
+        top = jnp.max(best_ref[slot, p], axis=1, keepdims=True)
+        best = jnp.max(jnp.where(lane == gene, top, 0.0), axis=0, keepdims=True)
+        out_ref[pl.ds(row + p, 1), :] = best
+
+
+def score_step(rows_bf16, shards, local, masks, per_step, best_ref, out_ref):
+    step = pl.program_id(0)
+    slot = lax.rem(step, 2)
+    reduce_lanes(best_ref, 1 - slot, out_ref, jnp.maximum(step - 1, 0) * per_step)
+    best_ref[slot] = lane_best(rows_bf16, shards, local, masks, per_step)
+
+    @pl.when(step == pl.num_programs(0) - 1)
+    def _():
+        reduce_lanes(best_ref, slot, out_ref, step * per_step)
 
 
 def near_kernel(per_step, pheno_ref, perm_ref, mate_ref, starts_ref, own_ref, twin_ref,
-                table_ref, out_ref, lead_ref, base_ref, rows_ref, mask_ref, best_ref):
+                table_ref, out_ref, far_mask_ref, base_ref, rows_ref, lead_ref, mask_ref, best_ref):
     genes, samples = pheno_ref.shape
     folds = samples // FOLD
     local = own_ref.shape[0]
     half_perms = perm_ref.shape[0]
     step = pl.program_id(0)
+    near_first, far_first = places(local)
 
     @pl.when(step == 0)
     def _():
@@ -119,7 +133,14 @@
         wide = jnp.broadcast_to(starts_ref[...].astype(jnp.float32), lead_ref.shape)
         lead = wide.T.astype(jnp.int32)
         lead_ref[...] = lead
-        fill_masks(places(local)[0], lead, mask_ref, local)
+        for i in range(2):
+            mask_ref[i] = window_mask(near_first[i], lead, local)
+
+    shard = jnp.minimum(step, len(far_first) - 1)
+    first = far_first[0]
+    for i in range(1, len(far_first)):
+        first = jnp.where(shard == i, far_first[i], first)
+    far_mask_ref[shard] = window_mask(first, lead_ref[...], local)
 
     within = lax.broadcasted_iota(jnp.int32, (FOLD, samples), 0)
     for k in range(per_step):
@@ -132,12 +153,8 @@
         for b in range(1, folds):
             chosen = jnp.where(block == b, picked[b * genes:(b + 1) * genes], chosen)
         table_ref[k * genes:(k + 1) * genes, :] = chosen.astype(jnp.bfloat16)
-    best = lane_best(table_ref[...], (own_ref, twin_ref), local, mask_ref, per_step)
-    best_ref[pl.ds(step * per_step, per_step)] = best
-
-    @pl.when(step == pl.num_programs(0) - 1)
-    def _():
-        reduce_lanes(best_ref, out_ref)
+    masks = [(mask_ref, 0), (mask_ref, 1)]
+    score_step(table_ref[...], (own_ref, twin_ref), local, masks, per_step, best_ref, out_ref)
 
 
 def params(limit):
@@ -172,18 +189,19 @@
         out_specs=[
             pl.BlockSpec((per_step * genes, samples), lambda i: (i, 0)),
             pl.BlockSpec((perms, genes), lambda i: (0, 0)),
-            pl.BlockSpec((genes, TILE // 2), lambda i: (0, 0)),
+            pl.BlockSpec((6, genes, local), lambda i: (0, 0, 0)),
         ],
         out_shape=[
             jax.ShapeDtypeStruct((perms * genes, samples), jnp.bfloat16),
             jax.ShapeDtypeStruct((perms, genes), jnp.float32),
-            jax.ShapeDtypeStruct((genes, TILE // 2), jnp.int32),
+            jax.ShapeDtypeStruct((6, genes, local), jnp.float32),
         ],
         scratch_shapes=[
             pltpu.VMEM((samples // FOLD * genes, FOLD), jnp.bfloat16),
             pltpu.VMEM((perms, samples), jnp.int32),
-            pltpu.VMEM((genes, 2 * local), jnp.float32),
-            pltpu.VMEM((perms, genes, TILE // 2), jnp.float32),
+            pltpu.VMEM((genes, TILE // 2), jnp.int32),
+            pltpu.VMEM((2, genes, local), jnp.float32),
+            pltpu.VMEM((2, per_step, genes, TILE // 2), jnp.float32),
         ],
         cost_estimate=cost(2 * perms * genes * samples * (2 * local + samples)),
         compiler_params=params(24),
@@ -191,53 +209,43 @@
     )(in_hbm(phenotypes), in_hbm(perm_rows), mate_rows, in_hbm(starts.reshape(1, genes)), *shards)
 
 
-def far_kernel(count, per_step, table_ref, lead_ref, before_ref, *refs):
-    shards, (out_ref, mask_ref, best_ref) = refs[:count], refs[count:]
+def far_kernel(pairs, per_step, table_ref, before_ref, *refs):
+    count = 2 * pairs
+    shards, mask_refs, (out_ref, best_ref) = refs[:count], refs[count:count + pairs], refs[count + pairs:]
     local = shards[0].shape[0]
-    step = pl.program_id(0)
-
-    @pl.when(step == 0)
+    masks = [(m, k) for m in mask_refs for k in range(2)]
+    score_step(table_ref[...], shards, local, masks, per_step, best_ref, out_ref)
+
+    @pl.when(pl.program_id(0) == pl.num_programs(0) - 1)
     def _():
-        fill_masks(places(local)[1], lead_ref[...], mask_ref, local)
-
-    best = lane_best(table_ref[...], shards, local, mask_ref, per_step)
-    best_ref[pl.ds(step * per_step, per_step)] = best
-
-    @pl.when(step == pl.num_programs(0) - 1)
-    def _():
-        reduce_lanes(best_ref, out_ref)
         out_ref[...] = jnp.maximum(out_ref[...], before_ref[...])
 
 
-def far_best(table, part, lead, before, shards):
+def far_best(table, part, before, before_part, masks, pairs, shards):
     samples = table.shape[1]
-    genes = lead.shape[0]
-    perms = before.shape[0] // 2
-    local = shards[0].shape[0]
+    _, genes, local = masks.shape
+    perms = table.shape[0] // genes // 2
     count = len(shards)
     per_step = 8
     steps = perms // per_step
     once = pl.Buffered(1)
     whole = pl.BlockSpec((local, samples), lambda i: (0, 0), pipeline_mode=once)
     return pl.pallas_call(
-        functools.partial(far_kernel, count, per_step),
+        functools.partial(far_kernel, len(pairs), per_step),
         grid=(steps,),
         in_specs=[
             pl.BlockSpec((per_step * genes, samples), lambda i: (i + part * steps, 0)),
-            pl.BlockSpec(lead.shape, lambda i: (0, 0), pipeline_mode=once),
-            pl.BlockSpec((perms, genes), lambda i: (part, 0), pipeline_mode=once),
+            pl.BlockSpec((perms, genes), lambda i: (before_part, 0), pipeline_mode=once),
             *[whole] * count,
+            *[pl.BlockSpec((2, genes, local), lambda i, k=k: (k, 0, 0), pipeline_mode=once) for k in pairs],
         ],
         out_specs=pl.BlockSpec((perms, genes), lambda i: (0, 0)),
         out_shape=jax.ShapeDtypeStruct((perms, genes), jnp.float32),
-        scratch_shapes=[
-            pltpu.VMEM((genes, count * local), jnp.float32),
-            pltpu.VMEM((perms, genes, TILE // 2), jnp.float32),
-        ],
+        scratch_shapes=[pltpu.VMEM((2, per_step, genes, TILE // 2), jnp.float32)],
         cost_estimate=cost(2 * perms * genes * samples * count * local),
         compiler_params=params(24),
         name="far",
-    )(table, lead, before, *shards)
+    )(table, before, *shards, *[masks] * len(pairs))
 
 
 def finish_kernel(spread, best_ref, mate_ref, maxima_ref, sums_ref, *, samples):
@@ -310,13 +318,14 @@
     above = lax.ppermute(own, "var", along(-1))
     deep = lax.ppermute(own, "perm", across)
     own_twin = lax.ppermute(own, "var", twin)
-    table, near, lead = near_best(phenotypes, perm_rows, mate_rows, starts, (own, own_twin))
-    below, above, deep, lead = lax.optimization_barrier((below, above, deep, lead))
+    table, near, masks = near_best(phenotypes, perm_rows, mate_rows, starts, (own, own_twin))
+    below, above, deep, masks = lax.optimization_barrier((below, above, deep, masks))
     far = [below, above, deep]
     far = far + [lax.ppermute(f, "var", twin) for f in far]
-    to_mate = far_best(table, 1, lead, near, far)
+    to_mate = far_best(table, 1, near, 1, masks, (0,), far[:2])
+    to_mate = far_best(table, 1, to_mate, 0, masks, (1, 2), far[2:])
     from_mate = lax.ppermute(to_mate, both, mate)
-    best = far_best(table, 0, lead, near, far)
+    best = far_best(table, 0, near, 0, masks, (0, 1, 2), far)
     count = lax.axis_size(("gene", "var", "perm"))
     maxima, sums = finished(best, from_mate, samples, count)
 

time: 70 us -> 69.6 us (level)
  waiting for transfers between devices: 4.15 us -> 2.22 us
  Pallas kernels: 32.1 us -> 33.1 us
  blocking collectives: 16.2 us -> 17.2 us
    ppermute x3, waiting for transfers between devices: 2.81 us -> 0.01 us  [shards_program(): far = far + [lax.ppermute(f, 'var', twin) for f in far]]
    ppermute x1, starting transfers between devices: 4.25 us -> 2.3 us  [shards_program(): from_mate = lax.ppermute(to_mate, both, mate)]
    ppermute x1, waiting for transfers between devices: 0.38 us -> 2.2 us  [shards_program(): deep = lax.ppermute(own, 'perm', across)]
    ppermute x1, starting transfers between devices: 0.78 us -> 2.28 us  [shards_program(): above = lax.ppermute(own, 'var', along(-1))]
    pallas_call x2 -> x3, Pallas kernels: 16.7 us -> 17.8 us  [far_best(): pl.pallas_call(functools.partial(far_kernel, len(pairs), per_step), grid=...]
    all_to_all x1, blocking collectives: 16.2 us -> 17.2 us  [shards_program(): sent = lax.all_to_all(sums, ('gene', 'var', 'perm'), 0, 0, tiled=True)]
    ppermute x1, waiting for transfers between devices: 0.76 us -> 0.01 us  [shards_program(): mate_rows = lax.ppermute(perm_rows, both, mate)]
  transfers between devices with their start and end apart: 9 -> 9, of which waited for: 6 -> 1; matrix products, arithmetic and copies ran while one was open for 0% -> 0% of each run, Pallas kernels for 31% -> 36%
where the time goes in v4:
time: 69.6 us; the launch traced here: 69.4 us
  Pallas kernels  33.1 us (48%)
  blocking collectives  17.2 us (25%)
  starting transfers between devices  15.1 us (22%)
  waiting for transfers between devices  2.22 us (3%)
  local copies, waits for them, and re-layouts  1.06 us (2%)
  between operations  0.73 us (1%)
    pallas_call x3, Pallas kernels, far_best(): pl.pallas_call(functools.partial(far_kernel, len(pairs), per_step), grid=...  17.8 us
    all_to_all x1, blocking collectives, shards_program(): sent = lax.all_to_all(sums, ('gene', 'var', 'perm'), 0, 0, tiled=True)  17.2 us
    pallas_call x1, Pallas kernels, near_best(): pl.pallas_call(functools.partial(near_kernel, per_step), grid=(perms // p...  13.2 us
    ppermute x1, starting transfers between devices, shards_program(): mate_rows = lax.ppermute(perm_rows, both, mate)  6.34 us
    ppermute x1, starting transfers between devices, shards_program(): from_mate = lax.ppermute(to_mate, both, mate)  2.3 us
    ppermute x3, starting transfers between devices, shards_program(): far = far + [lax.ppermute(f, 'var', twin) for f in far]  2.3 us
    ppermute x1, starting transfers between devices, shards_program(): above = lax.ppermute(own, 'var', along(-1))  2.28 us
    ppermute x1, waiting for transfers between devices, shards_program(): deep = lax.ppermute(own, 'perm', across)  2.2 us
  transfers between devices with their start and end apart: 9, of which 1 were waited for; matrix products, arithmetic and copies ran while one was open for 0% of the time, Pallas kernels for 36%

profile of v4, /device:TPU:1, one launch (start us, length us, event | category | flops | bytes accessed | tf_op | source)
XLA Modules:
  0.0 69.4 jit_solution(4628591938893574154)
XLA Ops:
  0.6 1.1 %copy-done = bf16[1,384,768]{2,1,0:T(8,128)(2,1)S(1)} copy-done((bf16[1,384,768]{2,1,0:T(8,128)(2,1)S(1)}, bf16[1,384,768]{2,1,0:T(8,128)(2,1)}, u32[]{:S(2)}) %copy-start) | copy-done | bytes 589848
  1.7 0.7 %standard.1.own_ref = bf16[384,768]{1,0:T(8,128)(2,1)S(1)} custom-call(bf16[1,384,768]{2,1,0:T(8,128)(2,1)S(1)} %copy-done), custom_call_target="tpu_custom_call" | custom-call | flops 2359296 | tf_op jit(solution)/shard_map/standard/pallas_call | solution.py:30
  2.4 1.5 %collective-permute-start.1 = (bf16[384,768]{1,0:T(8,128)(2,1)S(1)}, bf16[384,768]{1,0:T(8,128)(2,1)S(1)}, u32[]{:S(2)}, u32[]{:S(2)}) collective-permute-start(bf16[384,768]{1,0:T(8,128)(2,1)S(1)} %standard.1.own_ref), channel_id=1, source_target_pairs={{0,2},{2,0},{4,6},{6,4},{8,10},{10,8},{12,14},{14,12},{1,3},{3,1},... | collective-permute-start | bytes 1769480 | tf_op jit(solution)/shard_map/ppermute | solution.py:320
  3.9 6.3 %collective-permute-start = (s32[16,768]{1,0:T(8,128)}, s32[16,768]{1,0:T(8,128)S(1)}, u32[]{:S(2)}, u32[]{:S(2)}) collective-permute-start(s32[16,768]{1,0:T(8,128)} %perm_ref.1), channel_id=1, source_target_pairs={{0,9},{1,8},{2,11},{3,10},{4,13},{5,12},{6,15},{7,14},{8,1},{9,0},... | collective-permute-start | bytes 147464 | tf_op jit(solution)/shard_map/ppermute | solution.py:315
  10.2 0.4 collective-permute-start.2
  10.6 2.3 %collective-permute-start.3 = (bf16[384,768]{1,0:T(8,128)(2,1)S(1)}, bf16[384,768]{1,0:T(8,128)(2,1)S(1)}, u32[]{:S(2)}, u32[]{:S(2)}) collective-permute-start(bf16[384,768]{1,0:T(8,128)(2,1)S(1)} %standard.1.own_ref), channel_id=1, source_target_pairs={{0,12},{2,14},{4,0},{6,2},{8,4},{10,6},{12,8},{14,10},{1,13},{3,15... | collective-permute-start | bytes 1769480 | tf_op jit(solution)/shard_map/ppermute | solution.py:318
  12.9 0.0 collective-permute-start.4
  12.9 0.0 collective-permute-done.mate_ref
  12.9 13.2 %near.1 = (bf16[4096,768]{1,0:T(8,128)(2,1)S(1)}, f32[32,128]{1,0:T(8,128)S(1)}, f32[6,128,384]{2,1,0:T(8,128)S(1)}) custom-call(f32[128,768]{1,0:T(8,128)} %pheno_ref.1, s32[16,768]{1,0:T(8,128)} %perm_ref.1, s32[16,768]{1,0:T(8,128)S(1)} %collective-permute-done.mate_ref, s32[1,128]{1,0:T(1,128)} %bitcast.2, bf16[384,768]{1,0:T(8,128)(2,1)S(1)} %standard.1.own_ref, ...), custom_call_target="tpu_custom_call" | custom-call | flops 9663676416 | tf_op jit(solution)/shard_map/near/pallas_call | solution.py:178
  26.1 0.0 collective-permute-done.3.refs_1_
  26.2 2.2 %collective-permute-done.4.refs_2_.refs_0_ = bf16[384,768]{1,0:T(8,128)(2,1)S(1)} collective-permute-done((bf16[384,768]{1,0:T(8,128)(2,1)S(1)}, bf16[384,768]{1,0:T(8,128)(2,1)S(1)}, u32[]{:S(2)}, u32[]{:S(2)}) %collective-permute-start.4) | collective-permute-done | bytes 589856 | tf_op jit(solution)/shard_map/ppermute | solution.py:319
  28.3 1.8 %collective-permute-start.5 = (bf16[384,768]{1,0:T(8,128)(2,1)S(1)}, bf16[384,768]{1,0:T(8,128)(2,1)S(1)}, u32[]{:S(2)}, u32[]{:S(2)}) collective-permute-start(bf16[384,768]{1,0:T(8,128)(2,1)S(1)} %collective-permute-done.2.refs_0_), channel_id=1, source_target_pairs={{0,2},{2,0},{4,6},{6,4},{8,10},{10,8},{12,14},{14,12},{1,3},{3,1},... | collective-permute-start | bytes 1769480 | tf_op jit(solution)/shard_map/ppermute | solution.py:324
  30.1 0.0 collective-permute-start.6
  30.1 0.5 collective-permute-start.7
  30.6 3.3 %far.4.before_ref = f32[16,128]{1,0:T(8,128)S(1)} custom-call(bf16[4096,768]{1,0:T(8,128)(2,1)S(1)} %get-tuple-element.14.table_ref, f32[32,128]{1,0:T(8,128)S(1)} %get-tuple-element.15.before_ref, bf16[384,768]{1,0:T(8,128)(2,1)S(1)} %collective-permute-done.2.refs_0_, bf16[384,768]{1,0:T(8,128)(2,1)S(1)} %collective-permute-done.3.refs_1_, ...), custom_call_target="tpu_custom_call" | custom-call | flops 2415919104 | tf_op jit(solution)/shard_map/far/pallas_call | solution.py:233
  34.0 0.0 collective-permute-done.5.refs_3_.refs_1_
  34.0 0.0 collective-permute-done.6.refs_4_.refs_2_
  34.0 5.9 %far.5 = f32[16,128]{1,0:T(8,128)S(1)} custom-call(bf16[4096,768]{1,0:T(8,128)(2,1)S(1)} %get-tuple-element.14.table_ref, f32[16,128]{1,0:T(8,128)S(1)} %far.4.before_ref, bf16[384,768]{1,0:T(8,128)(2,1)S(1)} %collective-permute-done.4.refs_2_.refs_0_, bf16[384,768]{1,0:T(8,128)(2,1)S(1)} %collective-permute-done.5.refs_3_.refs_1_, ...), custom_call_target="tpu_custom_call" | custom-call | flops 4831838208 | tf_op jit(solution)/shard_map/far/pallas_call | solution.py:233
  40.0 2.3 %collective-permute-start.8 = (f32[16,128]{1,0:T(8,128)S(1)}, f32[16,128]{1,0:T(8,128)S(1)}, u32[]{:S(2)}, u32[]{:S(2)}) collective-permute-start(f32[16,128]{1,0:T(8,128)S(1)} %far.5), channel_id=1, source_target_pairs={{0,9},{1,8},{2,11},{3,10},{4,13},{5,12},{6,15},{7,14},{8,1},{9,0},... | collective-permute-start | bytes 24584 | tf_op jit(solution)/shard_map/ppermute | solution.py:327
  42.3 8.5 %far.3.best_ref = f32[16,128]{1,0:T(8,128)S(1)} custom-call(bf16[4096,768]{1,0:T(8,128)(2,1)S(1)} %get-tuple-element.14.table_ref, f32[32,128]{1,0:T(8,128)S(1)} %get-tuple-element.15.before_ref, bf16[384,768]{1,0:T(8,128)(2,1)S(1)} %collective-permute-done.2.refs_0_, bf16[384,768]{1,0:T(8,128)(2,1)S(1)} %collective-permute-done.3.refs_1_, ...), custom_call_target="tpu_custom_call" | custom-call | flops 7247757312 | tf_op jit(solution)/shard_map/far/pallas_call | solution.py:233
  50.8 0.0 collective-permute-done.8.mate_ref
  50.8 0.6 finish.1
  51.4 17.2 %all_to_all.5.sent_ref = f32[128,2,128]{2,1,0:T(2,128)S(1)} all-to-all(f32[128,2,128]{2,1,0:T(2,128)S(1)} %get-tuple-element.22), channel_id=1, replica_groups=mesh['gene'=8,'var'=8,'perm'=2] {'gene','var','perm'}, dimensions={0} | all-to-all | bytes 262144 | tf_op jit(solution)/shard_map/all_to_all | solution.py:332
  68.7 0.7 %totals.1 = (f32[2,128]{1,0:T(2,128)}, f32[1,2]{1,0:T(1,128)}) custom-call(f32[128,2,128]{2,1,0:T(2,128)S(1)} %all_to_all.5.sent_ref), custom_call_target="tpu_custom_call" | custom-call | tf_op jit(solution)/shard_map/totals/pallas_call | solution.py:288
  (4 shorter events, 0.0 us)
Async XLA Ops:
  0.6 1.1 %copy-start = (bf16[1,384,768]{2,1,0:T(8,128)(2,1)S(1)}, bf16[1,384,768]{2,1,0:T(8,128)(2,1)}, u32[]{:S(2)}) copy-start(bf16[1,384,768]{2,1,0:T(8,128)(2,1)} %x_ref.1) | copy-start | bytes 1769476
  2.4 10.5 %collective-permute-start.1 = (bf16[384,768]{1,0:T(8,128)(2,1)S(1)}, bf16[384,768]{1,0:T(8,128)(2,1)S(1)}, u32[]{:S(2)}, u32[]{:S(2)}) collective-permute-start(bf16[384,768]{1,0:T(8,128)(2,1)S(1)} %standard.1.own_ref), channel_id=1, source_target_pairs={{0,2},{2,0},{4,6},{6,4},{8,10},{10,8},{12,14},{14,12},{1,3},{3,1},... | collective-permute-start | bytes 1769480 | tf_op jit(solution)/shard_map/ppermute | solution.py:320
  3.9 9.0 %collective-permute-start = (s32[16,768]{1,0:T(8,128)}, s32[16,768]{1,0:T(8,128)S(1)}, u32[]{:S(2)}, u32[]{:S(2)}) collective-permute-start(s32[16,768]{1,0:T(8,128)} %perm_ref.1), channel_id=1, source_target_pairs={{0,9},{1,8},{2,11},{3,10},{4,13},{5,12},{6,15},{7,14},{8,1},{9,0},... | collective-permute-start | bytes 147464 | tf_op jit(solution)/shard_map/ppermute | solution.py:315
  10.2 15.9 %collective-permute-start.2 = (bf16[384,768]{1,0:T(8,128)(2,1)S(1)}, bf16[384,768]{1,0:T(8,128)(2,1)S(1)}, u32[]{:S(2)}, u32[]{:S(2)}) collective-permute-start(bf16[384,768]{1,0:T(8,128)(2,1)S(1)} %standard.1.own_ref), channel_id=1, source_target_pairs={{0,4},{2,6},{4,8},{6,10},{8,12},{10,14},{12,0},{14,2},{1,5},{3,7},... | collective-permute-start | bytes 1769480 | tf_op jit(solution)/shard_map/ppermute | solution.py:317
  10.6 15.5 %collective-permute-start.3 = (bf16[384,768]{1,0:T(8,128)(2,1)S(1)}, bf16[384,768]{1,0:T(8,128)(2,1)S(1)}, u32[]{:S(2)}, u32[]{:S(2)}) collective-permute-start(bf16[384,768]{1,0:T(8,128)(2,1)S(1)} %standard.1.own_ref), channel_id=1, source_target_pairs={{0,12},{2,14},{4,0},{6,2},{8,4},{10,6},{12,8},{14,10},{1,13},{3,15... | collective-permute-start | bytes 1769480 | tf_op jit(solution)/shard_map/ppermute | solution.py:318
  12.9 15.5 %collective-permute-start.4 = (bf16[384,768]{1,0:T(8,128)(2,1)S(1)}, bf16[384,768]{1,0:T(8,128)(2,1)S(1)}, u32[]{:S(2)}, u32[]{:S(2)}) collective-permute-start(bf16[384,768]{1,0:T(8,128)(2,1)S(1)} %standard.1.own_ref), channel_id=1, source_target_pairs={{0,1},{1,0},{2,3},{3,2},{4,5},{5,4},{6,7},{7,6},{8,9},{9,8},{10,11... | collective-permute-start | bytes 1769480 | tf_op jit(solution)/shard_map/ppermute | solution.py:319
  28.3 5.6 %collective-permute-start.5 = (bf16[384,768]{1,0:T(8,128)(2,1)S(1)}, bf16[384,768]{1,0:T(8,128)(2,1)S(1)}, u32[]{:S(2)}, u32[]{:S(2)}) collective-permute-start(bf16[384,768]{1,0:T(8,128)(2,1)S(1)} %collective-permute-done.2.refs_0_), channel_id=1, source_target_pairs={{0,2},{2,0},{4,6},{6,4},{8,10},{10,8},{12,14},{14,12},{1,3},{3,1},... | collective-permute-start | bytes 1769480 | tf_op jit(solution)/shard_map/ppermute | solution.py:324
  30.1 3.9 %collective-permute-start.6 = (bf16[384,768]{1,0:T(8,128)(2,1)S(1)}, bf16[384,768]{1,0:T(8,128)(2,1)S(1)}, u32[]{:S(2)}, u32[]{:S(2)}) collective-permute-start(bf16[384,768]{1,0:T(8,128)(2,1)S(1)} %collective-permute-done.3.refs_1_), channel_id=1, source_target_pairs={{0,2},{2,0},{4,6},{6,4},{8,10},{10,8},{12,14},{14,12},{1,3},{3,1},... | collective-permute-start | bytes 1769480 | tf_op jit(solution)/shard_map/ppermute | solution.py:324
  30.1 3.9 %collective-permute-start.7 = (bf16[384,768]{1,0:T(8,128)(2,1)S(1)}, bf16[384,768]{1,0:T(8,128)(2,1)S(1)}, u32[]{:S(2)}, u32[]{:S(2)}) collective-permute-start(bf16[384,768]{1,0:T(8,128)(2,1)S(1)} %collective-permute-done.4.refs_2_.refs_0_), channel_id=1, source_target_pairs={{0,2},{2,0},{4,6},{6,4},{8,10},{10,8},{12,14},{14,12},{1,3},{3,1},... | collective-permute-start | bytes 1769480 | tf_op jit(solution)/shard_map/ppermute | solution.py:324
  40.0 10.9 %collective-permute-start.8 = (f32[16,128]{1,0:T(8,128)S(1)}, f32[16,128]{1,0:T(8,128)S(1)}, u32[]{:S(2)}, u32[]{:S(2)}) collective-permute-start(f32[16,128]{1,0:T(8,128)S(1)} %far.5), channel_id=1, source_target_pairs={{0,9},{1,8},{2,11},{3,10},{4,13},{5,12},{6,15},{7,14},{8,1},{9,0},... | collective-permute-start | bytes 24584 | tf_op jit(solution)/shard_map/ppermute | solution.py:327

commit v5 on v4

--- a/solution.py
+++ b/solution.py
@@ -18,25 +18,6 @@
     centred = values - jnp.mean(values, axis=1, keepdims=True)
     inv_norm = lax.rsqrt(jnp.sum(centred * centred, axis=1, keepdims=True) + 1.0)
     return (centred * inv_norm).astype(jnp.bfloat16)
-
-
-def standard_kernel(x_ref, o_ref):
-    o_ref[...] = standardized(x_ref[0].astype(jnp.float32))
-
-
-def standard_rows(genotypes):
-    _, rows, samples = genotypes.shape
-    step = rows // 3
-    return pl.pallas_call(
-        standard_kernel,
-        grid=(3,),
-        in_specs=[pl.BlockSpec((1, step, samples), lambda i: (0, i, 0))],
-        out_specs=pl.BlockSpec((step, samples), lambda i: (i, 0)),
-        out_shape=jax.ShapeDtypeStruct((rows, samples), jnp.bfloat16),
-        cost_estimate=cost(8 * rows * samples),
-        compiler_params=params(16),
-        name="standard",
-    )(genotypes)
 
 
 def cost(flops):
@@ -114,10 +95,11 @@
         reduce_lanes(best_ref, slot, out_ref, step * per_step)
 
 
-def near_kernel(per_step, pheno_ref, perm_ref, mate_ref, starts_ref, own_ref, twin_ref,
-                table_ref, out_ref, far_mask_ref, base_ref, rows_ref, lead_ref, mask_ref, best_ref):
-    genes, samples = pheno_ref.shape
+def near_kernel(per_step, base_ref, perm_ref, mate_ref, lead_ref, own_ref, twin_ref,
+                table_ref, out_ref, far_mask_ref, rows_ref, mask_ref, best_ref):
+    samples = own_ref.shape[1]
     folds = samples // FOLD
+    genes = base_ref.shape[0] // folds
     local = own_ref.shape[0]
     half_perms = perm_ref.shape[0]
     step = pl.program_id(0)
@@ -125,16 +107,10 @@
 
     @pl.when(step == 0)
     def _():
-        std = standardized(pheno_ref[...])
-        for b in range(folds):
-            base_ref[b * genes:(b + 1) * genes, :] = std[:, b * FOLD:(b + 1) * FOLD]
         rows_ref[:half_perms, :] = perm_ref[...]
         rows_ref[half_perms:, :] = mate_ref[...]
-        wide = jnp.broadcast_to(starts_ref[...].astype(jnp.float32), lead_ref.shape)
-        lead = wide.T.astype(jnp.int32)
-        lead_ref[...] = lead
         for i in range(2):
-            mask_ref[i] = window_mask(near_first[i], lead, local)
+            mask_ref[i] = window_mask(near_first[i], lead_ref[...], local)
 
     shard = jnp.minimum(step, len(far_first) - 1)
     first = far_first[0]
@@ -165,8 +141,37 @@
     return pltpu.with_memory_space_constraint(array, pltpu.HBM)
 
 
-def near_best(phenotypes, perm_rows, mate_rows, starts, shards):
-    genes, samples = phenotypes.shape
+def head_kernel(x_ref, pheno_ref, perm_ref, starts_ref, own_ref, base_ref, rows_ref, lead_ref):
+    own_ref[...] = standardized(x_ref[0].astype(jnp.float32))
+    genes, samples = pheno_ref.shape
+    std = standardized(pheno_ref[...])
+    for b in range(samples // FOLD):
+        base_ref[b * genes:(b + 1) * genes, :] = std[:, b * FOLD:(b + 1) * FOLD]
+    rows_ref[...] = perm_ref[...]
+    wide = jnp.broadcast_to(starts_ref[...].astype(jnp.float32), (lead_ref.shape[1], genes))
+    lead_ref[...] = wide.T.astype(jnp.int32)
+
+
+def head(genotypes, phenotypes, perm_rows, starts):
+    _, local, samples = genotypes.shape
+    genes = phenotypes.shape[0]
+    inputs = (genotypes, phenotypes, perm_rows, starts.reshape(1, genes))
+    return pl.pallas_call(
+        head_kernel,
+        out_shape=[
+            jax.ShapeDtypeStruct((local, samples), jnp.bfloat16),
+            jax.ShapeDtypeStruct((samples // FOLD * genes, FOLD), jnp.bfloat16),
+            jax.ShapeDtypeStruct(perm_rows.shape, jnp.int32),
+            jax.ShapeDtypeStruct((genes, TILE // 2), jnp.int32),
+        ],
+        cost_estimate=cost(8 * local * samples),
+        compiler_params=params(16),
+        name="head",
+    )(*(in_hbm(i) for i in inputs))
+
+
+def near_best(base, perm_rows, mate_rows, lead, shards):
+    genes, samples = lead.shape[0], shards[0].shape[1]
     perms = perm_rows.shape[0] + mate_rows.shape[0]
     local = shards[0].shape[0]
     per_step = 4
@@ -179,10 +184,10 @@
         functools.partial(near_kernel, per_step),
         grid=(perms // per_step,),
         in_specs=[
-            whole((genes, samples)),
+            whole(base.shape),
             whole(perm_rows.shape),
             whole(mate_rows.shape),
-            whole((1, genes)),
+            whole(lead.shape),
             whole((local, samples)),
             whole((local, samples)),
         ],
@@ -197,16 +202,14 @@
             jax.ShapeDtypeStruct((6, genes, local), jnp.float32),
         ],
         scratch_shapes=[
-            pltpu.VMEM((samples // FOLD * genes, FOLD), jnp.bfloat16),
             pltpu.VMEM((perms, samples), jnp.int32),
-            pltpu.VMEM((genes, TILE // 2), jnp.int32),
             pltpu.VMEM((2, genes, local), jnp.float32),
             pltpu.VMEM((2, per_step, genes, TILE // 2), jnp.float32),
         ],
         cost_estimate=cost(2 * perms * genes * samples * (2 * local + samples)),
         compiler_params=params(24),
         name="near",
-    )(in_hbm(phenotypes), in_hbm(perm_rows), mate_rows, in_hbm(starts.reshape(1, genes)), *shards)
+    )(base, perm_rows, mate_rows, lead, *shards)
 
 
 def far_kernel(pairs, per_step, table_ref, before_ref, *refs):
@@ -248,7 +251,7 @@
     )(table, before, *shards, *[masks] * len(pairs))
 
 
-def finish_kernel(spread, best_ref, mate_ref, maxima_ref, sums_ref, *, samples):
+def finish_kernel(best_ref, mate_ref, maxima_ref, sums_ref, *, samples):
     best = jnp.maximum(best_ref[...], mate_ref[...])
     maxima = best * best * samples
     maxima_ref[...] = maxima
@@ -260,7 +263,7 @@
 def finished(best, from_mate, samples, spread):
     perms, genes = best.shape
     return pl.pallas_call(
-        functools.partial(finish_kernel, spread, samples=samples),
+        functools.partial(finish_kernel, samples=samples),
         out_shape=[
             jax.ShapeDtypeStruct((perms, genes), jnp.float32),
             jax.ShapeDtypeStruct((spread, 2, genes), jnp.float32),
@@ -313,12 +316,12 @@
     ]
 
     mate_rows = lax.ppermute(perm_rows, both, mate)
-    own = standard_rows(genotypes)
+    own, base, own_rows, lead = head(genotypes, phenotypes, perm_rows, starts)
+    deep = lax.ppermute(own, "perm", across)
     below = lax.ppermute(own, "var", along(1))
     above = lax.ppermute(own, "var", along(-1))
-    deep = lax.ppermute(own, "perm", across)
     own_twin = lax.ppermute(own, "var", twin)
-    table, near, masks = near_best(phenotypes, perm_rows, mate_rows, starts, (own, own_twin))
+    table, near, masks = near_best(base, own_rows, mate_rows, lead, (own, own_twin))
     below, above, deep, masks = lax.optimization_barrier((below, above, deep, masks))
     far = [below, above, deep]
     far = far + [lax.ppermute(f, "var", twin) for f in far]

time: 69.6 us -> 69.4 us (level)
  blocking collectives: 17.2 us -> 18.5 us
  waiting for transfers between devices: 2.22 us -> 3.52 us
  starting transfers between devices: 15.1 us -> 13.8 us
  local copies, waits for them, and re-layouts: 1.06 us -> 0 us
    ppermute x1, starting transfers between devices: 2.3 us -> 1.01 us  [shards_program(): from_mate = lax.ppermute(to_mate, both, mate)]
    all_to_all x1, blocking collectives: 17.2 us -> 18.5 us  [shards_program(): sent = lax.all_to_all(sums, ('gene', 'var', 'perm'), 0, 0, tiled=True)]
    pallas_call x1, Pallas kernels: 13.2 us -> 11.9 us  [near_best(): pl.pallas_call(functools.partial(near_kernel, per_step), grid=(perms // p...]
    ppermute x1, waiting for transfers between devices: 0.01 us -> 1.09 us  [shards_program(): below = lax.ppermute(own, 'var', along(1))]
    unnamed x2 -> x0, local copies, waits for them, and re-layouts: 1.06 us -> none
    pallas_call x2, Pallas kernels: 1.31 us -> 2.25 us  [the longest x1 1.64 us: head(): pl.pallas_call(head_kernel, out_shape=[jax.ShapeDtypeStruct((local, sampl...]
  transfers between devices with their start and end apart: 9 -> 9, of which waited for: 1 -> 2; matrix products, arithmetic and copies ran while one was open for 0% -> 0% of each run, Pallas kernels for 36% -> 34%
where the time goes in v5:
time: 69.4 us; the launch traced here: 69.3 us
  Pallas kernels  32.7 us (47%)
  blocking collectives  18.5 us (27%)
  starting transfers between devices  13.8 us (20%)
  waiting for transfers between devices  3.52 us (5%)
  between operations  0.71 us (1%)
    all_to_all x1, blocking collectives, shards_program(): sent = lax.all_to_all(sums, ('gene', 'var', 'perm'), 0, 0, tiled=True)  18.5 us
    pallas_call x3, Pallas kernels, far_best(): pl.pallas_call(functools.partial(far_kernel, len(pairs), per_step), grid=...  17.8 us
    pallas_call x1, Pallas kernels, near_best(): pl.pallas_call(functools.partial(near_kernel, per_step), grid=(perms // p...  11.9 us
    ppermute x1, starting transfers between devices, shards_program(): mate_rows = lax.ppermute(perm_rows, both, mate)  6.34 us
    ppermute x1, waiting for transfers between devices, shards_program(): deep = lax.ppermute(own, 'perm', across)  2.41 us
    ppermute x3, starting transfers between devices, shards_program(): far = far + [lax.ppermute(f, 'var', twin) for f in far]  2.3 us
    ppermute x1, starting transfers between devices, shards_program(): above = lax.ppermute(own, 'var', along(-1))  2.28 us
    pallas_call x1, Pallas kernels, head(): pl.pallas_call(head_kernel, out_shape=[jax.ShapeDtypeStruct((local, sampl...  1.64 us
  transfers between devices with their start and end apart: 9, of which 2 were waited for; matrix products, arithmetic and copies ran while one was open for 0% of the time, Pallas kernels for 34%

profile of v5, /device:TPU:1, one launch (start us, length us, event | category | flops | bytes accessed | tf_op | source)
XLA Modules:
  0.0 69.3 jit_solution(1706987375746875869)
XLA Ops:
  0.6 1.6 %head.1 = (bf16[384,768]{1,0:T(8,128)(2,1)S(1)}, bf16[384,256]{1,0:T(8,128)(2,1)S(1)}, s32[16,768]{1,0:T(8,128)S(1)}, s32[128,128]{1,0:T(8,128)S(1)}) custom-call(bf16[1,384,768]{2,1,0:T(8,128)(2,1)} %x_ref.1, f32[128,768]{1,0:T(8,128)} %pheno_ref.1, s32[16,768]{1,0:T(8,128)} %perm_ref.1, s32[1,128]{1,0:T(1,128)} %bitcast.2), custom_call_target="tpu_custom_call" | custom-call | flops 2359296 | tf_op jit(solution)/shard_map/head/pallas_call | solution.py:159
  2.3 1.5 %collective-permute-start.1 = (bf16[384,768]{1,0:T(8,128)(2,1)S(1)}, bf16[384,768]{1,0:T(8,128)(2,1)S(1)}, u32[]{:S(2)}, u32[]{:S(2)}) collective-permute-start(bf16[384,768]{1,0:T(8,128)(2,1)S(1)} %get-tuple-element.21.own_ref), channel_id=1, source_target_pairs={{0,2},{2,0},{4,6},{6,4},{8,10},{10,8},{12,14},{14,12},{1,3},{3,1},... | collective-permute-start | bytes 1769480 | tf_op jit(solution)/shard_map/ppermute | solution.py:323
  3.7 6.3 %collective-permute-start = (s32[16,768]{1,0:T(8,128)}, s32[16,768]{1,0:T(8,128)S(1)}, u32[]{:S(2)}, u32[]{:S(2)}) collective-permute-start(s32[16,768]{1,0:T(8,128)} %perm_ref.1), channel_id=1, source_target_pairs={{0,9},{1,8},{2,11},{3,10},{4,13},{5,12},{6,15},{7,14},{8,1},{9,0},... | collective-permute-start | bytes 147464 | tf_op jit(solution)/shard_map/ppermute | solution.py:318
  10.1 0.4 collective-permute-start.2
  10.5 2.3 %collective-permute-start.3 = (bf16[384,768]{1,0:T(8,128)(2,1)S(1)}, bf16[384,768]{1,0:T(8,128)(2,1)S(1)}, u32[]{:S(2)}, u32[]{:S(2)}) collective-permute-start(bf16[384,768]{1,0:T(8,128)(2,1)S(1)} %get-tuple-element.21.own_ref), channel_id=1, source_target_pairs={{0,12},{2,14},{4,0},{6,2},{8,4},{10,6},{12,8},{14,10},{1,13},{3,15... | collective-permute-start | bytes 1769480 | tf_op jit(solution)/shard_map/ppermute | solution.py:322
  12.8 0.0 collective-permute-start.4
  12.8 0.0 collective-permute-done.mate_ref
  12.8 0.0 collective-permute-done.1.twin_ref
  12.8 11.9 %near.1 = (bf16[4096,768]{1,0:T(8,128)(2,1)S(1)}, f32[32,128]{1,0:T(8,128)S(1)}, f32[6,128,384]{2,1,0:T(8,128)S(1)}) custom-call(bf16[384,256]{1,0:T(8,128)(2,1)S(1)} %get-tuple-element.18.base_ref, s32[16,768]{1,0:T(8,128)S(1)} %get-tuple-element.19.perm_ref, s32[16,768]{1,0:T(8,128)S(1)} %collective-permute-done.mate_ref, ...), custom_call_target="tpu_custom_call" | custom-call | flops 9663676416 | tf_op jit(solution)/shard_map/near/pallas_call | solution.py:183
  24.7 1.1 %collective-permute-done.2.refs_0_ = bf16[384,768]{1,0:T(8,128)(2,1)S(1)} collective-permute-done((bf16[384,768]{1,0:T(8,128)(2,1)S(1)}, bf16[384,768]{1,0:T(8,128)(2,1)S(1)}, u32[]{:S(2)}, u32[]{:S(2)}) %collective-permute-start.2) | collective-permute-done | bytes 589856 | tf_op jit(solution)/shard_map/ppermute | solution.py:321
  25.8 0.0 collective-permute-done.3.refs_1_
  25.8 2.4 %collective-permute-done.4.refs_2_.refs_0_ = bf16[384,768]{1,0:T(8,128)(2,1)S(1)} collective-permute-done((bf16[384,768]{1,0:T(8,128)(2,1)S(1)}, bf16[384,768]{1,0:T(8,128)(2,1)S(1)}, u32[]{:S(2)}, u32[]{:S(2)}) %collective-permute-start.4) | collective-permute-done | bytes 589856 | tf_op jit(solution)/shard_map/ppermute | solution.py:320
  28.2 1.8 %collective-permute-start.5 = (bf16[384,768]{1,0:T(8,128)(2,1)S(1)}, bf16[384,768]{1,0:T(8,128)(2,1)S(1)}, u32[]{:S(2)}, u32[]{:S(2)}) collective-permute-start(bf16[384,768]{1,0:T(8,128)(2,1)S(1)} %collective-permute-done.2.refs_0_), channel_id=1, source_target_pairs={{0,2},{2,0},{4,6},{6,4},{8,10},{10,8},{12,14},{14,12},{1,3},{3,1},... | collective-permute-start | bytes 1769480 | tf_op jit(solution)/shard_map/ppermute | solution.py:327
  30.0 0.0 collective-permute-start.6
  30.0 0.5 collective-permute-start.7
  30.5 3.3 %far.4.before_ref = f32[16,128]{1,0:T(8,128)S(1)} custom-call(bf16[4096,768]{1,0:T(8,128)(2,1)S(1)} %get-tuple-element.22.table_ref, f32[32,128]{1,0:T(8,128)S(1)} %get-tuple-element.23.before_ref, bf16[384,768]{1,0:T(8,128)(2,1)S(1)} %collective-permute-done.2.refs_0_, bf16[384,768]{1,0:T(8,128)(2,1)S(1)} %collective-permute-done.3.refs_1_, ...), custom_call_target="tpu_custom_call" | custom-call | flops 2415919104 | tf_op jit(solution)/shard_map/far/pallas_call | solution.py:236
  33.8 0.0 collective-permute-done.5.refs_3_.refs_1_
  33.9 5.9 %far.5 = f32[16,128]{1,0:T(8,128)S(1)} custom-call(bf16[4096,768]{1,0:T(8,128)(2,1)S(1)} %get-tuple-element.22.table_ref, f32[16,128]{1,0:T(8,128)S(1)} %far.4.before_ref, bf16[384,768]{1,0:T(8,128)(2,1)S(1)} %collective-permute-done.4.refs_2_.refs_0_, bf16[384,768]{1,0:T(8,128)(2,1)S(1)} %collective-permute-done.5.refs_3_.refs_1_, ...), custom_call_target="tpu_custom_call" | custom-call | flops 4831838208 | tf_op jit(solution)/shard_map/far/pallas_call | solution.py:236
  39.8 1.0 %collective-permute-start.8 = (f32[16,128]{1,0:T(8,128)S(1)}, f32[16,128]{1,0:T(8,128)S(1)}, u32[]{:S(2)}, u32[]{:S(2)}) collective-permute-start(f32[16,128]{1,0:T(8,128)S(1)} %far.5), channel_id=1, source_target_pairs={{0,9},{1,8},{2,11},{3,10},{4,13},{5,12},{6,15},{7,14},{8,1},{9,0},... | collective-permute-start | bytes 24584 | tf_op jit(solution)/shard_map/ppermute | solution.py:330
  40.8 8.5 %far.3.best_ref = f32[16,128]{1,0:T(8,128)S(1)} custom-call(bf16[4096,768]{1,0:T(8,128)(2,1)S(1)} %get-tuple-element.22.table_ref, f32[32,128]{1,0:T(8,128)S(1)} %get-tuple-element.23.before_ref, bf16[384,768]{1,0:T(8,128)(2,1)S(1)} %collective-permute-done.2.refs_0_, bf16[384,768]{1,0:T(8,128)(2,1)S(1)} %collective-permute-done.3.refs_1_, ...), custom_call_target="tpu_custom_call" | custom-call | flops 7247757312 | tf_op jit(solution)/shard_map/far/pallas_call | solution.py:236
  49.4 0.0 collective-permute-done.8.mate_ref
  49.4 0.6 finish.1
  50.0 18.5 %all_to_all.5.sent_ref = f32[128,2,128]{2,1,0:T(2,128)S(1)} all-to-all(f32[128,2,128]{2,1,0:T(2,128)S(1)} %get-tuple-element.30), channel_id=1, replica_groups=mesh['gene'=8,'var'=8,'perm'=2] {'gene','var','perm'}, dimensions={0} | all-to-all | bytes 262144 | tf_op jit(solution)/shard_map/all_to_all | solution.py:335
  68.5 0.7 %totals.1 = (f32[2,128]{1,0:T(2,128)}, f32[1,2]{1,0:T(1,128)}) custom-call(f32[128,2,128]{2,1,0:T(2,128)S(1)} %all_to_all.5.sent_ref), custom_call_target="tpu_custom_call" | custom-call | tf_op jit(solution)/shard_map/totals/pallas_call | solution.py:291
  (2 shorter events, 0.0 us)
Async XLA Ops:
  2.3 10.5 %collective-permute-start.1 = (bf16[384,768]{1,0:T(8,128)(2,1)S(1)}, bf16[384,768]{1,0:T(8,128)(2,1)S(1)}, u32[]{:S(2)}, u32[]{:S(2)}) collective-permute-start(bf16[384,768]{1,0:T(8,128)(2,1)S(1)} %get-tuple-element.21.own_ref), channel_id=1, source_target_pairs={{0,2},{2,0},{4,6},{6,4},{8,10},{10,8},{12,14},{14,12},{1,3},{3,1},... | collective-permute-start | bytes 1769480 | tf_op jit(solution)/shard_map/ppermute | solution.py:323
  3.7 9.0 %collective-permute-start = (s32[16,768]{1,0:T(8,128)}, s32[16,768]{1,0:T(8,128)S(1)}, u32[]{:S(2)}, u32[]{:S(2)}) collective-permute-start(s32[16,768]{1,0:T(8,128)} %perm_ref.1), channel_id=1, source_target_pairs={{0,9},{1,8},{2,11},{3,10},{4,13},{5,12},{6,15},{7,14},{8,1},{9,0},... | collective-permute-start | bytes 147464 | tf_op jit(solution)/shard_map/ppermute | solution.py:318
  10.1 15.7 %collective-permute-start.2 = (bf16[384,768]{1,0:T(8,128)(2,1)S(1)}, bf16[384,768]{1,0:T(8,128)(2,1)S(1)}, u32[]{:S(2)}, u32[]{:S(2)}) collective-permute-start(bf16[384,768]{1,0:T(8,128)(2,1)S(1)} %get-tuple-element.21.own_ref), channel_id=1, source_target_pairs={{0,4},{2,6},{4,8},{6,10},{8,12},{10,14},{12,0},{14,2},{1,5},{3,7},... | collective-permute-start | bytes 1769480 | tf_op jit(solution)/shard_map/ppermute | solution.py:321
  10.5 15.3 %collective-permute-start.3 = (bf16[384,768]{1,0:T(8,128)(2,1)S(1)}, bf16[384,768]{1,0:T(8,128)(2,1)S(1)}, u32[]{:S(2)}, u32[]{:S(2)}) collective-permute-start(bf16[384,768]{1,0:T(8,128)(2,1)S(1)} %get-tuple-element.21.own_ref), channel_id=1, source_target_pairs={{0,12},{2,14},{4,0},{6,2},{8,4},{10,6},{12,8},{14,10},{1,13},{3,15... | collective-permute-start | bytes 1769480 | tf_op jit(solution)/shard_map/ppermute | solution.py:322
  12.8 15.5 %collective-permute-start.4 = (bf16[384,768]{1,0:T(8,128)(2,1)S(1)}, bf16[384,768]{1,0:T(8,128)(2,1)S(1)}, u32[]{:S(2)}, u32[]{:S(2)}) collective-permute-start(bf16[384,768]{1,0:T(8,128)(2,1)S(1)} %get-tuple-element.21.own_ref), channel_id=1, source_target_pairs={{0,1},{1,0},{2,3},{3,2},{4,5},{5,4},{6,7},{7,6},{8,9},{9,8},{10,11... | collective-permute-start | bytes 1769480 | tf_op jit(solution)/shard_map/ppermute | solution.py:320
  28.2 5.6 %collective-permute-start.5 = (bf16[384,768]{1,0:T(8,128)(2,1)S(1)}, bf16[384,768]{1,0:T(8,128)(2,1)S(1)}, u32[]{:S(2)}, u32[]{:S(2)}) collective-permute-start(bf16[384,768]{1,0:T(8,128)(2,1)S(1)} %collective-permute-done.2.refs_0_), channel_id=1, source_target_pairs={{0,2},{2,0},{4,6},{6,4},{8,10},{10,8},{12,14},{14,12},{1,3},{3,1},... | collective-permute-start | bytes 1769480 | tf_op jit(solution)/shard_map/ppermute | solution.py:327
  30.0 3.9 %collective-permute-start.6 = (bf16[384,768]{1,0:T(8,128)(2,1)S(1)}, bf16[384,768]{1,0:T(8,128)(2,1)S(1)}, u32[]{:S(2)}, u32[]{:S(2)}) collective-permute-start(bf16[384,768]{1,0:T(8,128)(2,1)S(1)} %collective-permute-done.3.refs_1_), channel_id=1, source_target_pairs={{0,2},{2,0},{4,6},{6,4},{8,10},{10,8},{12,14},{14,12},{1,3},{3,1},... | collective-permute-start | bytes 1769480 | tf_op jit(solution)/shard_map/ppermute | solution.py:327
  30.0 3.9 %collective-permute-start.7 = (bf16[384,768]{1,0:T(8,128)(2,1)S(1)}, bf16[384,768]{1,0:T(8,128)(2,1)S(1)}, u32[]{:S(2)}, u32[]{:S(2)}) collective-permute-start(bf16[384,768]{1,0:T(8,128)(2,1)S(1)} %collective-permute-done.4.refs_2_.refs_0_), channel_id=1, source_target_pairs={{0,2},{2,0},{4,6},{6,4},{8,10},{10,8},{12,14},{14,12},{1,3},{3,1},... | collective-permute-start | bytes 1769480 | tf_op jit(solution)/shard_map/ppermute | solution.py:327
  39.8 9.6 %collective-permute-start.8 = (f32[16,128]{1,0:T(8,128)S(1)}, f32[16,128]{1,0:T(8,128)S(1)}, u32[]{:S(2)}, u32[]{:S(2)}) collective-permute-start(f32[16,128]{1,0:T(8,128)S(1)} %far.5), channel_id=1, source_target_pairs={{0,9},{1,8},{2,11},{3,10},{4,13},{5,12},{6,15},{7,14},{8,1},{9,0},... | collective-permute-start | bytes 24584 | tf_op jit(solution)/shard_map/ppermute | solution.py:330

commit v6 on v5

--- a/solution.py
+++ b/solution.py
@@ -35,7 +35,8 @@
         return ((lax.rem(y + up + rows_n, rows_n) * 2 + c) * 2 + d) * local
 
     near = [first(0, True, True), first(0, False, True)]
-    far = [first(u, c, d) for c in (True, False) for u, d in ((-1, True), (1, True), (0, False))]
+    order = [(c, u, True) for c in (True, False) for u in (-1, 1)] + [(c, 0, False) for c in (True, False)]
+    far = [first(u, c, d) for c, u, d in order]
     return near, far
 
 
@@ -229,7 +230,7 @@
     _, genes, local = masks.shape
     perms = table.shape[0] // genes // 2
     count = len(shards)
-    per_step = 8
+    per_step = perms if count == 2 else 8
     steps = perms // per_step
     once = pl.Buffered(1)
     whole = pl.BlockSpec((local, samples), lambda i: (0, 0), pipeline_mode=once)
@@ -322,12 +323,16 @@
     above = lax.ppermute(own, "var", along(-1))
     own_twin = lax.ppermute(own, "var", twin)
     table, near, masks = near_best(base, own_rows, mate_rows, lead, (own, own_twin))
-    below, above, deep, masks = lax.optimization_barrier((below, above, deep, masks))
-    far = [below, above, deep]
-    far = far + [lax.ppermute(f, "var", twin) for f in far]
-    to_mate = far_best(table, 1, near, 1, masks, (0,), far[:2])
-    to_mate = far_best(table, 1, to_mate, 0, masks, (1, 2), far[2:])
+    below, above, masks = lax.optimization_barrier((below, above, masks))
+    below_twin = lax.ppermute(below, "var", twin)
+    above_twin = lax.ppermute(above, "var", twin)
+    to_mate = far_best(table, 1, near, 1, masks, (0,), [below, above])
+    deep, to_mate = lax.optimization_barrier((deep, to_mate))
+    deep_twin = lax.ppermute(deep, "var", twin)
+    to_mate = far_best(table, 1, to_mate, 0, masks, (1,), [below_twin, above_twin])
+    to_mate = far_best(table, 1, to_mate, 0, masks, (2,), [deep, deep_twin])
     from_mate = lax.ppermute(to_mate, both, mate)
+    far = [below, above, below_twin, above_twin, deep, deep_twin]
     best = far_best(table, 0, near, 0, masks, (0, 1, 2), far)
     count = lax.axis_size(("gene", "var", "perm"))
     maxima, sums = finished(best, from_mate, samples, count)

time: 69.4 us -> 67.4 us (0.971)
  blocking collectives: 18.5 us -> 17.2 us
  Pallas kernels: 32.7 us -> 32 us
  starting transfers between devices: 13.8 us -> 14.5 us
    ppermute x1, waiting for transfers between devices: 2.41 us -> 0.01 us  [shards_program(): deep = lax.ppermute(own, 'perm', across)]
    ppermute x1, starting transfers between devices: 1.01 us -> 2.96 us  [shards_program(): from_mate = lax.ppermute(to_mate, both, mate)]
    ppermute x1, starting transfers between devices: 2.28 us -> 0.78 us  [shards_program(): above = lax.ppermute(own, 'var', along(-1))]
    all_to_all x1, blocking collectives: 18.5 us -> 17.2 us  [shards_program(): sent = lax.all_to_all(sums, ('gene', 'var', 'perm'), 0, 0, tiled=True)]
    ppermute x1, waiting for transfers between devices: 0.01 us -> 0.79 us  [shards_program(): above = lax.ppermute(own, 'var', along(-1))]
    ppermute x1, waiting for transfers between devices: 0.01 us -> 0.76 us  [shards_program(): mate_rows = lax.ppermute(perm_rows, both, mate)]
    pallas_call x3 -> x4, Pallas kernels: 17.8 us -> 17.1 us  [far_best(): pl.pallas_call(functools.partial(far_kernel, len(pairs), per_step), grid=...]
  transfers between devices with their start and end apart: 9 -> 9, of which waited for: 2 -> 3; matrix products, arithmetic and copies ran while one was open for 0% -> 0% of each run, Pallas kernels for 34% -> 39%
where the time goes in v6:
time: 67.4 us; the launch traced here: 67.2 us
  Pallas kernels  32 us (47%)
  blocking collectives  17.2 us (26%)
  starting transfers between devices  14.5 us (22%)
  waiting for transfers between devices  2.84 us (4%)
  between operations  0.68 us (1%)
    all_to_all x1, blocking collectives, shards_program(): sent = lax.all_to_all(sums, ('gene', 'var', 'perm'), 0, 0, tiled=True)  17.2 us
    pallas_call x4, Pallas kernels, far_best(): pl.pallas_call(functools.partial(far_kernel, len(pairs), per_step), grid=...  17.1 us
    pallas_call x1, Pallas kernels, near_best(): pl.pallas_call(functools.partial(near_kernel, per_step), grid=(perms // p...  11.9 us
    ppermute x1, starting transfers between devices, shards_program(): mate_rows = lax.ppermute(perm_rows, both, mate)  6.34 us
    ppermute x1, starting transfers between devices, shards_program(): from_mate = lax.ppermute(to_mate, both, mate)  2.96 us
    pallas_call x1, Pallas kernels, head(): pl.pallas_call(head_kernel, out_shape=[jax.ShapeDtypeStruct((local, sampl...  1.64 us
    ppermute x1, starting transfers between devices, shards_program(): below_twin = lax.ppermute(below, 'var', twin)  1.51 us
    ppermute x1, starting transfers between devices, shards_program(): own_twin = lax.ppermute(own, 'var', twin)  1.46 us
  transfers between devices with their start and end apart: 9, of which 3 were waited for; matrix products, arithmetic and copies ran while one was open for 0% of the time, Pallas kernels for 39%

profile of v6, /device:TPU:1, one launch (start us, length us, event | category | flops | bytes accessed | tf_op | source)
XLA Modules:
  0.0 67.2 jit_solution(11087311133727803803)
XLA Ops:
  0.6 1.6 %head.1 = (bf16[384,768]{1,0:T(8,128)(2,1)S(1)}, bf16[384,256]{1,0:T(8,128)(2,1)S(1)}, s32[16,768]{1,0:T(8,128)S(1)}, s32[128,128]{1,0:T(8,128)S(1)}) custom-call(bf16[1,384,768]{2,1,0:T(8,128)(2,1)} %x_ref.1, f32[128,768]{1,0:T(8,128)} %pheno_ref.1, s32[16,768]{1,0:T(8,128)} %perm_ref.1, s32[1,128]{1,0:T(1,128)} %bitcast.2), custom_call_target="tpu_custom_call" | custom-call | flops 2359296 | tf_op jit(solution)/shard_map/head/pallas_call | solution.py:160
  2.3 1.5 %collective-permute-start.1 = (bf16[384,768]{1,0:T(8,128)(2,1)S(1)}, bf16[384,768]{1,0:T(8,128)(2,1)S(1)}, u32[]{:S(2)}, u32[]{:S(2)}) collective-permute-start(bf16[384,768]{1,0:T(8,128)(2,1)S(1)} %get-tuple-element.22.own_ref), channel_id=1, source_target_pairs={{0,2},{2,0},{4,6},{6,4},{8,10},{10,8},{12,14},{14,12},{1,3},{3,1},... | collective-permute-start | bytes 1769480 | tf_op jit(solution)/shard_map/ppermute | solution.py:324
  3.7 6.3 %collective-permute-start = (s32[16,768]{1,0:T(8,128)}, s32[16,768]{1,0:T(8,128)S(1)}, u32[]{:S(2)}, u32[]{:S(2)}) collective-permute-start(s32[16,768]{1,0:T(8,128)} %perm_ref.1), channel_id=1, source_target_pairs={{0,9},{1,8},{2,11},{3,10},{4,13},{5,12},{6,15},{7,14},{8,1},{9,0},... | collective-permute-start | bytes 147464 | tf_op jit(solution)/shard_map/ppermute | solution.py:319
  10.1 0.8 %collective-permute-start.3 = (bf16[384,768]{1,0:T(8,128)(2,1)S(1)}, bf16[384,768]{1,0:T(8,128)(2,1)S(1)}, u32[]{:S(2)}, u32[]{:S(2)}) collective-permute-start(bf16[384,768]{1,0:T(8,128)(2,1)S(1)} %get-tuple-element.22.own_ref), channel_id=1, source_target_pairs={{0,12},{2,14},{4,0},{6,2},{8,4},{10,6},{12,8},{14,10},{1,13},{3,15... | collective-permute-start | bytes 1769480 | tf_op jit(solution)/shard_map/ppermute | solution.py:323
  10.9 0.7 %collective-permute-start.2 = (bf16[384,768]{1,0:T(8,128)(2,1)S(1)}, bf16[384,768]{1,0:T(8,128)(2,1)S(1)}, u32[]{:S(2)}, u32[]{:S(2)}) collective-permute-start(bf16[384,768]{1,0:T(8,128)(2,1)S(1)} %get-tuple-element.22.own_ref), channel_id=1, source_target_pairs={{0,4},{2,6},{4,8},{6,10},{8,12},{10,14},{12,0},{14,2},{1,5},{3,7},... | collective-permute-start | bytes 1769480 | tf_op jit(solution)/shard_map/ppermute | solution.py:322
  11.5 0.8 %collective-permute-done.mate_ref = s32[16,768]{1,0:T(8,128)S(1)} collective-permute-done((s32[16,768]{1,0:T(8,128)}, s32[16,768]{1,0:T(8,128)S(1)}, u32[]{:S(2)}, u32[]{:S(2)}) %collective-permute-start) | collective-permute-done | bytes 49184 | tf_op jit(solution)/shard_map/ppermute | solution.py:319
  12.3 11.9 %near.1 = (bf16[4096,768]{1,0:T(8,128)(2,1)S(1)}, f32[32,128]{1,0:T(8,128)S(1)}, f32[6,128,384]{2,1,0:T(8,128)S(1)}) custom-call(bf16[384,256]{1,0:T(8,128)(2,1)S(1)} %get-tuple-element.19.base_ref, s32[16,768]{1,0:T(8,128)S(1)} %get-tuple-element.20.perm_ref, s32[16,768]{1,0:T(8,128)S(1)} %collective-permute-done.mate_ref, ...), custom_call_target="tpu_custom_call" | custom-call | flops 9663676416 | tf_op jit(solution)/shard_map/near/pallas_call | solution.py:184
  24.2 0.8 %collective-permute-done.3.refs_1_ = bf16[384,768]{1,0:T(8,128)(2,1)S(1)} collective-permute-done((bf16[384,768]{1,0:T(8,128)(2,1)S(1)}, bf16[384,768]{1,0:T(8,128)(2,1)S(1)}, u32[]{:S(2)}, u32[]{:S(2)}) %collective-permute-start.3) | collective-permute-done | bytes 589856 | tf_op jit(solution)/shard_map/ppermute | solution.py:323
  25.0 1.3 %collective-permute-done.2.refs_0_ = bf16[384,768]{1,0:T(8,128)(2,1)S(1)} collective-permute-done((bf16[384,768]{1,0:T(8,128)(2,1)S(1)}, bf16[384,768]{1,0:T(8,128)(2,1)S(1)}, u32[]{:S(2)}, u32[]{:S(2)}) %collective-permute-start.2) | collective-permute-done | bytes 589856 | tf_op jit(solution)/shard_map/ppermute | solution.py:322
  26.3 1.5 %collective-permute-start.4 = (bf16[384,768]{1,0:T(8,128)(2,1)S(1)}, bf16[384,768]{1,0:T(8,128)(2,1)S(1)}, u32[]{:S(2)}, u32[]{:S(2)}) collective-permute-start(bf16[384,768]{1,0:T(8,128)(2,1)S(1)} %collective-permute-done.2.refs_0_), channel_id=1, source_target_pairs={{0,2},{2,0},{4,6},{6,4},{8,10},{10,8},{12,14},{14,12},{1,3},{3,1},... | collective-permute-start | bytes 1769480 | tf_op jit(solution)/shard_map/ppermute | solution.py:327
  27.8 0.0 collective-permute-start.5
  27.8 3.0 %far.4.before_ref = f32[16,128]{1,0:T(8,128)S(1)} custom-call(bf16[4096,768]{1,0:T(8,128)(2,1)S(1)} %get-tuple-element.23.table_ref, f32[32,128]{1,0:T(8,128)S(1)} %get-tuple-element.24.before_ref, bf16[384,768]{1,0:T(8,128)(2,1)S(1)} %collective-permute-done.2.refs_0_, bf16[384,768]{1,0:T(8,128)(2,1)S(1)} %collective-permute-done.3.refs_1_, ...), custom_call_target="tpu_custom_call" | custom-call | flops 2415919104 | tf_op jit(solution)/shard_map/far/pallas_call | solution.py:237
  30.8 0.8 %collective-permute-start.7 = (bf16[384,768]{1,0:T(8,128)(2,1)S(1)}, bf16[384,768]{1,0:T(8,128)(2,1)S(1)}, u32[]{:S(2)}, u32[]{:S(2)}) collective-permute-start(bf16[384,768]{1,0:T(8,128)(2,1)S(1)} %collective-permute-done.6.refs_4_.refs_0_), channel_id=1, source_target_pairs={{0,2},{2,0},{4,6},{6,4},{8,10},{10,8},{12,14},{14,12},{1,3},{3,1},... | collective-permute-start | bytes 1769480 | tf_op jit(solution)/shard_map/ppermute | solution.py:331
  31.5 0.0 collective-permute-done.4.refs_2_.refs_0_
  31.5 0.0 collective-permute-done.5.refs_3_.refs_1_
  31.5 3.0 %far.6.before_ref = f32[16,128]{1,0:T(8,128)S(1)} custom-call(bf16[4096,768]{1,0:T(8,128)(2,1)S(1)} %get-tuple-element.23.table_ref, f32[16,128]{1,0:T(8,128)S(1)} %far.4.before_ref, bf16[384,768]{1,0:T(8,128)(2,1)S(1)} %collective-permute-done.4.refs_2_.refs_0_, bf16[384,768]{1,0:T(8,128)(2,1)S(1)} %collective-permute-done.5.refs_3_.refs_1_, ...), custom_call_target="tpu_custom_call" | custom-call | flops 2415919104 | tf_op jit(solution)/shard_map/far/pallas_call | solution.py:237
  34.5 0.0 collective-permute-done.7.refs_5_.refs_1_
  34.5 3.0 %far.7 = f32[16,128]{1,0:T(8,128)S(1)} custom-call(bf16[4096,768]{1,0:T(8,128)(2,1)S(1)} %get-tuple-element.23.table_ref, f32[16,128]{1,0:T(8,128)S(1)} %far.6.before_ref, bf16[384,768]{1,0:T(8,128)(2,1)S(1)} %collective-permute-done.6.refs_4_.refs_0_, bf16[384,768]{1,0:T(8,128)(2,1)S(1)} %collective-permute-done.7.refs_5_.refs_1_, ...), custom_call_target="tpu_custom_call" | custom-call | flops 2415919104 | tf_op jit(solution)/shard_map/far/pallas_call | solution.py:237
  37.5 3.0 %collective-permute-start.8 = (f32[16,128]{1,0:T(8,128)S(1)}, f32[16,128]{1,0:T(8,128)S(1)}, u32[]{:S(2)}, u32[]{:S(2)}) collective-permute-start(f32[16,128]{1,0:T(8,128)S(1)} %far.7), channel_id=1, source_target_pairs={{0,9},{1,8},{2,11},{3,10},{4,13},{5,12},{6,15},{7,14},{8,1},{9,0},... | collective-permute-start | bytes 24584 | tf_op jit(solution)/shard_map/ppermute | solution.py:334
  40.4 8.3 %far.5.best_ref = f32[16,128]{1,0:T(8,128)S(1)} custom-call(bf16[4096,768]{1,0:T(8,128)(2,1)S(1)} %get-tuple-element.23.table_ref, f32[32,128]{1,0:T(8,128)S(1)} %get-tuple-element.24.before_ref, bf16[384,768]{1,0:T(8,128)(2,1)S(1)} %collective-permute-done.2.refs_0_, bf16[384,768]{1,0:T(8,128)(2,1)S(1)} %collective-permute-done.3.refs_1_, ...), custom_call_target="tpu_custom_call" | custom-call | flops 7247757312 | tf_op jit(solution)/shard_map/far/pallas_call | solution.py:237
  48.7 0.0 collective-permute-done.8.mate_ref
  48.7 0.6 finish.1
  49.3 17.2 %all_to_all.5.sent_ref = f32[128,2,128]{2,1,0:T(2,128)S(1)} all-to-all(f32[128,2,128]{2,1,0:T(2,128)S(1)} %get-tuple-element.32), channel_id=1, replica_groups=mesh['gene'=8,'var'=8,'perm'=2] {'gene','var','perm'}, dimensions={0} | all-to-all | bytes 262144 | tf_op jit(solution)/shard_map/all_to_all | solution.py:340
  66.5 0.7 %totals.1 = (f32[2,128]{1,0:T(2,128)}, f32[1,2]{1,0:T(1,128)}) custom-call(f32[128,2,128]{2,1,0:T(2,128)S(1)} %all_to_all.5.sent_ref), custom_call_target="tpu_custom_call" | custom-call | tf_op jit(solution)/shard_map/totals/pallas_call | solution.py:292
  (3 shorter events, 0.0 us)
Async XLA Ops:
  2.3 10.0 %collective-permute-start.1 = (bf16[384,768]{1,0:T(8,128)(2,1)S(1)}, bf16[384,768]{1,0:T(8,128)(2,1)S(1)}, u32[]{:S(2)}, u32[]{:S(2)}) collective-permute-start(bf16[384,768]{1,0:T(8,128)(2,1)S(1)} %get-tuple-element.22.own_ref), channel_id=1, source_target_pairs={{0,2},{2,0},{4,6},{6,4},{8,10},{10,8},{12,14},{14,12},{1,3},{3,1},... | collective-permute-start | bytes 1769480 | tf_op jit(solution)/shard_map/ppermute | solution.py:324
  3.7 8.6 %collective-permute-start = (s32[16,768]{1,0:T(8,128)}, s32[16,768]{1,0:T(8,128)S(1)}, u32[]{:S(2)}, u32[]{:S(2)}) collective-permute-start(s32[16,768]{1,0:T(8,128)} %perm_ref.1), channel_id=1, source_target_pairs={{0,9},{1,8},{2,11},{3,10},{4,13},{5,12},{6,15},{7,14},{8,1},{9,0},... | collective-permute-start | bytes 147464 | tf_op jit(solution)/shard_map/ppermute | solution.py:319
  10.1 20.7 %collective-permute-start.6 = (bf16[384,768]{1,0:T(8,128)(2,1)S(1)}, bf16[384,768]{1,0:T(8,128)(2,1)S(1)}, u32[]{:S(2)}, u32[]{:S(2)}) collective-permute-start(bf16[384,768]{1,0:T(8,128)(2,1)S(1)} %get-tuple-element.22.own_ref), channel_id=1, source_target_pairs={{0,1},{1,0},{2,3},{3,2},{4,5},{5,4},{6,7},{7,6},{8,9},{9,8},{10,11... | collective-permute-start | bytes 1769480 | tf_op jit(solution)/shard_map/ppermute | solution.py:321
  10.1 14.9 %collective-permute-start.3 = (bf16[384,768]{1,0:T(8,128)(2,1)S(1)}, bf16[384,768]{1,0:T(8,128)(2,1)S(1)}, u32[]{:S(2)}, u32[]{:S(2)}) collective-permute-start(bf16[384,768]{1,0:T(8,128)(2,1)S(1)} %get-tuple-element.22.own_ref), channel_id=1, source_target_pairs={{0,12},{2,14},{4,0},{6,2},{8,4},{10,6},{12,8},{14,10},{1,13},{3,15... | collective-permute-start | bytes 1769480 | tf_op jit(solution)/shard_map/ppermute | solution.py:323
  10.9 15.4 %collective-permute-start.2 = (bf16[384,768]{1,0:T(8,128)(2,1)S(1)}, bf16[384,768]{1,0:T(8,128)(2,1)S(1)}, u32[]{:S(2)}, u32[]{:S(2)}) collective-permute-start(bf16[384,768]{1,0:T(8,128)(2,1)S(1)} %get-tuple-element.22.own_ref), channel_id=1, source_target_pairs={{0,4},{2,6},{4,8},{6,10},{8,12},{10,14},{12,0},{14,2},{1,5},{3,7},... | collective-permute-start | bytes 1769480 | tf_op jit(solution)/shard_map/ppermute | solution.py:322
  26.3 5.2 %collective-permute-start.4 = (bf16[384,768]{1,0:T(8,128)(2,1)S(1)}, bf16[384,768]{1,0:T(8,128)(2,1)S(1)}, u32[]{:S(2)}, u32[]{:S(2)}) collective-permute-start(bf16[384,768]{1,0:T(8,128)(2,1)S(1)} %collective-permute-done.2.refs_0_), channel_id=1, source_target_pairs={{0,2},{2,0},{4,6},{6,4},{8,10},{10,8},{12,14},{14,12},{1,3},{3,1},... | collective-permute-start | bytes 1769480 | tf_op jit(solution)/shard_map/ppermute | solution.py:327
  27.8 3.7 %collective-permute-start.5 = (bf16[384,768]{1,0:T(8,128)(2,1)S(1)}, bf16[384,768]{1,0:T(8,128)(2,1)S(1)}, u32[]{:S(2)}, u32[]{:S(2)}) collective-permute-start(bf16[384,768]{1,0:T(8,128)(2,1)S(1)} %collective-permute-done.3.refs_1_), channel_id=1, source_target_pairs={{0,2},{2,0},{4,6},{6,4},{8,10},{10,8},{12,14},{14,12},{1,3},{3,1},... | collective-permute-start | bytes 1769480 | tf_op jit(solution)/shard_map/ppermute | solution.py:328
  30.8 3.7 %collective-permute-start.7 = (bf16[384,768]{1,0:T(8,128)(2,1)S(1)}, bf16[384,768]{1,0:T(8,128)(2,1)S(1)}, u32[]{:S(2)}, u32[]{:S(2)}) collective-permute-start(bf16[384,768]{1,0:T(8,128)(2,1)S(1)} %collective-permute-done.6.refs_4_.refs_0_), channel_id=1, source_target_pairs={{0,2},{2,0},{4,6},{6,4},{8,10},{10,8},{12,14},{14,12},{1,3},{3,1},... | collective-permute-start | bytes 1769480 | tf_op jit(solution)/shard_map/ppermute | solution.py:331
  37.5 11.3 %collective-permute-start.8 = (f32[16,128]{1,0:T(8,128)S(1)}, f32[16,128]{1,0:T(8,128)S(1)}, u32[]{:S(2)}, u32[]{:S(2)}) collective-permute-start(f32[16,128]{1,0:T(8,128)S(1)} %far.7), channel_id=1, source_target_pairs={{0,9},{1,8},{2,11},{3,10},{4,13},{5,12},{6,15},{7,14},{8,1},{9,0},... | collective-permute-start | bytes 24584 | tf_op jit(solution)/shard_map/ppermute | solution.py:334

commit v7 on v6

--- a/solution.py
+++ b/solution.py
@@ -213,65 +213,76 @@
     )(base, perm_rows, mate_rows, lead, *shards)
 
 
-def far_kernel(pairs, per_step, table_ref, before_ref, *refs):
-    count = 2 * pairs
-    shards, mask_refs, (out_ref, best_ref) = refs[:count], refs[count:count + pairs], refs[count + pairs:]
-    local = shards[0].shape[0]
-    masks = [(m, k) for m in mask_refs for k in range(2)]
-    score_step(table_ref[...], shards, local, masks, per_step, best_ref, out_ref)
-
-    @pl.when(pl.program_id(0) == pl.num_programs(0) - 1)
-    def _():
-        out_ref[...] = jnp.maximum(out_ref[...], before_ref[...])
-
-
-def far_best(table, part, before, before_part, masks, pairs, shards):
-    samples = table.shape[1]
-    _, genes, local = masks.shape
-    perms = table.shape[0] // genes // 2
-    count = len(shards)
-    per_step = perms if count == 2 else 8
-    steps = perms // per_step
-    once = pl.Buffered(1)
-    whole = pl.BlockSpec((local, samples), lambda i: (0, 0), pipeline_mode=once)
-    return pl.pallas_call(
-        functools.partial(far_kernel, len(pairs), per_step),
-        grid=(steps,),
-        in_specs=[
-            pl.BlockSpec((per_step * genes, samples), lambda i: (i + part * steps, 0)),
-            pl.BlockSpec((perms, genes), lambda i: (before_part, 0), pipeline_mode=once),
-            *[whole] * count,
-            *[pl.BlockSpec((2, genes, local), lambda i, k=k: (k, 0, 0), pipeline_mode=once) for k in pairs],
-        ],
-        out_specs=pl.BlockSpec((perms, genes), lambda i: (0, 0)),
-        out_shape=jax.ShapeDtypeStruct((perms, genes), jnp.float32),
-        scratch_shapes=[pltpu.VMEM((2, per_step, genes, TILE // 2), jnp.float32)],
-        cost_estimate=cost(2 * perms * genes * samples * count * local),
-        compiler_params=params(24),
-        name="far",
-    )(table, before, *shards, *[masks] * len(pairs))
-
-
-def finish_kernel(best_ref, mate_ref, maxima_ref, sums_ref, *, samples):
-    best = jnp.maximum(best_ref[...], mate_ref[...])
-    maxima = best * best * samples
+def reduced(best):
+    perms, genes, half = best.shape
+    lane = lax.broadcasted_iota(jnp.int32, (genes, half), 1)
+    gene = lax.broadcasted_iota(jnp.int32, (genes, half), 0)
+    rows = []
+    for p in range(perms):
+        top = jnp.max(best[p], axis=1, keepdims=True)
+        rows.append(jnp.max(jnp.where(lane == gene, top, 0.0), axis=0, keepdims=True))
+    return jnp.concatenate(rows, axis=0)
+
+
+def far_kernel(start, close, table_ref, near_ref, mask_ref, one_ref, two_ref, *refs):
+    genes = near_ref.shape[1]
+    local = one_ref.shape[0]
+    copies = table_ref.shape[0] // genes
+    best = lane_best(
+        table_ref[...], (one_ref, two_ref), local, [(mask_ref, 0), (mask_ref, 1)], copies
+    )
+    refs = list(refs)
+    if not start:
+        best = jnp.maximum(best, refs.pop(0)[...])
+    if close == "none":
+        refs[0][...] = best
+        return
+    top = jnp.maximum(reduced(best), near_ref[...])
+    if close == "send":
+        refs[0][...] = top
+        return
+    mate_ref, maxima_ref, sums_ref = refs
+    top = jnp.maximum(top, mate_ref[...])
+    maxima = top * top * one_ref.shape[1]
     maxima_ref[...] = maxima
     log_stat = jnp.log1p(maxima)
     sums = jnp.stack((jnp.sum(log_stat, axis=0), jnp.sum(log_stat * log_stat, axis=0)))
     sums_ref[...] = jnp.broadcast_to(sums[None], sums_ref.shape)
 
 
-def finished(best, from_mate, samples, spread):
-    perms, genes = best.shape
-    return pl.pallas_call(
-        functools.partial(finish_kernel, samples=samples),
-        out_shape=[
-            jax.ShapeDtypeStruct((perms, genes), jnp.float32),
-            jax.ShapeDtypeStruct((spread, 2, genes), jnp.float32),
-        ],
-        compiler_params=params(4),
-        name="finish",
-    )(best, from_mate)
+def far_best(table, part, near, masks, pair, shards, carried=None, close="none", from_mate=None, spread=0):
+    samples = table.shape[1]
+    _, genes, local = masks.shape
+    perms = table.shape[0] // genes // 2
+    rows = perms * genes
+    wide = (perms, genes, TILE // 2)
+    once = pl.Buffered(1)
+
+    def whole(shape):
+        return pl.BlockSpec(shape, lambda i: (0,) * len(shape), pipeline_mode=once)
+
+    extra = [x for x in (carried, from_mate) if x is not None]
+    shape = {
+        "none": [wide], "send": [(perms, genes)], "finish": [(perms, genes), (spread, 2, genes)]
+    }[close]
+    out = pl.pallas_call(
+        functools.partial(far_kernel, carried is None, close),
+        grid=(1,),
+        in_specs=[
+            pl.BlockSpec((rows, samples), lambda i: (part, 0), pipeline_mode=once),
+            pl.BlockSpec((perms, genes), lambda i: (part, 0), pipeline_mode=once),
+            pl.BlockSpec((2, genes, local), lambda i: (pair, 0, 0), pipeline_mode=once),
+            whole((local, samples)),
+            whole((local, samples)),
+            *[whole(x.shape) for x in extra],
+        ],
+        out_specs=[whole(x) for x in shape],
+        out_shape=[jax.ShapeDtypeStruct(x, jnp.float32) for x in shape],
+        cost_estimate=cost(2 * rows * samples * 2 * local),
+        compiler_params=params(24),
+        name="far",
+    )(table, near, masks, *shards, *extra)
+    return out if len(out) > 1 else out[0]
 
 
 def totals_kernel(sent_ref, moments_ref, pooled_ref):
@@ -304,7 +315,6 @@
     var_n = lax.axis_size("var")
     rows_n = var_n // 2
     both = ("var", "perm")
-    samples = phenotypes.shape[1]
 
     def along(step):
         return [(v, ((v // 2 + step) % rows_n) * 2 + v % 2) for v in range(var_n)]
@@ -326,16 +336,18 @@
     below, above, masks = lax.optimization_barrier((below, above, masks))
     below_twin = lax.ppermute(below, "var", twin)
     above_twin = lax.ppermute(above, "var", twin)
-    to_mate = far_best(table, 1, near, 1, masks, (0,), [below, above])
-    deep, to_mate = lax.optimization_barrier((deep, to_mate))
+    lanes = far_best(table, 1, near, masks, 0, (below, above))
+    deep, lanes = lax.optimization_barrier((deep, lanes))
     deep_twin = lax.ppermute(deep, "var", twin)
-    to_mate = far_best(table, 1, to_mate, 0, masks, (1,), [below_twin, above_twin])
-    to_mate = far_best(table, 1, to_mate, 0, masks, (2,), [deep, deep_twin])
+    lanes = far_best(table, 1, near, masks, 1, (below_twin, above_twin), lanes)
+    to_mate = far_best(table, 1, near, masks, 2, (deep, deep_twin), lanes, "send")
     from_mate = lax.ppermute(to_mate, both, mate)
-    far = [below, above, below_twin, above_twin, deep, deep_twin]
-    best = far_best(table, 0, near, 0, masks, (0, 1, 2), far)
+    lanes = far_best(table, 0, near, masks, 0, (below, above))
+    lanes = far_best(table, 0, near, masks, 1, (below_twin, above_twin), lanes)
     count = lax.axis_size(("gene", "var", "perm"))
-    maxima, sums = finished(best, from_mate, samples, count)
+    maxima, sums = far_best(
+        table, 0, near, masks, 2, (deep, deep_twin), lanes, "finish", from_mate, count
+    )
 
     sent = lax.all_to_all(sums, ("gene", "var", "perm"), 0, 0, tiled=True)
     moments, pooled = totals(sent)

time: 67.4 us -> 68.9 us (1.022)
  waiting for transfers between devices: 2.84 us -> 3.59 us
  blocking collectives: 17.2 us -> 17.9 us
    all_to_all x1, blocking collectives: 17.2 us -> 17.9 us  [shards_program(): sent = lax.all_to_all(sums, ('gene', 'var', 'perm'), 0, 0, tiled=True)]
    ppermute x1, waiting for transfers between devices: 0.01 us -> 0.75 us  [shards_program(): from_mate = lax.ppermute(to_mate, both, mate)]
    pallas_call x5 -> x6, Pallas kernels: 17.7 us -> 17.5 us  [far_best(): pl.pallas_call(functools.partial(far_kernel, carried is None, close), gri...]
  transfers between devices with their start and end apart: 9 -> 9, of which waited for: 3 -> 4; matrix products, arithmetic and copies ran while one was open for 0% -> 0% of each run, Pallas kernels for 39% -> 33%
where the time goes in v7:
time: 68.9 us; the launch traced here: 68.7 us
  Pallas kernels  31.8 us (46%)
  blocking collectives  17.9 us (26%)
  starting transfers between devices  14.7 us (21%)
  waiting for transfers between devices  3.59 us (5%)
  between operations  0.71 us (1%)
    all_to_all x1, blocking collectives, shards_program(): sent = lax.all_to_all(sums, ('gene', 'var', 'perm'), 0, 0, tiled=True)  17.9 us
    pallas_call x6, Pallas kernels, far_best(): pl.pallas_call(functools.partial(far_kernel, carried is None, close), gri...  17.5 us
    pallas_call x1, Pallas kernels, near_best(): pl.pallas_call(functools.partial(near_kernel, per_step), grid=(perms // p...  11.9 us
    ppermute x1, starting transfers between devices, shards_program(): mate_rows = lax.ppermute(perm_rows, both, mate)  6.34 us
    ppermute x1, starting transfers between devices, shards_program(): from_mate = lax.ppermute(to_mate, both, mate)  3.19 us
    pallas_call x1, Pallas kernels, head(): pl.pallas_call(head_kernel, out_shape=[jax.ShapeDtypeStruct((local, sampl...  1.64 us
    ppermute x1, starting transfers between devices, shards_program(): below_twin = lax.ppermute(below, 'var', twin)  1.51 us
    ppermute x1, starting transfers between devices, shards_program(): own_twin = lax.ppermute(own, 'var', twin)  1.46 us
  transfers between devices with their start and end apart: 9, of which 4 were waited for; matrix products, arithmetic and copies ran while one was open for 0% of the time, Pallas kernels for 33%

profile of v7, /device:TPU:1, one launch (start us, length us, event | category | flops | bytes accessed | tf_op | source)
XLA Modules:
  0.0 68.7 jit_solution(7453416131541104833)
XLA Ops:
  0.6 1.6 %head.1 = (bf16[384,768]{1,0:T(8,128)(2,1)S(1)}, bf16[384,256]{1,0:T(8,128)(2,1)S(1)}, s32[16,768]{1,0:T(8,128)S(1)}, s32[128,128]{1,0:T(8,128)S(1)}) custom-call(bf16[1,384,768]{2,1,0:T(8,128)(2,1)} %x_ref.1, f32[128,768]{1,0:T(8,128)} %pheno_ref.1, s32[16,768]{1,0:T(8,128)} %perm_ref.1, s32[1,128]{1,0:T(1,128)} %bitcast.2), custom_call_target="tpu_custom_call" | custom-call | flops 2359296 | tf_op jit(solution)/shard_map/head/pallas_call | solution.py:160
  2.3 1.5 %collective-permute-start.1 = (bf16[384,768]{1,0:T(8,128)(2,1)S(1)}, bf16[384,768]{1,0:T(8,128)(2,1)S(1)}, u32[]{:S(2)}, u32[]{:S(2)}) collective-permute-start(bf16[384,768]{1,0:T(8,128)(2,1)S(1)} %get-tuple-element.22.own_ref), channel_id=1, source_target_pairs={{0,2},{2,0},{4,6},{6,4},{8,10},{10,8},{12,14},{14,12},{1,3},{3,1},... | collective-permute-start | bytes 1769480 | tf_op jit(solution)/shard_map/ppermute | solution.py:334
  3.7 6.3 %collective-permute-start = (s32[16,768]{1,0:T(8,128)}, s32[16,768]{1,0:T(8,128)S(1)}, u32[]{:S(2)}, u32[]{:S(2)}) collective-permute-start(s32[16,768]{1,0:T(8,128)} %perm_ref.1), channel_id=1, source_target_pairs={{0,9},{1,8},{2,11},{3,10},{4,13},{5,12},{6,15},{7,14},{8,1},{9,0},... | collective-permute-start | bytes 147464 | tf_op jit(solution)/shard_map/ppermute | solution.py:329
  10.1 0.0 collective-permute-start.4
  10.1 0.8 %collective-permute-start.3 = (bf16[384,768]{1,0:T(8,128)(2,1)S(1)}, bf16[384,768]{1,0:T(8,128)(2,1)S(1)}, u32[]{:S(2)}, u32[]{:S(2)}) collective-permute-start(bf16[384,768]{1,0:T(8,128)(2,1)S(1)} %get-tuple-element.22.own_ref), channel_id=1, source_target_pairs={{0,12},{2,14},{4,0},{6,2},{8,4},{10,6},{12,8},{14,10},{1,13},{3,15... | collective-permute-start | bytes 1769480 | tf_op jit(solution)/shard_map/ppermute | solution.py:333
  10.9 0.7 %collective-permute-start.2 = (bf16[384,768]{1,0:T(8,128)(2,1)S(1)}, bf16[384,768]{1,0:T(8,128)(2,1)S(1)}, u32[]{:S(2)}, u32[]{:S(2)}) collective-permute-start(bf16[384,768]{1,0:T(8,128)(2,1)S(1)} %get-tuple-element.22.own_ref), channel_id=1, source_target_pairs={{0,4},{2,6},{4,8},{6,10},{8,12},{10,14},{12,0},{14,2},{1,5},{3,7},... | collective-permute-start | bytes 1769480 | tf_op jit(solution)/shard_map/ppermute | solution.py:332
  11.5 0.8 %collective-permute-done.mate_ref = s32[16,768]{1,0:T(8,128)S(1)} collective-permute-done((s32[16,768]{1,0:T(8,128)}, s32[16,768]{1,0:T(8,128)S(1)}, u32[]{:S(2)}, u32[]{:S(2)}) %collective-permute-start) | collective-permute-done | bytes 49184 | tf_op jit(solution)/shard_map/ppermute | solution.py:329
  12.3 11.9 %near.1 = (bf16[4096,768]{1,0:T(8,128)(2,1)S(1)}, f32[32,128]{1,0:T(8,128)S(1)}, f32[6,128,384]{2,1,0:T(8,128)S(1)}) custom-call(bf16[384,256]{1,0:T(8,128)(2,1)S(1)} %get-tuple-element.19.base_ref, s32[16,768]{1,0:T(8,128)S(1)} %get-tuple-element.20.perm_ref, s32[16,768]{1,0:T(8,128)S(1)} %collective-permute-done.mate_ref, ...), custom_call_target="tpu_custom_call" | custom-call | flops 9663676416 | tf_op jit(solution)/shard_map/near/pallas_call | solution.py:184
  24.2 0.8 %collective-permute-done.3.two_ref = bf16[384,768]{1,0:T(8,128)(2,1)S(1)} collective-permute-done((bf16[384,768]{1,0:T(8,128)(2,1)S(1)}, bf16[384,768]{1,0:T(8,128)(2,1)S(1)}, u32[]{:S(2)}, u32[]{:S(2)}) %collective-permute-start.3) | collective-permute-done | bytes 589856 | tf_op jit(solution)/shard_map/ppermute | solution.py:333
  25.0 1.3 %collective-permute-done.2.one_ref = bf16[384,768]{1,0:T(8,128)(2,1)S(1)} collective-permute-done((bf16[384,768]{1,0:T(8,128)(2,1)S(1)}, bf16[384,768]{1,0:T(8,128)(2,1)S(1)}, u32[]{:S(2)}, u32[]{:S(2)}) %collective-permute-start.2) | collective-permute-done | bytes 589856 | tf_op jit(solution)/shard_map/ppermute | solution.py:332
  26.3 1.5 %collective-permute-start.6 = (bf16[384,768]{1,0:T(8,128)(2,1)S(1)}, bf16[384,768]{1,0:T(8,128)(2,1)S(1)}, u32[]{:S(2)}, u32[]{:S(2)}) collective-permute-start(bf16[384,768]{1,0:T(8,128)(2,1)S(1)} %collective-permute-done.2.one_ref), channel_id=1, source_target_pairs={{0,2},{2,0},{4,6},{6,4},{8,10},{10,8},{12,14},{14,12},{1,3},{3,1},... | collective-permute-start | bytes 1769480 | tf_op jit(solution)/shard_map/ppermute | solution.py:337
  27.8 0.0 collective-permute-start.7
  27.8 2.7 %far.6.refs_0_ = f32[16,128,128]{2,1,0:T(8,128)S(1)} custom-call(bf16[4096,768]{1,0:T(8,128)(2,1)S(1)} %get-tuple-element.23.table_ref, f32[32,128]{1,0:T(8,128)S(1)} %get-tuple-element.24.near_ref, f32[6,128,384]{2,1,0:T(8,128)S(1)} %get-tuple-element.26.mask_ref, bf16[384,768]{1,0:T(8,128)(2,1)S(1)} %collective-permute-done.2.one_ref, ...), custom_call_target="tpu_custom_call" | custom-call | flops 2415919104 | tf_op jit(solution)/shard_map/far/pallas_call | solution.py:268
  30.5 0.0 collective-permute-done.4.one_ref
  30.5 0.8 %collective-permute-start.5 = (bf16[384,768]{1,0:T(8,128)(2,1)S(1)}, bf16[384,768]{1,0:T(8,128)(2,1)S(1)}, u32[]{:S(2)}, u32[]{:S(2)}) collective-permute-start(bf16[384,768]{1,0:T(8,128)(2,1)S(1)} %collective-permute-done.4.one_ref), channel_id=1, source_target_pairs={{0,2},{2,0},{4,6},{6,4},{8,10},{10,8},{12,14},{14,12},{1,3},{3,1},... | collective-permute-start | bytes 1769480 | tf_op jit(solution)/shard_map/ppermute | solution.py:341
  31.3 2.7 %far.7.refs_0_ = f32[16,128,128]{2,1,0:T(8,128)S(1)} custom-call(bf16[4096,768]{1,0:T(8,128)(2,1)S(1)} %get-tuple-element.23.table_ref, f32[32,128]{1,0:T(8,128)S(1)} %get-tuple-element.24.near_ref, f32[6,128,384]{2,1,0:T(8,128)S(1)} %get-tuple-element.26.mask_ref, bf16[384,768]{1,0:T(8,128)(2,1)S(1)} %collective-permute-done.2.one_ref, ...), custom_call_target="tpu_custom_call" | custom-call | flops 2415919104 | tf_op jit(solution)/shard_map/far/pallas_call | solution.py:268
  34.0 2.8 %far.9.refs_0_ = f32[16,128,128]{2,1,0:T(8,128)S(1)} custom-call(bf16[4096,768]{1,0:T(8,128)(2,1)S(1)} %get-tuple-element.23.table_ref, f32[32,128]{1,0:T(8,128)S(1)} %get-tuple-element.24.near_ref, f32[6,128,384]{2,1,0:T(8,128)S(1)} %get-tuple-element.26.mask_ref, bf16[384,768]{1,0:T(8,128)(2,1)S(1)} %collective-permute-done.6.one_ref, ...), custom_call_target="tpu_custom_call" | custom-call | flops 2415919104 | tf_op jit(solution)/shard_map/far/pallas_call | solution.py:268
  36.8 3.0 %far.10 = f32[16,128]{1,0:T(8,128)S(1)} custom-call(bf16[4096,768]{1,0:T(8,128)(2,1)S(1)} %get-tuple-element.23.table_ref, f32[32,128]{1,0:T(8,128)S(1)} %get-tuple-element.24.near_ref, f32[6,128,384]{2,1,0:T(8,128)S(1)} %get-tuple-element.26.mask_ref, bf16[384,768]{1,0:T(8,128)(2,1)S(1)} %collective-permute-done.4.one_ref, ...), custom_call_target="tpu_custom_call" | custom-call | flops 2415919104 | tf_op jit(solution)/shard_map/far/pallas_call | solution.py:268
  39.8 3.2 %collective-permute-start.8 = (f32[16,128]{1,0:T(8,128)S(1)}, f32[16,128]{1,0:T(8,128)S(1)}, u32[]{:S(2)}, u32[]{:S(2)}) collective-permute-start(f32[16,128]{1,0:T(8,128)S(1)} %far.10), channel_id=1, source_target_pairs={{0,9},{1,8},{2,11},{3,10},{4,13},{5,12},{6,15},{7,14},{8,1},{9,0},... | collective-permute-start | bytes 24584 | tf_op jit(solution)/shard_map/ppermute | solution.py:344
  43.0 2.8 %far.8.refs_0_ = f32[16,128,128]{2,1,0:T(8,128)S(1)} custom-call(bf16[4096,768]{1,0:T(8,128)(2,1)S(1)} %get-tuple-element.23.table_ref, f32[32,128]{1,0:T(8,128)S(1)} %get-tuple-element.24.near_ref, f32[6,128,384]{2,1,0:T(8,128)S(1)} %get-tuple-element.26.mask_ref, bf16[384,768]{1,0:T(8,128)(2,1)S(1)} %collective-permute-done.6.one_ref, ...), custom_call_target="tpu_custom_call" | custom-call | flops 2415919104 | tf_op jit(solution)/shard_map/far/pallas_call | solution.py:268
  45.7 0.8 %collective-permute-done.8.refs_1_ = f32[16,128]{1,0:T(8,128)S(1)} collective-permute-done((f32[16,128]{1,0:T(8,128)S(1)}, f32[16,128]{1,0:T(8,128)S(1)}, u32[]{:S(2)}, u32[]{:S(2)}) %collective-permute-start.8) | collective-permute-done | bytes 8224 | tf_op jit(solution)/shard_map/ppermute | solution.py:344
  46.5 3.6 %far.11 = (f32[16,128]{1,0:T(8,128)}, f32[128,2,128]{2,1,0:T(2,128)S(1)}) custom-call(bf16[4096,768]{1,0:T(8,128)(2,1)S(1)} %get-tuple-element.23.table_ref, f32[32,128]{1,0:T(8,128)S(1)} %get-tuple-element.24.near_ref, f32[6,128,384]{2,1,0:T(8,128)S(1)} %get-tuple-element.26.mask_ref, bf16[384,768]{1,0:T(8,128)(2,1)S(1)} %collective-permute-done.4.one_ref, ...), custom_call_target="tpu_custom_call" | custom-call | flops 2415919104 | tf_op jit(solution)/shard_map/far/pallas_call | solution.py:268
  50.1 17.9 %all_to_all.5.sent_ref = f32[128,2,128]{2,1,0:T(2,128)S(1)} all-to-all(f32[128,2,128]{2,1,0:T(2,128)S(1)} %get-tuple-element.32), channel_id=1, replica_groups=mesh['gene'=8,'var'=8,'perm'=2] {'gene','var','perm'}, dimensions={0} | all-to-all | bytes 262144 | tf_op jit(solution)/shard_map/all_to_all | solution.py:352
  68.0 0.7 %totals.1 = (f32[2,128]{1,0:T(2,128)}, f32[1,2]{1,0:T(1,128)}) custom-call(f32[128,2,128]{2,1,0:T(2,128)S(1)} %all_to_all.5.sent_ref), custom_call_target="tpu_custom_call" | custom-call | tf_op jit(solution)/shard_map/totals/pallas_call | solution.py:303
  (4 shorter events, 0.0 us)
Async XLA Ops:
  2.3 10.0 %collective-permute-start.1 = (bf16[384,768]{1,0:T(8,128)(2,1)S(1)}, bf16[384,768]{1,0:T(8,128)(2,1)S(1)}, u32[]{:S(2)}, u32[]{:S(2)}) collective-permute-start(bf16[384,768]{1,0:T(8,128)(2,1)S(1)} %get-tuple-element.22.own_ref), channel_id=1, source_target_pairs={{0,2},{2,0},{4,6},{6,4},{8,10},{10,8},{12,14},{14,12},{1,3},{3,1},... | collective-permute-start | bytes 1769480 | tf_op jit(solution)/shard_map/ppermute | solution.py:334
  3.7 8.6 %collective-permute-start = (s32[16,768]{1,0:T(8,128)}, s32[16,768]{1,0:T(8,128)S(1)}, u32[]{:S(2)}, u32[]{:S(2)}) collective-permute-start(s32[16,768]{1,0:T(8,128)} %perm_ref.1), channel_id=1, source_target_pairs={{0,9},{1,8},{2,11},{3,10},{4,13},{5,12},{6,15},{7,14},{8,1},{9,0},... | collective-permute-start | bytes 147464 | tf_op jit(solution)/shard_map/ppermute | solution.py:329
  10.1 20.4 %collective-permute-start.4 = (bf16[384,768]{1,0:T(8,128)(2,1)S(1)}, bf16[384,768]{1,0:T(8,128)(2,1)S(1)}, u32[]{:S(2)}, u32[]{:S(2)}) collective-permute-start(bf16[384,768]{1,0:T(8,128)(2,1)S(1)} %get-tuple-element.22.own_ref), channel_id=1, source_target_pairs={{0,1},{1,0},{2,3},{3,2},{4,5},{5,4},{6,7},{7,6},{8,9},{9,8},{10,11... | collective-permute-start | bytes 1769480 | tf_op jit(solution)/shard_map/ppermute | solution.py:331
  10.1 14.9 %collective-permute-start.3 = (bf16[384,768]{1,0:T(8,128)(2,1)S(1)}, bf16[384,768]{1,0:T(8,128)(2,1)S(1)}, u32[]{:S(2)}, u32[]{:S(2)}) collective-permute-start(bf16[384,768]{1,0:T(8,128)(2,1)S(1)} %get-tuple-element.22.own_ref), channel_id=1, source_target_pairs={{0,12},{2,14},{4,0},{6,2},{8,4},{10,6},{12,8},{14,10},{1,13},{3,15... | collective-permute-start | bytes 1769480 | tf_op jit(solution)/shard_map/ppermute | solution.py:333
  10.9 15.4 %collective-permute-start.2 = (bf16[384,768]{1,0:T(8,128)(2,1)S(1)}, bf16[384,768]{1,0:T(8,128)(2,1)S(1)}, u32[]{:S(2)}, u32[]{:S(2)}) collective-permute-start(bf16[384,768]{1,0:T(8,128)(2,1)S(1)} %get-tuple-element.22.own_ref), channel_id=1, source_target_pairs={{0,4},{2,6},{4,8},{6,10},{8,12},{10,14},{12,0},{14,2},{1,5},{3,7},... | collective-permute-start | bytes 1769480 | tf_op jit(solution)/shard_map/ppermute | solution.py:332
  26.3 7.7 %collective-permute-start.6 = (bf16[384,768]{1,0:T(8,128)(2,1)S(1)}, bf16[384,768]{1,0:T(8,128)(2,1)S(1)}, u32[]{:S(2)}, u32[]{:S(2)}) collective-permute-start(bf16[384,768]{1,0:T(8,128)(2,1)S(1)} %collective-permute-done.2.one_ref), channel_id=1, source_target_pairs={{0,2},{2,0},{4,6},{6,4},{8,10},{10,8},{12,14},{14,12},{1,3},{3,1},... | collective-permute-start | bytes 1769480 | tf_op jit(solution)/shard_map/ppermute | solution.py:337
  27.8 6.2 %collective-permute-start.7 = (bf16[384,768]{1,0:T(8,128)(2,1)S(1)}, bf16[384,768]{1,0:T(8,128)(2,1)S(1)}, u32[]{:S(2)}, u32[]{:S(2)}) collective-permute-start(bf16[384,768]{1,0:T(8,128)(2,1)S(1)} %collective-permute-done.3.two_ref), channel_id=1, source_target_pairs={{0,2},{2,0},{4,6},{6,4},{8,10},{10,8},{12,14},{14,12},{1,3},{3,1},... | collective-permute-start | bytes 1769480 | tf_op jit(solution)/shard_map/ppermute | solution.py:338
  30.5 6.3 %collective-permute-start.5 = (bf16[384,768]{1,0:T(8,128)(2,1)S(1)}, bf16[384,768]{1,0:T(8,128)(2,1)S(1)}, u32[]{:S(2)}, u32[]{:S(2)}) collective-permute-start(bf16[384,768]{1,0:T(8,128)(2,1)S(1)} %collective-permute-done.4.one_ref), channel_id=1, source_target_pairs={{0,2},{2,0},{4,6},{6,4},{8,10},{10,8},{12,14},{14,12},{1,3},{3,1},... | collective-permute-start | bytes 1769480 | tf_op jit(solution)/shard_map/ppermute | solution.py:341
  39.8 6.7 %collective-permute-start.8 = (f32[16,128]{1,0:T(8,128)S(1)}, f32[16,128]{1,0:T(8,128)S(1)}, u32[]{:S(2)}, u32[]{:S(2)}) collective-permute-start(f32[16,128]{1,0:T(8,128)S(1)} %far.10), channel_id=1, source_target_pairs={{0,9},{1,8},{2,11},{3,10},{4,13},{5,12},{6,15},{7,14},{8,1},{9,0},... | collective-permute-start | bytes 24584 | tf_op jit(solution)/shard_map/ppermute | solution.py:344

commit v8 on v7

--- a/solution.py
+++ b/solution.py
@@ -12,6 +12,7 @@
 FOLD = 256
 TILE = 256
 LARGE = 3.0e38
+CHUNK = 4
 
 
 def standardized(values):
@@ -227,17 +228,22 @@
 def far_kernel(start, close, table_ref, near_ref, mask_ref, one_ref, two_ref, *refs):
     genes = near_ref.shape[1]
     local = one_ref.shape[0]
-    copies = table_ref.shape[0] // genes
-    best = lane_best(
-        table_ref[...], (one_ref, two_ref), local, [(mask_ref, 0), (mask_ref, 1)], copies
-    )
     refs = list(refs)
-    if not start:
-        best = jnp.maximum(best, refs.pop(0)[...])
+    carried_ref = None if start else refs.pop(0)
+    masks = [(mask_ref, 0), (mask_ref, 1)]
+    tops = []
+    for p in range(0, table_ref.shape[0] // genes, CHUNK):
+        lhs = table_ref[p * genes:(p + CHUNK) * genes, :]
+        best = lane_best(lhs, (one_ref, two_ref), local, masks, CHUNK)
+        if not start:
+            best = jnp.maximum(best, carried_ref[p:p + CHUNK])
+        if close == "none":
+            refs[0][p:p + CHUNK] = best
+        else:
+            tops.append(reduced(best))
     if close == "none":
-        refs[0][...] = best
         return
-    top = jnp.maximum(reduced(best), near_ref[...])
+    top = jnp.maximum(jnp.concatenate(tops, axis=0), near_ref[...])
     if close == "send":
         refs[0][...] = top
         return
@@ -341,6 +347,7 @@
     deep_twin = lax.ppermute(deep, "var", twin)
     lanes = far_best(table, 1, near, masks, 1, (below_twin, above_twin), lanes)
     to_mate = far_best(table, 1, near, masks, 2, (deep, deep_twin), lanes, "send")
+    to_mate, masks = lax.optimization_barrier((to_mate, masks))
     from_mate = lax.ppermute(to_mate, both, mate)
     lanes = far_best(table, 0, near, masks, 0, (below, above))
     lanes = far_best(table, 0, near, masks, 1, (below_twin, above_twin), lanes)

time: 68.9 us -> 68.3 us (level)
  transfers between devices with their start and end apart: 9 -> 9, of which waited for: 4 -> 4; matrix products, arithmetic and copies ran while one was open for 0% -> 0% of each run, Pallas kernels for 33% -> 29%
where the time goes in v8:
time: 68.3 us; the launch traced here: 68.1 us
  Pallas kernels  31.4 us (46%)
  blocking collectives  17.9 us (26%)
  starting transfers between devices  14.5 us (21%)
  waiting for transfers between devices  3.63 us (5%)
  between operations  0.69 us (1%)
    all_to_all x1, blocking collectives, shards_program(): sent = lax.all_to_all(sums, ('gene', 'var', 'perm'), 0, 0, tiled=True)  17.9 us
    pallas_call x6, Pallas kernels, far_best(): pl.pallas_call(functools.partial(far_kernel, carried is None, close), gri...  17.1 us
    pallas_call x1, Pallas kernels, near_best(): pl.pallas_call(functools.partial(near_kernel, per_step), grid=(perms // p...  11.9 us
    ppermute x1, starting transfers between devices, shards_program(): mate_rows = lax.ppermute(perm_rows, both, mate)  6.34 us
    ppermute x1, starting transfers between devices, shards_program(): from_mate = lax.ppermute(to_mate, both, mate)  2.97 us
    pallas_call x1, Pallas kernels, head(): pl.pallas_call(head_kernel, out_shape=[jax.ShapeDtypeStruct((local, sampl...  1.64 us
    ppermute x1, starting transfers between devices, shards_program(): below_twin = lax.ppermute(below, 'var', twin)  1.51 us
    ppermute x1, starting transfers between devices, shards_program(): own_twin = lax.ppermute(own, 'var', twin)  1.46 us
  transfers between devices with their start and end apart: 9, of which 4 were waited for; matrix products, arithmetic and copies ran while one was open for 0% of the time, Pallas kernels for 29%

profile of v8, /device:TPU:1, one launch (start us, length us, event | category | flops | bytes accessed | tf_op | source)
XLA Modules:
  0.0 68.1 jit_solution(679002633255911230)
XLA Ops:
  0.6 1.6 %head.1 = (bf16[384,768]{1,0:T(8,128)(2,1)S(1)}, bf16[384,256]{1,0:T(8,128)(2,1)S(1)}, s32[16,768]{1,0:T(8,128)S(1)}, s32[128,128]{1,0:T(8,128)S(1)}) custom-call(bf16[1,384,768]{2,1,0:T(8,128)(2,1)} %x_ref.1, f32[128,768]{1,0:T(8,128)} %pheno_ref.1, s32[16,768]{1,0:T(8,128)} %perm_ref.1, s32[1,128]{1,0:T(1,128)} %bitcast.2), custom_call_target="tpu_custom_call" | custom-call | flops 2359296 | tf_op jit(solution)/shard_map/head/pallas_call | solution.py:161
  2.3 1.5 %collective-permute-start.1 = (bf16[384,768]{1,0:T(8,128)(2,1)S(1)}, bf16[384,768]{1,0:T(8,128)(2,1)S(1)}, u32[]{:S(2)}, u32[]{:S(2)}) collective-permute-start(bf16[384,768]{1,0:T(8,128)(2,1)S(1)} %get-tuple-element.24.own_ref), channel_id=1, source_target_pairs={{0,2},{2,0},{4,6},{6,4},{8,10},{10,8},{12,14},{14,12},{1,3},{3,1},... | collective-permute-start | bytes 1769480 | tf_op jit(solution)/shard_map/ppermute | solution.py:340
  3.7 6.3 %collective-permute-start = (s32[16,768]{1,0:T(8,128)}, s32[16,768]{1,0:T(8,128)S(1)}, u32[]{:S(2)}, u32[]{:S(2)}) collective-permute-start(s32[16,768]{1,0:T(8,128)} %perm_ref.1), channel_id=1, source_target_pairs={{0,9},{1,8},{2,11},{3,10},{4,13},{5,12},{6,15},{7,14},{8,1},{9,0},... | collective-permute-start | bytes 147464 | tf_op jit(solution)/shard_map/ppermute | solution.py:335
  10.1 0.8 %collective-permute-start.3 = (bf16[384,768]{1,0:T(8,128)(2,1)S(1)}, bf16[384,768]{1,0:T(8,128)(2,1)S(1)}, u32[]{:S(2)}, u32[]{:S(2)}) collective-permute-start(bf16[384,768]{1,0:T(8,128)(2,1)S(1)} %get-tuple-element.24.own_ref), channel_id=1, source_target_pairs={{0,12},{2,14},{4,0},{6,2},{8,4},{10,6},{12,8},{14,10},{1,13},{3,15... | collective-permute-start | bytes 1769480 | tf_op jit(solution)/shard_map/ppermute | solution.py:339
  10.9 0.7 %collective-permute-start.2 = (bf16[384,768]{1,0:T(8,128)(2,1)S(1)}, bf16[384,768]{1,0:T(8,128)(2,1)S(1)}, u32[]{:S(2)}, u32[]{:S(2)}) collective-permute-start(bf16[384,768]{1,0:T(8,128)(2,1)S(1)} %get-tuple-element.24.own_ref), channel_id=1, source_target_pairs={{0,4},{2,6},{4,8},{6,10},{8,12},{10,14},{12,0},{14,2},{1,5},{3,7},... | collective-permute-start | bytes 1769480 | tf_op jit(solution)/shard_map/ppermute | solution.py:338
  11.5 0.8 %collective-permute-done.mate_ref = s32[16,768]{1,0:T(8,128)S(1)} collective-permute-done((s32[16,768]{1,0:T(8,128)}, s32[16,768]{1,0:T(8,128)S(1)}, u32[]{:S(2)}, u32[]{:S(2)}) %collective-permute-start) | collective-permute-done | bytes 49184 | tf_op jit(solution)/shard_map/ppermute | solution.py:335
  12.3 11.9 %near.1 = (bf16[4096,768]{1,0:T(8,128)(2,1)S(1)}, f32[32,128]{1,0:T(8,128)S(1)}, f32[6,128,384]{2,1,0:T(8,128)S(1)}) custom-call(bf16[384,256]{1,0:T(8,128)(2,1)S(1)} %get-tuple-element.21.base_ref, s32[16,768]{1,0:T(8,128)S(1)} %get-tuple-element.22.perm_ref, s32[16,768]{1,0:T(8,128)S(1)} %collective-permute-done.mate_ref, ...), custom_call_target="tpu_custom_call" | custom-call | flops 9663676416 | tf_op jit(solution)/shard_map/near/pallas_call | solution.py:185
  24.2 0.8 %collective-permute-done.3.two_ref = bf16[384,768]{1,0:T(8,128)(2,1)S(1)} collective-permute-done((bf16[384,768]{1,0:T(8,128)(2,1)S(1)}, bf16[384,768]{1,0:T(8,128)(2,1)S(1)}, u32[]{:S(2)}, u32[]{:S(2)}) %collective-permute-start.3) | collective-permute-done | bytes 589856 | tf_op jit(solution)/shard_map/ppermute | solution.py:339
  25.0 1.3 %collective-permute-done.2.one_ref = bf16[384,768]{1,0:T(8,128)(2,1)S(1)} collective-permute-done((bf16[384,768]{1,0:T(8,128)(2,1)S(1)}, bf16[384,768]{1,0:T(8,128)(2,1)S(1)}, u32[]{:S(2)}, u32[]{:S(2)}) %collective-permute-start.2) | collective-permute-done | bytes 589856 | tf_op jit(solution)/shard_map/ppermute | solution.py:338
  26.3 1.5 %collective-permute-start.6 = (bf16[384,768]{1,0:T(8,128)(2,1)S(1)}, bf16[384,768]{1,0:T(8,128)(2,1)S(1)}, u32[]{:S(2)}, u32[]{:S(2)}) collective-permute-start(bf16[384,768]{1,0:T(8,128)(2,1)S(1)} %collective-permute-done.2.one_ref), channel_id=1, source_target_pairs={{0,2},{2,0},{4,6},{6,4},{8,10},{10,8},{12,14},{14,12},{1,3},{3,1},... | collective-permute-start | bytes 1769480 | tf_op jit(solution)/shard_map/ppermute | solution.py:343
  27.8 0.0 collective-permute-start.7
  27.8 2.7 %far.6.refs_0_ = f32[16,128,128]{2,1,0:T(8,128)S(1)} custom-call(bf16[4096,768]{1,0:T(8,128)(2,1)S(1)} %get-tuple-element.25.table_ref, f32[32,128]{1,0:T(8,128)S(1)} %get-tuple-element.26.near_ref, f32[6,128,384]{2,1,0:T(8,128)S(1)} %get-tuple-element.33.mask_ref, bf16[384,768]{1,0:T(8,128)(2,1)S(1)} %collective-permute-done.2.one_ref, ...), custom_call_target="tpu_custom_call" | custom-call | flops 2415919104 | tf_op jit(solution)/shard_map/far/pallas_call | solution.py:274
  30.5 0.0 collective-permute-done.4.one_ref
  30.5 0.8 %collective-permute-start.5 = (bf16[384,768]{1,0:T(8,128)(2,1)S(1)}, bf16[384,768]{1,0:T(8,128)(2,1)S(1)}, u32[]{:S(2)}, u32[]{:S(2)}) collective-permute-start(bf16[384,768]{1,0:T(8,128)(2,1)S(1)} %collective-permute-done.4.one_ref), channel_id=1, source_target_pairs={{0,2},{2,0},{4,6},{6,4},{8,10},{10,8},{12,14},{14,12},{1,3},{3,1},... | collective-permute-start | bytes 1769480 | tf_op jit(solution)/shard_map/ppermute | solution.py:347
  31.3 2.7 %far.7.refs_0_ = f32[16,128,128]{2,1,0:T(8,128)S(1)} custom-call(bf16[4096,768]{1,0:T(8,128)(2,1)S(1)} %get-tuple-element.25.table_ref, f32[32,128]{1,0:T(8,128)S(1)} %get-tuple-element.26.near_ref, f32[6,128,384]{2,1,0:T(8,128)S(1)} %get-tuple-element.33.mask_ref, bf16[384,768]{1,0:T(8,128)(2,1)S(1)} %collective-permute-done.6.one_ref, ...), custom_call_target="tpu_custom_call" | custom-call | flops 2415919104 | tf_op jit(solution)/shard_map/far/pallas_call | solution.py:274
  34.0 0.0 collective-permute-done.5.two_ref
  34.0 2.8 %far.8 = f32[16,128]{1,0:T(8,128)S(1)} custom-call(bf16[4096,768]{1,0:T(8,128)(2,1)S(1)} %get-tuple-element.25.table_ref, f32[32,128]{1,0:T(8,128)S(1)} %get-tuple-element.26.near_ref, f32[6,128,384]{2,1,0:T(8,128)S(1)} %get-tuple-element.33.mask_ref, bf16[384,768]{1,0:T(8,128)(2,1)S(1)} %collective-permute-done.4.one_ref, ...), custom_call_target="tpu_custom_call" | custom-call | flops 2415919104 | tf_op jit(solution)/shard_map/far/pallas_call | solution.py:274
  36.8 2.7 %far.9.refs_0_ = f32[16,128,128]{2,1,0:T(8,128)S(1)} custom-call(bf16[4096,768]{1,0:T(8,128)(2,1)S(1)} %get-tuple-element.25.table_ref, f32[32,128]{1,0:T(8,128)S(1)} %get-tuple-element.26.near_ref, f32[6,128,384]{2,1,0:T(8,128)S(1)} %get-tuple-element.33.mask_ref, bf16[384,768]{1,0:T(8,128)(2,1)S(1)} %collective-permute-done.2.one_ref, ...), custom_call_target="tpu_custom_call" | custom-call | flops 2415919104 | tf_op jit(solution)/shard_map/far/pallas_call | solution.py:274
  39.5 3.0 %collective-permute-start.8 = (f32[16,128]{1,0:T(8,128)S(1)}, f32[16,128]{1,0:T(8,128)S(1)}, u32[]{:S(2)}, u32[]{:S(2)}) collective-permute-start(f32[16,128]{1,0:T(8,128)S(1)} %far.8), channel_id=1, source_target_pairs={{0,9},{1,8},{2,11},{3,10},{4,13},{5,12},{6,15},{7,14},{8,1},{9,0},... | collective-permute-start | bytes 24584 | tf_op jit(solution)/shard_map/ppermute | solution.py:351
  42.5 2.7 %far.10.refs_0_ = f32[16,128,128]{2,1,0:T(8,128)S(1)} custom-call(bf16[4096,768]{1,0:T(8,128)(2,1)S(1)} %get-tuple-element.25.table_ref, f32[32,128]{1,0:T(8,128)S(1)} %get-tuple-element.26.near_ref, f32[6,128,384]{2,1,0:T(8,128)S(1)} %get-tuple-element.33.mask_ref, bf16[384,768]{1,0:T(8,128)(2,1)S(1)} %collective-permute-done.6.one_ref, ...), custom_call_target="tpu_custom_call" | custom-call | flops 2415919104 | tf_op jit(solution)/shard_map/far/pallas_call | solution.py:274
  45.2 0.8 %collective-permute-done.8.refs_1_ = f32[16,128]{1,0:T(8,128)S(1)} collective-permute-done((f32[16,128]{1,0:T(8,128)S(1)}, f32[16,128]{1,0:T(8,128)S(1)}, u32[]{:S(2)}, u32[]{:S(2)}) %collective-permute-start.8) | collective-permute-done | bytes 8224 | tf_op jit(solution)/shard_map/ppermute | solution.py:351
  46.0 3.4 %far.11 = (f32[16,128]{1,0:T(8,128)}, f32[128,2,128]{2,1,0:T(2,128)S(1)}) custom-call(bf16[4096,768]{1,0:T(8,128)(2,1)S(1)} %get-tuple-element.25.table_ref, f32[32,128]{1,0:T(8,128)S(1)} %get-tuple-element.26.near_ref, f32[6,128,384]{2,1,0:T(8,128)S(1)} %get-tuple-element.33.mask_ref, bf16[384,768]{1,0:T(8,128)(2,1)S(1)} %collective-permute-done.4.one_ref, ...), custom_call_target="tpu_custom_call" | custom-call | flops 2415919104 | tf_op jit(solution)/shard_map/far/pallas_call | solution.py:274
  49.5 17.9 %all_to_all.5.sent_ref = f32[128,2,128]{2,1,0:T(2,128)S(1)} all-to-all(f32[128,2,128]{2,1,0:T(2,128)S(1)} %get-tuple-element.36), channel_id=1, replica_groups=mesh['gene'=8,'var'=8,'perm'=2] {'gene','var','perm'}, dimensions={0} | all-to-all | bytes 262144 | tf_op jit(solution)/shard_map/all_to_all | solution.py:359
  67.4 0.7 %totals.1 = (f32[2,128]{1,0:T(2,128)}, f32[1,2]{1,0:T(1,128)}) custom-call(f32[128,2,128]{2,1,0:T(2,128)S(1)} %all_to_all.5.sent_ref), custom_call_target="tpu_custom_call" | custom-call | tf_op jit(solution)/shard_map/totals/pallas_call | solution.py:309
  (4 shorter events, 0.0 us)
Async XLA Ops:
  2.3 10.0 %collective-permute-start.1 = (bf16[384,768]{1,0:T(8,128)(2,1)S(1)}, bf16[384,768]{1,0:T(8,128)(2,1)S(1)}, u32[]{:S(2)}, u32[]{:S(2)}) collective-permute-start(bf16[384,768]{1,0:T(8,128)(2,1)S(1)} %get-tuple-element.24.own_ref), channel_id=1, source_target_pairs={{0,2},{2,0},{4,6},{6,4},{8,10},{10,8},{12,14},{14,12},{1,3},{3,1},... | collective-permute-start | bytes 1769480 | tf_op jit(solution)/shard_map/ppermute | solution.py:340
  3.7 8.6 %collective-permute-start = (s32[16,768]{1,0:T(8,128)}, s32[16,768]{1,0:T(8,128)S(1)}, u32[]{:S(2)}, u32[]{:S(2)}) collective-permute-start(s32[16,768]{1,0:T(8,128)} %perm_ref.1), channel_id=1, source_target_pairs={{0,9},{1,8},{2,11},{3,10},{4,13},{5,12},{6,15},{7,14},{8,1},{9,0},... | collective-permute-start | bytes 147464 | tf_op jit(solution)/shard_map/ppermute | solution.py:335
  10.1 20.4 %collective-permute-start.4 = (bf16[384,768]{1,0:T(8,128)(2,1)S(1)}, bf16[384,768]{1,0:T(8,128)(2,1)S(1)}, u32[]{:S(2)}, u32[]{:S(2)}) collective-permute-start(bf16[384,768]{1,0:T(8,128)(2,1)S(1)} %get-tuple-element.24.own_ref), channel_id=1, source_target_pairs={{0,1},{1,0},{2,3},{3,2},{4,5},{5,4},{6,7},{7,6},{8,9},{9,8},{10,11... | collective-permute-start | bytes 1769480 | tf_op jit(solution)/shard_map/ppermute | solution.py:337
  10.1 14.9 %collective-permute-start.3 = (bf16[384,768]{1,0:T(8,128)(2,1)S(1)}, bf16[384,768]{1,0:T(8,128)(2,1)S(1)}, u32[]{:S(2)}, u32[]{:S(2)}) collective-permute-start(bf16[384,768]{1,0:T(8,128)(2,1)S(1)} %get-tuple-element.24.own_ref), channel_id=1, source_target_pairs={{0,12},{2,14},{4,0},{6,2},{8,4},{10,6},{12,8},{14,10},{1,13},{3,15... | collective-permute-start | bytes 1769480 | tf_op jit(solution)/shard_map/ppermute | solution.py:339
  10.9 15.4 %collective-permute-start.2 = (bf16[384,768]{1,0:T(8,128)(2,1)S(1)}, bf16[384,768]{1,0:T(8,128)(2,1)S(1)}, u32[]{:S(2)}, u32[]{:S(2)}) collective-permute-start(bf16[384,768]{1,0:T(8,128)(2,1)S(1)} %get-tuple-element.24.own_ref), channel_id=1, source_target_pairs={{0,4},{2,6},{4,8},{6,10},{8,12},{10,14},{12,0},{14,2},{1,5},{3,7},... | collective-permute-start | bytes 1769480 | tf_op jit(solution)/shard_map/ppermute | solution.py:338
  26.3 5.0 %collective-permute-start.6 = (bf16[384,768]{1,0:T(8,128)(2,1)S(1)}, bf16[384,768]{1,0:T(8,128)(2,1)S(1)}, u32[]{:S(2)}, u32[]{:S(2)}) collective-permute-start(bf16[384,768]{1,0:T(8,128)(2,1)S(1)} %collective-permute-done.2.one_ref), channel_id=1, source_target_pairs={{0,2},{2,0},{4,6},{6,4},{8,10},{10,8},{12,14},{14,12},{1,3},{3,1},... | collective-permute-start | bytes 1769480 | tf_op jit(solution)/shard_map/ppermute | solution.py:343
  27.8 3.5 %collective-permute-start.7 = (bf16[384,768]{1,0:T(8,128)(2,1)S(1)}, bf16[384,768]{1,0:T(8,128)(2,1)S(1)}, u32[]{:S(2)}, u32[]{:S(2)}) collective-permute-start(bf16[384,768]{1,0:T(8,128)(2,1)S(1)} %collective-permute-done.3.two_ref), channel_id=1, source_target_pairs={{0,2},{2,0},{4,6},{6,4},{8,10},{10,8},{12,14},{14,12},{1,3},{3,1},... | collective-permute-start | bytes 1769480 | tf_op jit(solution)/shard_map/ppermute | solution.py:344
  30.5 3.5 %collective-permute-start.5 = (bf16[384,768]{1,0:T(8,128)(2,1)S(1)}, bf16[384,768]{1,0:T(8,128)(2,1)S(1)}, u32[]{:S(2)}, u32[]{:S(2)}) collective-permute-start(bf16[384,768]{1,0:T(8,128)(2,1)S(1)} %collective-permute-done.4.one_ref), channel_id=1, source_target_pairs={{0,2},{2,0},{4,6},{6,4},{8,10},{10,8},{12,14},{14,12},{1,3},{3,1},... | collective-permute-start | bytes 1769480 | tf_op jit(solution)/shard_map/ppermute | solution.py:347
  39.5 6.5 %collective-permute-start.8 = (f32[16,128]{1,0:T(8,128)S(1)}, f32[16,128]{1,0:T(8,128)S(1)}, u32[]{:S(2)}, u32[]{:S(2)}) collective-permute-start(f32[16,128]{1,0:T(8,128)S(1)} %far.8), channel_id=1, source_target_pairs={{0,9},{1,8},{2,11},{3,10},{4,13},{5,12},{6,15},{7,14},{8,1},{9,0},... | collective-permute-start | bytes 24584 | tf_op jit(solution)/shard_map/ppermute | solution.py:351

commit v9 on v8

--- a/solution.py
+++ b/solution.py
@@ -225,16 +225,17 @@
     return jnp.concatenate(rows, axis=0)
 
 
-def far_kernel(start, close, table_ref, near_ref, mask_ref, one_ref, two_ref, *refs):
+def far_kernel(start, close, pairs, table_ref, near_ref, *refs):
     genes = near_ref.shape[1]
-    local = one_ref.shape[0]
+    mask_refs, shards, refs = refs[:pairs], refs[pairs:3 * pairs], refs[3 * pairs:]
+    local, samples = shards[0].shape
     refs = list(refs)
     carried_ref = None if start else refs.pop(0)
-    masks = [(mask_ref, 0), (mask_ref, 1)]
+    masks = [(m, k) for m in mask_refs for k in range(2)]
     tops = []
     for p in range(0, table_ref.shape[0] // genes, CHUNK):
         lhs = table_ref[p * genes:(p + CHUNK) * genes, :]
-        best = lane_best(lhs, (one_ref, two_ref), local, masks, CHUNK)
+        best = lane_best(lhs, shards, local, masks, CHUNK)
         if not start:
             best = jnp.maximum(best, carried_ref[p:p + CHUNK])
         if close == "none":
@@ -249,14 +250,14 @@
         return
     mate_ref, maxima_ref, sums_ref = refs
     top = jnp.maximum(top, mate_ref[...])
-    maxima = top * top * one_ref.shape[1]
+    maxima = top * top * samples
     maxima_ref[...] = maxima
     log_stat = jnp.log1p(maxima)
     sums = jnp.stack((jnp.sum(log_stat, axis=0), jnp.sum(log_stat * log_stat, axis=0)))
     sums_ref[...] = jnp.broadcast_to(sums[None], sums_ref.shape)
 
 
-def far_best(table, part, near, masks, pair, shards, carried=None, close="none", from_mate=None, spread=0):
+def far_best(table, part, near, masks, pairs, shards, carried=None, close="none", from_mate=None, spread=0):
     samples = table.shape[1]
     _, genes, local = masks.shape
     perms = table.shape[0] // genes // 2
@@ -272,22 +273,21 @@
         "none": [wide], "send": [(perms, genes)], "finish": [(perms, genes), (spread, 2, genes)]
     }[close]
     out = pl.pallas_call(
-        functools.partial(far_kernel, carried is None, close),
+        functools.partial(far_kernel, carried is None, close, len(pairs)),
         grid=(1,),
         in_specs=[
             pl.BlockSpec((rows, samples), lambda i: (part, 0), pipeline_mode=once),
             pl.BlockSpec((perms, genes), lambda i: (part, 0), pipeline_mode=once),
-            pl.BlockSpec((2, genes, local), lambda i: (pair, 0, 0), pipeline_mode=once),
-            whole((local, samples)),
-            whole((local, samples)),
+            *[pl.BlockSpec((2, genes, local), lambda i, k=k: (k, 0, 0), pipeline_mode=once) for k in pairs],
+            *[whole((local, samples))] * len(shards),
             *[whole(x.shape) for x in extra],
         ],
         out_specs=[whole(x) for x in shape],
         out_shape=[jax.ShapeDtypeStruct(x, jnp.float32) for x in shape],
-        cost_estimate=cost(2 * rows * samples * 2 * local),
+        cost_estimate=cost(2 * rows * samples * len(shards) * local),
         compiler_params=params(24),
         name="far",
-    )(table, near, masks, *shards, *extra)
+    )(table, near, *[masks] * len(pairs), *shards, *extra)
     return out if len(out) > 1 else out[0]
 
 
@@ -342,18 +342,16 @@
     below, above, masks = lax.optimization_barrier((below, above, masks))
     below_twin = lax.ppermute(below, "var", twin)
     above_twin = lax.ppermute(above, "var", twin)
-    lanes = far_best(table, 1, near, masks, 0, (below, above))
+    lanes = far_best(table, 1, near, masks, (0,), (below, above))
     deep, lanes = lax.optimization_barrier((deep, lanes))
     deep_twin = lax.ppermute(deep, "var", twin)
-    lanes = far_best(table, 1, near, masks, 1, (below_twin, above_twin), lanes)
-    to_mate = far_best(table, 1, near, masks, 2, (deep, deep_twin), lanes, "send")
-    to_mate, masks = lax.optimization_barrier((to_mate, masks))
+    lanes = far_best(table, 1, near, masks, (1,), (below_twin, above_twin), lanes)
+    to_mate = far_best(table, 1, near, masks, (2,), (deep, deep_twin), lanes, "send")
     from_mate = lax.ppermute(to_mate, both, mate)
-    lanes = far_best(table, 0, near, masks, 0, (below, above))
-    lanes = far_best(table, 0, near, masks, 1, (below_twin, above_twin), lanes)
+    lanes = far_best(table, 0, near, masks, (0, 1), (below, above, below_twin, above_twin))
     count = lax.axis_size(("gene", "var", "perm"))
     maxima, sums = far_best(
-        table, 0, near, masks, 2, (deep, deep_twin), lanes, "finish", from_mate, count
+        table, 0, near, masks, (2,), (deep, deep_twin), lanes, "finish", from_mate, count
     )
 
     sent = lax.all_to_all(sums, ("gene", "var", "perm"), 0, 0, tiled=True)

time: 68.3 us -> 66.5 us (0.974)
  waiting for transfers between devices: 3.63 us -> 2.84 us
  blocking collectives: 17.9 us -> 17.2 us
    ppermute x1, waiting for transfers between devices: 0.79 us -> 0.01 us  [shards_program(): from_mate = lax.ppermute(to_mate, both, mate)]
    all_to_all x1, blocking collectives: 17.9 us -> 17.2 us  [shards_program(): sent = lax.all_to_all(sums, ('gene', 'var', 'perm'), 0, 0, tiled=True)]
    pallas_call x6 -> x5, Pallas kernels: 17.1 us -> 16.9 us  [far_best(): pl.pallas_call(functools.partial(far_kernel, carried is None, close, len(...]
  transfers between devices with their start and end apart: 9 -> 9, of which waited for: 4 -> 3; matrix products, arithmetic and copies ran while one was open for 0% -> 0% of each run, Pallas kernels for 29% -> 34%
where the time goes in v9:
time: 66.5 us; the launch traced here: 66.3 us
  Pallas kernels  31.2 us (47%)
  blocking collectives  17.2 us (26%)
  starting transfers between devices  14.5 us (22%)
  waiting for transfers between devices  2.84 us (4%)
  between operations  0.69 us (1%)
    all_to_all x1, blocking collectives, shards_program(): sent = lax.all_to_all(sums, ('gene', 'var', 'perm'), 0, 0, tiled=True)  17.2 us
    pallas_call x5, Pallas kernels, far_best(): pl.pallas_call(functools.partial(far_kernel, carried is None, close, len(...  16.9 us
    pallas_call x1, Pallas kernels, near_best(): pl.pallas_call(functools.partial(near_kernel, per_step), grid=(perms // p...  11.9 us
    ppermute x1, starting transfers between devices, shards_program(): mate_rows = lax.ppermute(perm_rows, both, mate)  6.34 us
    ppermute x1, starting transfers between devices, shards_program(): from_mate = lax.ppermute(to_mate, both, mate)  3.15 us
    pallas_call x1, Pallas kernels, head(): pl.pallas_call(head_kernel, out_shape=[jax.ShapeDtypeStruct((local, sampl...  1.64 us
    ppermute x1, starting transfers between devices, shards_program(): below_twin = lax.ppermute(below, 'var', twin)  1.51 us
    ppermute x1, starting transfers between devices, shards_program(): own_twin = lax.ppermute(own, 'var', twin)  1.46 us
  transfers between devices with their start and end apart: 9, of which 3 were waited for; matrix products, arithmetic and copies ran while one was open for 0% of the time, Pallas kernels for 34%

profile of v9, /device:TPU:1, one launch (start us, length us, event | category | flops | bytes accessed | tf_op | source)
XLA Modules:
  0.0 66.3 jit_solution(3428597837260939456)
XLA Ops:
  0.6 1.6 %head.1 = (bf16[384,768]{1,0:T(8,128)(2,1)S(1)}, bf16[384,256]{1,0:T(8,128)(2,1)S(1)}, s32[16,768]{1,0:T(8,128)S(1)}, s32[128,128]{1,0:T(8,128)S(1)}) custom-call(bf16[1,384,768]{2,1,0:T(8,128)(2,1)} %x_ref.1, f32[128,768]{1,0:T(8,128)} %pheno_ref.1, s32[16,768]{1,0:T(8,128)} %perm_ref.1, s32[1,128]{1,0:T(1,128)} %bitcast.2), custom_call_target="tpu_custom_call" | custom-call | flops 2359296 | tf_op jit(solution)/shard_map/head/pallas_call | solution.py:161
  2.3 1.5 %collective-permute-start.1 = (bf16[384,768]{1,0:T(8,128)(2,1)S(1)}, bf16[384,768]{1,0:T(8,128)(2,1)S(1)}, u32[]{:S(2)}, u32[]{:S(2)}) collective-permute-start(bf16[384,768]{1,0:T(8,128)(2,1)S(1)} %get-tuple-element.22.own_ref), channel_id=1, source_target_pairs={{0,2},{2,0},{4,6},{6,4},{8,10},{10,8},{12,14},{14,12},{1,3},{3,1},... | collective-permute-start | bytes 1769480 | tf_op jit(solution)/shard_map/ppermute | solution.py:340
  3.7 6.3 %collective-permute-start = (s32[16,768]{1,0:T(8,128)}, s32[16,768]{1,0:T(8,128)S(1)}, u32[]{:S(2)}, u32[]{:S(2)}) collective-permute-start(s32[16,768]{1,0:T(8,128)} %perm_ref.1), channel_id=1, source_target_pairs={{0,9},{1,8},{2,11},{3,10},{4,13},{5,12},{6,15},{7,14},{8,1},{9,0},... | collective-permute-start | bytes 147464 | tf_op jit(solution)/shard_map/ppermute | solution.py:335
  10.1 0.8 %collective-permute-start.3 = (bf16[384,768]{1,0:T(8,128)(2,1)S(1)}, bf16[384,768]{1,0:T(8,128)(2,1)S(1)}, u32[]{:S(2)}, u32[]{:S(2)}) collective-permute-start(bf16[384,768]{1,0:T(8,128)(2,1)S(1)} %get-tuple-element.22.own_ref), channel_id=1, source_target_pairs={{0,12},{2,14},{4,0},{6,2},{8,4},{10,6},{12,8},{14,10},{1,13},{3,15... | collective-permute-start | bytes 1769480 | tf_op jit(solution)/shard_map/ppermute | solution.py:339
  10.9 0.7 %collective-permute-start.2 = (bf16[384,768]{1,0:T(8,128)(2,1)S(1)}, bf16[384,768]{1,0:T(8,128)(2,1)S(1)}, u32[]{:S(2)}, u32[]{:S(2)}) collective-permute-start(bf16[384,768]{1,0:T(8,128)(2,1)S(1)} %get-tuple-element.22.own_ref), channel_id=1, source_target_pairs={{0,4},{2,6},{4,8},{6,10},{8,12},{10,14},{12,0},{14,2},{1,5},{3,7},... | collective-permute-start | bytes 1769480 | tf_op jit(solution)/shard_map/ppermute | solution.py:338
  11.5 0.8 %collective-permute-done.mate_ref = s32[16,768]{1,0:T(8,128)S(1)} collective-permute-done((s32[16,768]{1,0:T(8,128)}, s32[16,768]{1,0:T(8,128)S(1)}, u32[]{:S(2)}, u32[]{:S(2)}) %collective-permute-start) | collective-permute-done | bytes 49184 | tf_op jit(solution)/shard_map/ppermute | solution.py:335
  12.3 11.9 %near.1 = (bf16[4096,768]{1,0:T(8,128)(2,1)S(1)}, f32[32,128]{1,0:T(8,128)S(1)}, f32[6,128,384]{2,1,0:T(8,128)S(1)}) custom-call(bf16[384,256]{1,0:T(8,128)(2,1)S(1)} %get-tuple-element.19.base_ref, s32[16,768]{1,0:T(8,128)S(1)} %get-tuple-element.20.perm_ref, s32[16,768]{1,0:T(8,128)S(1)} %collective-permute-done.mate_ref, ...), custom_call_target="tpu_custom_call" | custom-call | flops 9663676416 | tf_op jit(solution)/shard_map/near/pallas_call | solution.py:185
  24.2 0.8 %collective-permute-done.3.refs_2_.refs_3_ = bf16[384,768]{1,0:T(8,128)(2,1)S(1)} collective-permute-done((bf16[384,768]{1,0:T(8,128)(2,1)S(1)}, bf16[384,768]{1,0:T(8,128)(2,1)S(1)}, u32[]{:S(2)}, u32[]{:S(2)}) %collective-permute-start.3) | collective-permute-done | bytes 589856 | tf_op jit(solution)/shard_map/ppermute | solution.py:339
  25.0 1.3 %collective-permute-done.2.refs_1_.refs_2_ = bf16[384,768]{1,0:T(8,128)(2,1)S(1)} collective-permute-done((bf16[384,768]{1,0:T(8,128)(2,1)S(1)}, bf16[384,768]{1,0:T(8,128)(2,1)S(1)}, u32[]{:S(2)}, u32[]{:S(2)}) %collective-permute-start.2) | collective-permute-done | bytes 589856 | tf_op jit(solution)/shard_map/ppermute | solution.py:338
  26.3 1.5 %collective-permute-start.6 = (bf16[384,768]{1,0:T(8,128)(2,1)S(1)}, bf16[384,768]{1,0:T(8,128)(2,1)S(1)}, u32[]{:S(2)}, u32[]{:S(2)}) collective-permute-start(bf16[384,768]{1,0:T(8,128)(2,1)S(1)} %collective-permute-done.2.refs_1_.refs_2_), channel_id=1, source_target_pairs={{0,2},{2,0},{4,6},{6,4},{8,10},{10,8},{12,14},{14,12},{1,3},{3,1},... | collective-permute-start | bytes 1769480 | tf_op jit(solution)/shard_map/ppermute | solution.py:343
  27.8 0.0 collective-permute-start.7
  27.8 2.7 %far.5.refs_3_ = f32[16,128,128]{2,1,0:T(8,128)S(1)} custom-call(bf16[4096,768]{1,0:T(8,128)(2,1)S(1)} %get-tuple-element.23.table_ref, f32[32,128]{1,0:T(8,128)S(1)} %get-tuple-element.24.near_ref, f32[6,128,384]{2,1,0:T(8,128)S(1)} %get-tuple-element.26.refs_0_.refs_1_, bf16[384,768]{1,0:T(8,128)(2,1)S(1)} %collective-permute-done.2.refs_1_.refs_2_, ...), custom_call_target="tpu_custom_call" | custom-call | flops 2415919104 | tf_op jit(solution)/shard_map/far/pallas_call | solution.py:275
  30.5 0.0 collective-permute-done.4.refs_1_
  30.5 0.6 collective-permute-start.5
  31.1 0.0 collective-permute-done.7.refs_5_.refs_2_
  31.1 2.7 %far.7.refs_3_ = f32[16,128,128]{2,1,0:T(8,128)S(1)} custom-call(bf16[4096,768]{1,0:T(8,128)(2,1)S(1)} %get-tuple-element.23.table_ref, f32[32,128]{1,0:T(8,128)S(1)} %get-tuple-element.24.near_ref, f32[6,128,384]{2,1,0:T(8,128)S(1)} %get-tuple-element.26.refs_0_.refs_1_, bf16[384,768]{1,0:T(8,128)(2,1)S(1)} %collective-permute-done.6.refs_4_.refs_1_, ...), custom_call_target="tpu_custom_call" | custom-call | flops 2415919104 | tf_op jit(solution)/shard_map/far/pallas_call | solution.py:275
  33.8 0.0 collective-permute-done.5.refs_2_
  33.8 2.9 %far.8 = f32[16,128]{1,0:T(8,128)S(1)} custom-call(bf16[4096,768]{1,0:T(8,128)(2,1)S(1)} %get-tuple-element.23.table_ref, f32[32,128]{1,0:T(8,128)S(1)} %get-tuple-element.24.near_ref, f32[6,128,384]{2,1,0:T(8,128)S(1)} %get-tuple-element.26.refs_0_.refs_1_, bf16[384,768]{1,0:T(8,128)(2,1)S(1)} %collective-permute-done.4.refs_1_, ...), custom_call_target="tpu_custom_call" | custom-call | flops 2415919104 | tf_op jit(solution)/shard_map/far/pallas_call | solution.py:275
  36.7 3.2 %collective-permute-start.8 = (f32[16,128]{1,0:T(8,128)S(1)}, f32[16,128]{1,0:T(8,128)S(1)}, u32[]{:S(2)}, u32[]{:S(2)}) collective-permute-start(f32[16,128]{1,0:T(8,128)S(1)} %far.8), channel_id=1, source_target_pairs={{0,9},{1,8},{2,11},{3,10},{4,13},{5,12},{6,15},{7,14},{8,1},{9,0},... | collective-permute-start | bytes 24584 | tf_op jit(solution)/shard_map/ppermute | solution.py:350
  39.9 5.2 %far.6.refs_3_ = f32[16,128,128]{2,1,0:T(8,128)S(1)} custom-call(bf16[4096,768]{1,0:T(8,128)(2,1)S(1)} %get-tuple-element.23.table_ref, f32[32,128]{1,0:T(8,128)S(1)} %get-tuple-element.24.near_ref, f32[6,128,384]{2,1,0:T(8,128)S(1)} %get-tuple-element.26.refs_0_.refs_1_, f32[6,128,384]{2,1,0:T(8,128)S(1)} %get-tuple-element.26.refs_0_.refs_1_, ...), custom_call_target="tpu_custom_call" | custom-call | flops 4831838208 | tf_op jit(solution)/shard_map/far/pallas_call | solution.py:275
  45.0 0.0 collective-permute-done.8.refs_4_
  45.1 3.4 %far.9 = (f32[16,128]{1,0:T(8,128)}, f32[128,2,128]{2,1,0:T(2,128)S(1)}) custom-call(bf16[4096,768]{1,0:T(8,128)(2,1)S(1)} %get-tuple-element.23.table_ref, f32[32,128]{1,0:T(8,128)S(1)} %get-tuple-element.24.near_ref, f32[6,128,384]{2,1,0:T(8,128)S(1)} %get-tuple-element.26.refs_0_.refs_1_, bf16[384,768]{1,0:T(8,128)(2,1)S(1)} %collective-permute-done.4.refs_1_, ...), custom_call_target="tpu_custom_call" | custom-call | flops 2415919104 | tf_op jit(solution)/shard_map/far/pallas_call | solution.py:275
  48.5 17.2 %all_to_all.5.sent_ref = f32[128,2,128]{2,1,0:T(2,128)S(1)} all-to-all(f32[128,2,128]{2,1,0:T(2,128)S(1)} %get-tuple-element.32), channel_id=1, replica_groups=mesh['gene'=8,'var'=8,'perm'=2] {'gene','var','perm'}, dimensions={0} | all-to-all | bytes 262144 | tf_op jit(solution)/shard_map/all_to_all | solution.py:357
  65.6 0.7 %totals.1 = (f32[2,128]{1,0:T(2,128)}, f32[1,2]{1,0:T(1,128)}) custom-call(f32[128,2,128]{2,1,0:T(2,128)S(1)} %all_to_all.5.sent_ref), custom_call_target="tpu_custom_call" | custom-call | tf_op jit(solution)/shard_map/totals/pallas_call | solution.py:309
  (3 shorter events, 0.0 us)
Async XLA Ops:
  2.3 10.0 %collective-permute-start.1 = (bf16[384,768]{1,0:T(8,128)(2,1)S(1)}, bf16[384,768]{1,0:T(8,128)(2,1)S(1)}, u32[]{:S(2)}, u32[]{:S(2)}) collective-permute-start(bf16[384,768]{1,0:T(8,128)(2,1)S(1)} %get-tuple-element.22.own_ref), channel_id=1, source_target_pairs={{0,2},{2,0},{4,6},{6,4},{8,10},{10,8},{12,14},{14,12},{1,3},{3,1},... | collective-permute-start | bytes 1769480 | tf_op jit(solution)/shard_map/ppermute | solution.py:340
  3.7 8.6 %collective-permute-start = (s32[16,768]{1,0:T(8,128)}, s32[16,768]{1,0:T(8,128)S(1)}, u32[]{:S(2)}, u32[]{:S(2)}) collective-permute-start(s32[16,768]{1,0:T(8,128)} %perm_ref.1), channel_id=1, source_target_pairs={{0,9},{1,8},{2,11},{3,10},{4,13},{5,12},{6,15},{7,14},{8,1},{9,0},... | collective-permute-start | bytes 147464 | tf_op jit(solution)/shard_map/ppermute | solution.py:335
  10.1 20.4 %collective-permute-start.4 = (bf16[384,768]{1,0:T(8,128)(2,1)S(1)}, bf16[384,768]{1,0:T(8,128)(2,1)S(1)}, u32[]{:S(2)}, u32[]{:S(2)}) collective-permute-start(bf16[384,768]{1,0:T(8,128)(2,1)S(1)} %get-tuple-element.22.own_ref), channel_id=1, source_target_pairs={{0,1},{1,0},{2,3},{3,2},{4,5},{5,4},{6,7},{7,6},{8,9},{9,8},{10,11... | collective-permute-start | bytes 1769480 | tf_op jit(solution)/shard_map/ppermute | solution.py:337
  10.1 14.9 %collective-permute-start.3 = (bf16[384,768]{1,0:T(8,128)(2,1)S(1)}, bf16[384,768]{1,0:T(8,128)(2,1)S(1)}, u32[]{:S(2)}, u32[]{:S(2)}) collective-permute-start(bf16[384,768]{1,0:T(8,128)(2,1)S(1)} %get-tuple-element.22.own_ref), channel_id=1, source_target_pairs={{0,12},{2,14},{4,0},{6,2},{8,4},{10,6},{12,8},{14,10},{1,13},{3,15... | collective-permute-start | bytes 1769480 | tf_op jit(solution)/shard_map/ppermute | solution.py:339
  10.9 15.4 %collective-permute-start.2 = (bf16[384,768]{1,0:T(8,128)(2,1)S(1)}, bf16[384,768]{1,0:T(8,128)(2,1)S(1)}, u32[]{:S(2)}, u32[]{:S(2)}) collective-permute-start(bf16[384,768]{1,0:T(8,128)(2,1)S(1)} %get-tuple-element.22.own_ref), channel_id=1, source_target_pairs={{0,4},{2,6},{4,8},{6,10},{8,12},{10,14},{12,0},{14,2},{1,5},{3,7},... | collective-permute-start | bytes 1769480 | tf_op jit(solution)/shard_map/ppermute | solution.py:338
  26.3 4.8 %collective-permute-start.6 = (bf16[384,768]{1,0:T(8,128)(2,1)S(1)}, bf16[384,768]{1,0:T(8,128)(2,1)S(1)}, u32[]{:S(2)}, u32[]{:S(2)}) collective-permute-start(bf16[384,768]{1,0:T(8,128)(2,1)S(1)} %collective-permute-done.2.refs_1_.refs_2_), channel_id=1, source_target_pairs={{0,2},{2,0},{4,6},{6,4},{8,10},{10,8},{12,14},{14,12},{1,3},{3,1},... | collective-permute-start | bytes 1769480 | tf_op jit(solution)/shard_map/ppermute | solution.py:343
  27.8 3.3 %collective-permute-start.7 = (bf16[384,768]{1,0:T(8,128)(2,1)S(1)}, bf16[384,768]{1,0:T(8,128)(2,1)S(1)}, u32[]{:S(2)}, u32[]{:S(2)}) collective-permute-start(bf16[384,768]{1,0:T(8,128)(2,1)S(1)} %collective-permute-done.3.refs_2_.refs_3_), channel_id=1, source_target_pairs={{0,2},{2,0},{4,6},{6,4},{8,10},{10,8},{12,14},{14,12},{1,3},{3,1},... | collective-permute-start | bytes 1769480 | tf_op jit(solution)/shard_map/ppermute | solution.py:344
  30.5 3.3 %collective-permute-start.5 = (bf16[384,768]{1,0:T(8,128)(2,1)S(1)}, bf16[384,768]{1,0:T(8,128)(2,1)S(1)}, u32[]{:S(2)}, u32[]{:S(2)}) collective-permute-start(bf16[384,768]{1,0:T(8,128)(2,1)S(1)} %collective-permute-done.4.refs_1_), channel_id=1, source_target_pairs={{0,2},{2,0},{4,6},{6,4},{8,10},{10,8},{12,14},{14,12},{1,3},{3,1},... | collective-permute-start | bytes 1769480 | tf_op jit(solution)/shard_map/ppermute | solution.py:347
  36.7 8.3 %collective-permute-start.8 = (f32[16,128]{1,0:T(8,128)S(1)}, f32[16,128]{1,0:T(8,128)S(1)}, u32[]{:S(2)}, u32[]{:S(2)}) collective-permute-start(f32[16,128]{1,0:T(8,128)S(1)} %far.8), channel_id=1, source_target_pairs={{0,9},{1,8},{2,11},{3,10},{4,13},{5,12},{6,15},{7,14},{8,1},{9,0},... | collective-permute-start | bytes 24584 | tf_op jit(solution)/shard_map/ppermute | solution.py:350

commit v10 on v9

--- a/solution.py
+++ b/solution.py
@@ -12,7 +12,7 @@
 FOLD = 256
 TILE = 256
 LARGE = 3.0e38
-CHUNK = 4
+CHUNK = 8
 
 
 def standardized(values):
@@ -291,7 +291,8 @@
     return out if len(out) > 1 else out[0]
 
 
-def totals_kernel(sent_ref, moments_ref, pooled_ref):
+def totals_kernel(sent_ref, held_ref, maxima_ref, moments_ref, pooled_ref):
+    maxima_ref[...] = held_ref[...]
     count, _, genes = sent_ref.shape
     blocks = lax.axis_size("gene")
     members = count // blocks
@@ -305,16 +306,17 @@
     pooled_ref[...] = spread[:, :2]
 
 
-def totals(sent):
+def totals(sent, held):
     return pl.pallas_call(
         totals_kernel,
         out_shape=[
+            jax.ShapeDtypeStruct(held.shape, jnp.float32),
             jax.ShapeDtypeStruct(sent.shape[1:], jnp.float32),
             jax.ShapeDtypeStruct((1, 2), jnp.float32),
         ],
         compiler_params=params(4),
         name="totals",
-    )(sent)
+    )(sent, held)
 
 
 def shards_program(genotypes, phenotypes, perm_rows, starts):
@@ -350,12 +352,12 @@
     from_mate = lax.ppermute(to_mate, both, mate)
     lanes = far_best(table, 0, near, masks, (0, 1), (below, above, below_twin, above_twin))
     count = lax.axis_size(("gene", "var", "perm"))
-    maxima, sums = far_best(
+    held, sums = far_best(
         table, 0, near, masks, (2,), (deep, deep_twin), lanes, "finish", from_mate, count
     )
 
     sent = lax.all_to_all(sums, ("gene", "var", "perm"), 0, 0, tiled=True)
-    moments, pooled = totals(sent)
+    maxima, moments, pooled = totals(sent, held)
     return (maxima, moments, pooled.reshape(2))
 
 

time: 66.5 us -> 65.9 us (level)
  Pallas kernels: 31.2 us -> 30.5 us
where the time goes in v10:
time: 65.9 us; the launch traced here: 65.7 us
  Pallas kernels  30.5 us (46%)
  blocking collectives  17.2 us (26%)
  starting transfers between devices  14.5 us (22%)
  waiting for transfers between devices  2.84 us (4%)
  between operations  0.7 us (1%)
    all_to_all x1, blocking collectives, shards_program(): sent = lax.all_to_all(sums, ('gene', 'var', 'perm'), 0, 0, tiled=True)  17.2 us
    pallas_call x5, Pallas kernels, far_best(): pl.pallas_call(functools.partial(far_kernel, carried is None, close, len(...  16.2 us
    pallas_call x1, Pallas kernels, near_best(): pl.pallas_call(functools.partial(near_kernel, per_step), grid=(perms // p...  11.9 us
    ppermute x1, starting transfers between devices, shards_program(): mate_rows = lax.ppermute(perm_rows, both, mate)  6.34 us
    ppermute x1, starting transfers between devices, shards_program(): from_mate = lax.ppermute(to_mate, both, mate)  3.15 us
    pallas_call x1, Pallas kernels, head(): pl.pallas_call(head_kernel, out_shape=[jax.ShapeDtypeStruct((local, sampl...  1.64 us
    ppermute x1, starting transfers between devices, shards_program(): below_twin = lax.ppermute(below, 'var', twin)  1.51 us
    ppermute x1, starting transfers between devices, shards_program(): own_twin = lax.ppermute(own, 'var', twin)  1.46 us
  transfers between devices with their start and end apart: 9, of which 3 were waited for; matrix products, arithmetic and copies ran while one was open for 0% of the time, Pallas kernels for 34%

profile of v10, /device:TPU:1, one launch (start us, length us, event | category | flops | bytes accessed | tf_op | source)
XLA Modules:
  0.0 65.7 jit_solution(17255460290555265264)
XLA Ops:
  0.6 1.6 %head.1 = (bf16[384,768]{1,0:T(8,128)(2,1)S(1)}, bf16[384,256]{1,0:T(8,128)(2,1)S(1)}, s32[16,768]{1,0:T(8,128)S(1)}, s32[128,128]{1,0:T(8,128)S(1)}) custom-call(bf16[1,384,768]{2,1,0:T(8,128)(2,1)} %x_ref.1, f32[128,768]{1,0:T(8,128)} %pheno_ref.1, s32[16,768]{1,0:T(8,128)} %perm_ref.1, s32[1,128]{1,0:T(1,128)} %bitcast.2), custom_call_target="tpu_custom_call" | custom-call | flops 2359296 | tf_op jit(solution)/shard_map/head/pallas_call | solution.py:161
  2.3 1.5 %collective-permute-start.1 = (bf16[384,768]{1,0:T(8,128)(2,1)S(1)}, bf16[384,768]{1,0:T(8,128)(2,1)S(1)}, u32[]{:S(2)}, u32[]{:S(2)}) collective-permute-start(bf16[384,768]{1,0:T(8,128)(2,1)S(1)} %get-tuple-element.23.own_ref), channel_id=1, source_target_pairs={{0,2},{2,0},{4,6},{6,4},{8,10},{10,8},{12,14},{14,12},{1,3},{3,1},... | collective-permute-start | bytes 1769480 | tf_op jit(solution)/shard_map/ppermute | solution.py:342
  3.7 6.3 %collective-permute-start = (s32[16,768]{1,0:T(8,128)}, s32[16,768]{1,0:T(8,128)S(1)}, u32[]{:S(2)}, u32[]{:S(2)}) collective-permute-start(s32[16,768]{1,0:T(8,128)} %perm_ref.1), channel_id=1, source_target_pairs={{0,9},{1,8},{2,11},{3,10},{4,13},{5,12},{6,15},{7,14},{8,1},{9,0},... | collective-permute-start | bytes 147464 | tf_op jit(solution)/shard_map/ppermute | solution.py:337
  10.1 0.0 collective-permute-start.4
  10.1 0.8 %collective-permute-start.3 = (bf16[384,768]{1,0:T(8,128)(2,1)S(1)}, bf16[384,768]{1,0:T(8,128)(2,1)S(1)}, u32[]{:S(2)}, u32[]{:S(2)}) collective-permute-start(bf16[384,768]{1,0:T(8,128)(2,1)S(1)} %get-tuple-element.23.own_ref), channel_id=1, source_target_pairs={{0,12},{2,14},{4,0},{6,2},{8,4},{10,6},{12,8},{14,10},{1,13},{3,15... | collective-permute-start | bytes 1769480 | tf_op jit(solution)/shard_map/ppermute | solution.py:341
  10.9 0.7 %collective-permute-start.2 = (bf16[384,768]{1,0:T(8,128)(2,1)S(1)}, bf16[384,768]{1,0:T(8,128)(2,1)S(1)}, u32[]{:S(2)}, u32[]{:S(2)}) collective-permute-start(bf16[384,768]{1,0:T(8,128)(2,1)S(1)} %get-tuple-element.23.own_ref), channel_id=1, source_target_pairs={{0,4},{2,6},{4,8},{6,10},{8,12},{10,14},{12,0},{14,2},{1,5},{3,7},... | collective-permute-start | bytes 1769480 | tf_op jit(solution)/shard_map/ppermute | solution.py:340
  11.5 0.8 %collective-permute-done.mate_ref = s32[16,768]{1,0:T(8,128)S(1)} collective-permute-done((s32[16,768]{1,0:T(8,128)}, s32[16,768]{1,0:T(8,128)S(1)}, u32[]{:S(2)}, u32[]{:S(2)}) %collective-permute-start) | collective-permute-done | bytes 49184 | tf_op jit(solution)/shard_map/ppermute | solution.py:337
  12.3 0.0 collective-permute-done.1.twin_ref
  12.3 11.9 %near.1 = (bf16[4096,768]{1,0:T(8,128)(2,1)S(1)}, f32[32,128]{1,0:T(8,128)S(1)}, f32[6,128,384]{2,1,0:T(8,128)S(1)}) custom-call(bf16[384,256]{1,0:T(8,128)(2,1)S(1)} %get-tuple-element.20.base_ref, s32[16,768]{1,0:T(8,128)S(1)} %get-tuple-element.21.perm_ref, s32[16,768]{1,0:T(8,128)S(1)} %collective-permute-done.mate_ref, ...), custom_call_target="tpu_custom_call" | custom-call | flops 9663676416 | tf_op jit(solution)/shard_map/near/pallas_call | solution.py:185
  24.2 0.8 %collective-permute-done.3.refs_2_.refs_3_ = bf16[384,768]{1,0:T(8,128)(2,1)S(1)} collective-permute-done((bf16[384,768]{1,0:T(8,128)(2,1)S(1)}, bf16[384,768]{1,0:T(8,128)(2,1)S(1)}, u32[]{:S(2)}, u32[]{:S(2)}) %collective-permute-start.3) | collective-permute-done | bytes 589856 | tf_op jit(solution)/shard_map/ppermute | solution.py:341
  25.0 1.3 %collective-permute-done.2.refs_1_.refs_2_ = bf16[384,768]{1,0:T(8,128)(2,1)S(1)} collective-permute-done((bf16[384,768]{1,0:T(8,128)(2,1)S(1)}, bf16[384,768]{1,0:T(8,128)(2,1)S(1)}, u32[]{:S(2)}, u32[]{:S(2)}) %collective-permute-start.2) | collective-permute-done | bytes 589856 | tf_op jit(solution)/shard_map/ppermute | solution.py:340
  26.3 1.5 %collective-permute-start.6 = (bf16[384,768]{1,0:T(8,128)(2,1)S(1)}, bf16[384,768]{1,0:T(8,128)(2,1)S(1)}, u32[]{:S(2)}, u32[]{:S(2)}) collective-permute-start(bf16[384,768]{1,0:T(8,128)(2,1)S(1)} %collective-permute-done.2.refs_1_.refs_2_), channel_id=1, source_target_pairs={{0,2},{2,0},{4,6},{6,4},{8,10},{10,8},{12,14},{14,12},{1,3},{3,1},... | collective-permute-start | bytes 1769480 | tf_op jit(solution)/shard_map/ppermute | solution.py:345
  27.8 0.0 collective-permute-start.7
  27.8 2.7 %far.5.refs_3_ = f32[16,128,128]{2,1,0:T(8,128)S(1)} custom-call(bf16[4096,768]{1,0:T(8,128)(2,1)S(1)} %get-tuple-element.24.table_ref, f32[32,128]{1,0:T(8,128)S(1)} %get-tuple-element.25.near_ref, f32[6,128,384]{2,1,0:T(8,128)S(1)} %get-tuple-element.27.refs_0_.refs_1_, bf16[384,768]{1,0:T(8,128)(2,1)S(1)} %collective-permute-done.2.refs_1_.refs_2_, ...), custom_call_target="tpu_custom_call" | custom-call | flops 2415919104 | tf_op jit(solution)/shard_map/far/pallas_call | solution.py:275
  30.5 0.0 collective-permute-done.4.refs_1_
  30.5 0.6 collective-permute-start.5
  31.1 2.7 %far.7.refs_3_ = f32[16,128,128]{2,1,0:T(8,128)S(1)} custom-call(bf16[4096,768]{1,0:T(8,128)(2,1)S(1)} %get-tuple-element.24.table_ref, f32[32,128]{1,0:T(8,128)S(1)} %get-tuple-element.25.near_ref, f32[6,128,384]{2,1,0:T(8,128)S(1)} %get-tuple-element.27.refs_0_.refs_1_, bf16[384,768]{1,0:T(8,128)(2,1)S(1)} %collective-permute-done.6.refs_4_.refs_1_, ...), custom_call_target="tpu_custom_call" | custom-call | flops 2415919104 | tf_op jit(solution)/shard_map/far/pallas_call | solution.py:275
  33.8 0.0 collective-permute-done.5.refs_2_
  33.8 2.9 %far.8 = f32[16,128]{1,0:T(8,128)S(1)} custom-call(bf16[4096,768]{1,0:T(8,128)(2,1)S(1)} %get-tuple-element.24.table_ref, f32[32,128]{1,0:T(8,128)S(1)} %get-tuple-element.25.near_ref, f32[6,128,384]{2,1,0:T(8,128)S(1)} %get-tuple-element.27.refs_0_.refs_1_, bf16[384,768]{1,0:T(8,128)(2,1)S(1)} %collective-permute-done.4.refs_1_, ...), custom_call_target="tpu_custom_call" | custom-call | flops 2415919104 | tf_op jit(solution)/shard_map/far/pallas_call | solution.py:275
  36.7 3.1 %collective-permute-start.8 = (f32[16,128]{1,0:T(8,128)S(1)}, f32[16,128]{1,0:T(8,128)S(1)}, u32[]{:S(2)}, u32[]{:S(2)}) collective-permute-start(f32[16,128]{1,0:T(8,128)S(1)} %far.8), channel_id=1, source_target_pairs={{0,9},{1,8},{2,11},{3,10},{4,13},{5,12},{6,15},{7,14},{8,1},{9,0},... | collective-permute-start | bytes 24584 | tf_op jit(solution)/shard_map/ppermute | solution.py:352
  39.8 5.1 %far.6.refs_3_ = f32[16,128,128]{2,1,0:T(8,128)S(1)} custom-call(bf16[4096,768]{1,0:T(8,128)(2,1)S(1)} %get-tuple-element.24.table_ref, f32[32,128]{1,0:T(8,128)S(1)} %get-tuple-element.25.near_ref, f32[6,128,384]{2,1,0:T(8,128)S(1)} %get-tuple-element.27.refs_0_.refs_1_, f32[6,128,384]{2,1,0:T(8,128)S(1)} %get-tuple-element.27.refs_0_.refs_1_, ...), custom_call_target="tpu_custom_call" | custom-call | flops 4831838208 | tf_op jit(solution)/shard_map/far/pallas_call | solution.py:275
  45.0 2.8 %far.9 = (f32[16,128]{1,0:T(8,128)S(1)}, f32[128,2,128]{2,1,0:T(2,128)S(1)}) custom-call(bf16[4096,768]{1,0:T(8,128)(2,1)S(1)} %get-tuple-element.24.table_ref, f32[32,128]{1,0:T(8,128)S(1)} %get-tuple-element.25.near_ref, f32[6,128,384]{2,1,0:T(8,128)S(1)} %get-tuple-element.27.refs_0_.refs_1_, bf16[384,768]{1,0:T(8,128)(2,1)S(1)} %collective-permute-done.4.refs_1_, ...), custom_call_target="tpu_custom_call" | custom-call | flops 2415919104 | tf_op jit(solution)/shard_map/far/pallas_call | solution.py:275
  47.8 17.2 %all_to_all.5.sent_ref = f32[128,2,128]{2,1,0:T(2,128)S(1)} all-to-all(f32[128,2,128]{2,1,0:T(2,128)S(1)} %get-tuple-element.32), channel_id=1, replica_groups=mesh['gene'=8,'var'=8,'perm'=2] {'gene','var','perm'}, dimensions={0} | all-to-all | bytes 262144 | tf_op jit(solution)/shard_map/all_to_all | solution.py:359
  65.0 0.7 %totals.1 = (f32[16,128]{1,0:T(8,128)}, f32[2,128]{1,0:T(2,128)}, f32[1,2]{1,0:T(1,128)}) custom-call(f32[128,2,128]{2,1,0:T(2,128)S(1)} %all_to_all.5.sent_ref, f32[16,128]{1,0:T(8,128)S(1)} %get-tuple-element.33.held_ref), custom_call_target="tpu_custom_call" | custom-call | tf_op jit(solution)/shard_map/totals/pallas_call | solution.py:310
  (3 shorter events, 0.0 us)
Async XLA Ops:
  2.3 10.0 %collective-permute-start.1 = (bf16[384,768]{1,0:T(8,128)(2,1)S(1)}, bf16[384,768]{1,0:T(8,128)(2,1)S(1)}, u32[]{:S(2)}, u32[]{:S(2)}) collective-permute-start(bf16[384,768]{1,0:T(8,128)(2,1)S(1)} %get-tuple-element.23.own_ref), channel_id=1, source_target_pairs={{0,2},{2,0},{4,6},{6,4},{8,10},{10,8},{12,14},{14,12},{1,3},{3,1},... | collective-permute-start | bytes 1769480 | tf_op jit(solution)/shard_map/ppermute | solution.py:342
  3.7 8.6 %collective-permute-start = (s32[16,768]{1,0:T(8,128)}, s32[16,768]{1,0:T(8,128)S(1)}, u32[]{:S(2)}, u32[]{:S(2)}) collective-permute-start(s32[16,768]{1,0:T(8,128)} %perm_ref.1), channel_id=1, source_target_pairs={{0,9},{1,8},{2,11},{3,10},{4,13},{5,12},{6,15},{7,14},{8,1},{9,0},... | collective-permute-start | bytes 147464 | tf_op jit(solution)/shard_map/ppermute | solution.py:337
  10.1 20.4 %collective-permute-start.4 = (bf16[384,768]{1,0:T(8,128)(2,1)S(1)}, bf16[384,768]{1,0:T(8,128)(2,1)S(1)}, u32[]{:S(2)}, u32[]{:S(2)}) collective-permute-start(bf16[384,768]{1,0:T(8,128)(2,1)S(1)} %get-tuple-element.23.own_ref), channel_id=1, source_target_pairs={{0,1},{1,0},{2,3},{3,2},{4,5},{5,4},{6,7},{7,6},{8,9},{9,8},{10,11... | collective-permute-start | bytes 1769480 | tf_op jit(solution)/shard_map/ppermute | solution.py:339
  10.1 14.9 %collective-permute-start.3 = (bf16[384,768]{1,0:T(8,128)(2,1)S(1)}, bf16[384,768]{1,0:T(8,128)(2,1)S(1)}, u32[]{:S(2)}, u32[]{:S(2)}) collective-permute-start(bf16[384,768]{1,0:T(8,128)(2,1)S(1)} %get-tuple-element.23.own_ref), channel_id=1, source_target_pairs={{0,12},{2,14},{4,0},{6,2},{8,4},{10,6},{12,8},{14,10},{1,13},{3,15... | collective-permute-start | bytes 1769480 | tf_op jit(solution)/shard_map/ppermute | solution.py:341
  10.9 15.4 %collective-permute-start.2 = (bf16[384,768]{1,0:T(8,128)(2,1)S(1)}, bf16[384,768]{1,0:T(8,128)(2,1)S(1)}, u32[]{:S(2)}, u32[]{:S(2)}) collective-permute-start(bf16[384,768]{1,0:T(8,128)(2,1)S(1)} %get-tuple-element.23.own_ref), channel_id=1, source_target_pairs={{0,4},{2,6},{4,8},{6,10},{8,12},{10,14},{12,0},{14,2},{1,5},{3,7},... | collective-permute-start | bytes 1769480 | tf_op jit(solution)/shard_map/ppermute | solution.py:340
  26.3 4.8 %collective-permute-start.6 = (bf16[384,768]{1,0:T(8,128)(2,1)S(1)}, bf16[384,768]{1,0:T(8,128)(2,1)S(1)}, u32[]{:S(2)}, u32[]{:S(2)}) collective-permute-start(bf16[384,768]{1,0:T(8,128)(2,1)S(1)} %collective-permute-done.2.refs_1_.refs_2_), channel_id=1, source_target_pairs={{0,2},{2,0},{4,6},{6,4},{8,10},{10,8},{12,14},{14,12},{1,3},{3,1},... | collective-permute-start | bytes 1769480 | tf_op jit(solution)/shard_map/ppermute | solution.py:345
  27.8 3.3 %collective-permute-start.7 = (bf16[384,768]{1,0:T(8,128)(2,1)S(1)}, bf16[384,768]{1,0:T(8,128)(2,1)S(1)}, u32[]{:S(2)}, u32[]{:S(2)}) collective-permute-start(bf16[384,768]{1,0:T(8,128)(2,1)S(1)} %collective-permute-done.3.refs_2_.refs_3_), channel_id=1, source_target_pairs={{0,2},{2,0},{4,6},{6,4},{8,10},{10,8},{12,14},{14,12},{1,3},{3,1},... | collective-permute-start | bytes 1769480 | tf_op jit(solution)/shard_map/ppermute | solution.py:346
  30.5 3.3 %collective-permute-start.5 = (bf16[384,768]{1,0:T(8,128)(2,1)S(1)}, bf16[384,768]{1,0:T(8,128)(2,1)S(1)}, u32[]{:S(2)}, u32[]{:S(2)}) collective-permute-start(bf16[384,768]{1,0:T(8,128)(2,1)S(1)} %collective-permute-done.4.refs_1_), channel_id=1, source_target_pairs={{0,2},{2,0},{4,6},{6,4},{8,10},{10,8},{12,14},{14,12},{1,3},{3,1},... | collective-permute-start | bytes 1769480 | tf_op jit(solution)/shard_map/ppermute | solution.py:349
  36.7 8.3 %collective-permute-start.8 = (f32[16,128]{1,0:T(8,128)S(1)}, f32[16,128]{1,0:T(8,128)S(1)}, u32[]{:S(2)}, u32[]{:S(2)}) collective-permute-start(f32[16,128]{1,0:T(8,128)S(1)} %far.8), channel_id=1, source_target_pairs={{0,9},{1,8},{2,11},{3,10},{4,13},{5,12},{6,15},{7,14},{8,1},{9,0},... | collective-permute-start | bytes 24584 | tf_op jit(solution)/shard_map/ppermute | solution.py:352
